TPU v7x, 256 devices: a whole 4x4x8 slice. The times are simulated.
256 devices in a mesh: dap: 128 (over z_lo, x, y, core), rep: 2 (over z_hi).
Axes of the slice: x: 4, y: 4, z: 8 (z_hi: 2, z_lo: 4; z = z_hi * 4 + z_lo), core: 2. Of those that a mesh axis runs over, the one named last changes fastest.
Arguments:
- related_chain_embedding: bfloat16 [256, 384, 256], P('dap'), may hold values from -6 to 6
- couple_representation: bfloat16 [384, 384, 128], P('dap'), may hold values from -6 to 6
- homolog_present: int32 [256], replicated, may hold values 0 or 1
- amino_present: int32 [384], replicated, may hold values 0 or 1
- horizontal_query_factors: bfloat16 [4, 256, 256], P(None, None, 'rep'), may hold values from -3 to 3
- across_chain_closing_transform: bfloat16 [256, 256], P('rep'), may hold values from -0.375 to 0.375
- couple_offset_factor: bfloat16 [128, 8], P(None, 'rep'), may hold values from -1.5859375 to 1.5859375
- vertical_query_factors: bfloat16 [4, 256, 256], P(None, None, 'rep'), may hold values from -3 to 3
- down_position_closing_transform: bfloat16 [256, 256], P('rep'), may hold values from -0.375 to 0.375
- trilateral_left_right_factors: bfloat16 [4, 128, 128], P(None, None, 'rep'), may hold values from -0.5 to 0.5
- trilateral_final_factor: bfloat16 [128, 128], P('rep'), may hold values from -0.5 to 0.5
- trilateral_sigmoid_factor: bfloat16 [128, 128], P(None, 'rep'), may hold values from -0.5 to 0.5
Outputs:
- alignment_output: bfloat16 [256, 384, 256], P(None, 'dap', 'rep')
- pair_output: bfloat16 [384, 384, 128], P('dap', None, 'rep')
Inputs may be any that keep to these rules, and one draw needn't show every extreme that they name: `homolog_present`: 1 marks a sequence that keys may attend to. `amino_present`: 1 marks a residue that keys and the triangle products use.
All inputs are finite; a program needn't handle non-finite values.
Results may differ from a plain program's by a relative error of at most 0.012.
The roundings to bfloat16 on the way count: a program that leaves them out, or rounds other values in their place, can miss the bound.
Values may be sent and summed in bfloat16 or wider, within the bound.
A program may use at most 128 MiB of HBM per device.

v0:
```python
import jax
import jax.numpy as jnp
from jax import lax
from jax.sharding import Mesh
from jax.sharding import PartitionSpec as P

GROUP_BREADTH = 32
DAP = ("dap_0", "dap_1", "dap_2", "dap_3")


EPS = 1e-05
NEG = 1000000000.0


def sent_to_all(value, axis):
    copies = jnp.broadcast_to(value, (lax.axis_size(axis), *value.shape))
    return lax.all_to_all(copies, axis, split_axis=0, concat_axis=0, tiled=True)


def joined_along(parts, dim):
    dims = list(parts.shape[1:])
    dims[dim] *= parts.shape[0]
    return jnp.moveaxis(parts, 0, dim).reshape(dims)


def gather_axes(value, axes, dim):
    far, near = axes
    parts = sent_to_all(sent_to_all(value, far), near)
    return joined_along(parts.swapaxes(0, 1).reshape(-1, *value.shape), dim)


def over_copies(value, axis):
    return sent_to_all(value, axis).sum(axis=0)


def in_blocks(value, dim, devices):
    before, after = (value.shape[:dim], value.shape[dim + 1 :])
    return jnp.moveaxis(value.reshape(*before, devices, -1, *after), dim, 0)


def sum_at_owner(value, axis, dim):
    devices = lax.axis_size(axis)
    parts = lax.all_to_all(in_blocks(value, dim, devices), axis, 0, 0, tiled=True)
    return jnp.sum(parts.astype(jnp.float32), axis=0)


def together(arrays, axis):
    vector, at, finished = (jnp.concatenate([a.reshape(-1) for a in arrays]), 0, [])
    total = over_copies(vector, axis)
    for a in arrays:
        finished.append(total[at : at + a.size].reshape(a.shape))
        at += a.size
    return tuple(finished)


def standardize_features(values):
    values = values.astype(jnp.float32)
    center = jnp.mean(values, axis=-1, keepdims=True)
    spread = jnp.mean(jnp.square(values - center), axis=-1, keepdims=True)
    return (values - center) * lax.rsqrt(spread + EPS)


def project_four(standardized_features, weights):
    heads_here = weights.shape[2] // GROUP_BREADTH
    array_extent = standardized_features.shape[:-1] + (heads_here, GROUP_BREADTH)
    return tuple(
        (
            jnp.dot(standardized_features, weights[number], preferred_element_type=jnp.float32)
            .astype(jnp.bfloat16)
            .reshape(array_extent)
            for number in range(4)
        )
    )


def attend(query, keys, values, gate, bias):
    scores = (
        jnp.einsum("qhd,khd->hqk", query, keys, preferred_element_type=jnp.float32)
        / jnp.sqrt(jnp.float32(GROUP_BREADTH))
        + bias
    )
    weights = jax.nn.softmax(scores, axis=-1).astype(jnp.bfloat16)
    mixed = jnp.einsum("hqk,khd->qhd", weights, values, preferred_element_type=jnp.float32)
    return (mixed * jax.nn.sigmoid(gate.astype(jnp.float32))).astype(jnp.bfloat16)


def per_device(
    related_chain_embedding,
    couple_representation,
    homolog_present,
    amino_present,
    horizontal_query_factors,
    across_chain_closing_transform,
    couple_offset_factor,
    vertical_query_factors,
    down_position_closing_transform,
    trilateral_left_right_factors,
    trilateral_final_factor,
    trilateral_sigmoid_factor,
):
    rows_here = couple_representation.shape[0]
    row_start = lax.axis_index(DAP) * rows_here
    res_float = amino_present.astype(jnp.float32)
    mask_rows = lax.dynamic_slice_in_dim(res_float, row_start, rows_here, 0)
    pair_ln = standardize_features(couple_representation).astype(jnp.bfloat16)
    local_bias = jnp.einsum(
        "ijc,ch->hij", pair_ln, couple_offset_factor, preferred_element_type=jnp.float32
    ).astype(jnp.bfloat16)
    pair_bias = gather_axes(local_bias, (("dap_0", "dap_1", "dap_2"), "dap_3"), 1)
    row_bias = pair_bias.astype(jnp.float32) + NEG * (res_float - 1.0)[None, None, :]
    standardized_features = standardize_features(related_chain_embedding).astype(jnp.bfloat16)
    row_parts = project_four(standardized_features, horizontal_query_factors)

    def one_row(parts):
        return attend(parts[0], parts[1], parts[2], parts[3], row_bias)

    horizontal_mixed_result = lax.map(one_row, row_parts)
    horizontal_reshaped = horizontal_mixed_result.reshape(
        related_chain_embedding.shape[0],
        related_chain_embedding.shape[1],
        across_chain_closing_transform.shape[0],
    )
    partial_value = jnp.dot(
        horizontal_reshaped, across_chain_closing_transform, preferred_element_type=jnp.float32
    )
    accumulated_result = over_copies(partial_value, "rep")
    homolog_stack_lone = (related_chain_embedding.astype(jnp.float32) + accumulated_result).astype(
        jnp.bfloat16
    )
    column_block = lax.all_to_all(homolog_stack_lone, DAP, split_axis=1, concat_axis=0, tiled=True)
    width = column_block.shape[2] // lax.axis_size("rep")
    retained_half = lax.dynamic_slice_in_dim(column_block, lax.axis_index("rep") * width, width, 2)
    seqs_all = column_block.shape[0]
    cols_here = column_block.shape[1]
    column_normalized = standardize_features(column_block).astype(jnp.bfloat16)
    col_parts = project_four(column_normalized, vertical_query_factors)
    heads_here = vertical_query_factors.shape[2] // GROUP_BREADTH
    col_bias = (NEG * (homolog_present.astype(jnp.float32) - 1.0))[None, None, :]
    block = min(512, seqs_all)

    def one_column(column):
        query, keys, values, gate = [
            lax.dynamic_index_in_dim(part, column, 1, keepdims=False) for part in col_parts
        ]

        def one_block(start):
            return attend(query, keys, values, gate, col_bias)

        starts = jnp.arange(0, seqs_all, block, dtype=jnp.int32)
        return lax.map(one_block, starts).reshape(seqs_all, heads_here, GROUP_BREADTH)

    col_mixed = lax.map(one_column, jnp.arange(cols_here, dtype=jnp.int32))
    produced_tensor = down_position_closing_transform.reshape(
        heads_here, GROUP_BREADTH, down_position_closing_transform.shape[1]
    )
    col_partial = jnp.einsum(
        "rshd,hdz->srz", col_mixed, produced_tensor, preferred_element_type=jnp.float32
    )
    column_delta = sum_at_owner(col_partial.astype(jnp.bfloat16), "rep", 2)
    alignment_output = (retained_half.astype(jnp.float32) + column_delta).astype(jnp.bfloat16)
    pair_mask = mask_rows[:, None] * res_float[None, :]

    def gated_side(gate_weight, value_weight):
        gate = jnp.einsum("ikd,dc->cik", pair_ln, gate_weight, preferred_element_type=jnp.float32)
        value = jnp.einsum("ikd,dc->cik", pair_ln, value_weight, preferred_element_type=jnp.float32)
        return (jax.nn.sigmoid(gate) * value * pair_mask[None]).astype(jnp.bfloat16)

    left = gated_side(trilateral_left_right_factors[0], trilateral_left_right_factors[1])
    right = gated_side(trilateral_left_right_factors[2], trilateral_left_right_factors[3])
    block_product = jnp.einsum(
        "cik,cjk->cij",
        left,
        lax.all_gather(right, DAP, axis=1, tiled=True),
        preferred_element_type=jnp.float32,
    )
    first, second = together(
        (jnp.sum(block_product, axis=0), jnp.sum(block_product * block_product, axis=0)), "rep"
    )
    count = jnp.float32(block_product.shape[0] * lax.axis_size("rep"))
    mean = first / count
    square = second / count
    scaled = ((block_product - mean) * lax.rsqrt(square - mean * mean + EPS)).astype(jnp.bfloat16)
    tri_partial = jnp.einsum(
        "cij,cz->ijz", scaled, trilateral_final_factor, preferred_element_type=jnp.float32
    )
    tri_update = sum_at_owner(tri_partial.astype(jnp.bfloat16), "rep", 2)
    half = tri_update.shape[2]
    pair_half = lax.dynamic_slice_in_dim(
        couple_representation, lax.axis_index("rep") * half, half, 2
    )
    gate_out = jax.nn.sigmoid(
        jnp.dot(pair_ln, trilateral_sigmoid_factor, preferred_element_type=jnp.float32)
    )
    pair_output = (pair_half.astype(jnp.float32) + gate_out * tri_update).astype(jnp.bfloat16)
    return (alignment_output, pair_output)


def solution(mesh):
    finer = Mesh(
        mesh.devices.reshape(4, 4, 4, 2, mesh.shape["rep"]),
        ("dap_0", "dap_1", "dap_2", "dap_3", "rep"),
    )
    return jax.shard_map(
        per_device,
        mesh=finer,
        in_specs=(
            P(DAP, None, None),
            P(DAP, None, None),
            P(),
            P(),
            P(None, None, "rep"),
            P("rep", None),
            P(None, "rep"),
            P(None, None, "rep"),
            P("rep", None),
            P(None, None, "rep"),
            P("rep", None),
            P(None, "rep"),
        ),
        out_specs=(P(None, DAP, "rep"), P(DAP, None, "rep")),
        check_vma=False,
    )
```

profile of v0, /device:TPU:32, one launch (start us, length us, event | category | flops | bytes accessed | tf_op | source)
XLA Modules:
  0.0 365.1 jit_solution(14324703924220986987)
XLA Ops:
  7.3 0.7 convert_element_type.158
  8.0 1.1 convert_reduce_fusion.3
  9.2 1.4 fusion.97
  10.7 1.5 fusion.71
  12.3 1.9 fusion.83
  14.2 0.5 fusion.85
  14.7 1.0 broadcast_in_dim.32
  15.7 11.7 %all-to-all-start = ((bf16[64,4,3,384]{3,1,2,0:T(4,128)(2,1)}), bf16[64,4,3,384]{3,1,2,0:T(4,128)(2,1)S(1)}, u32[]{:S(2)}, u32[]{:S(2)}) async-start(bf16[64,4,3,384]{3,1,2,0:T(4,128)(2,1)} %broadcast_in_dim.32), calls=%async_computation | async-start | bytes 1179648 | tf_op jit(solution)/shard_map/all_to_all | solution.py:17
  27.6 0.3 fusion.92
  27.9 1.2 convolution_convert_fusion.8
  29.1 0.5 convolution_convert_fusion.7
  29.6 0.5 convolution_convert_fusion.6
  30.0 1.2 convolution_convert_fusion.5
  31.2 16.4 %all-to-all-done = bf16[64,4,3,384]{3,1,2,0:T(4,128)(2,1)S(1)} async-done(((bf16[64,4,3,384]{3,1,2,0:T(4,128)(2,1)}), bf16[64,4,3,384]{3,1,2,0:T(4,128)(2,1)S(1)}, u32[]{:S(2)}, u32[]{:S(2)}) %all-to-all-start) | async-done | bytes 589856 | tf_op jit(solution)/shard_map/all_to_all | solution.py:17
  47.6 0.3 broadcast_in_dim.33
  47.9 4.7 %all_to_all.49 = bf16[2,64,4,3,384]{4,2,3,1,0:T(4,128)(2,1)S(1)} all-to-all(bf16[2,64,4,3,384]{4,2,3,1,0:T(4,128)(2,1)S(1)} %broadcast_in_dim.33), channel_id=1, replica_groups=mesh['dap_0'=4,'dap_1'=4,'dap_2'=4,'dap_3'=2,'rep'=2] {'dap_3'}, dimensions={0} | all-to-all | bytes 2359296 | tf_op jit(solution)/shard_map/all_to_all | solution.py:17
  52.7 0.3 convert_bitcast_fusion
  53.0 0.4 copy.154
  53.4 2.0 bitcast_add_fusion
  55.4 2.8 copy.156
  58.3 13.0 %while.24 = (s32[]{:T(128)}, bf16[2,384,4,32]{1,3,2,0:T(8,128)(2,1)}, bf16[2,384,4,32]{1,3,2,0:T(8,128)(2,1)}, bf16[2,384,4,32]{1,3,2,0:T(8,128)(2,1)S(1)}, bf16...) while((s32[]{:T(128)}, ...), condition=%wide.region_7.8_spmd, body=%wide.region_4.7_spmd.sunk | while | flops 118851840 | bytes 12500053 | solution.py:117
  58.3 1.9 multiply_add_fusion.2
  60.2 0.8 fusion.180
  61.1 3.7 %fusion.181 = bf16[2,384,4,32]{1,3,2,0:T(8,128)(2,1)} fusion(bf16[2,384,4,32]{1,3,2,0:T(8,128)(2,1)} %get-tuple-element.292, s32[]{:T(128)} %get-tuple-element.291, f32[4,384]{1,0:T(4,128)S(1)} %fusion.180, bf16[2,384,4,32]{1,3,2,0:T(8,128)(2,1)} %get-tuple-element.305, bf16[2,384,4,32]{1,3,2,0:T(8,128)(2,1)} %get-tuple-element.301, ...), kind=kOutput, calls=%fused_computation.9.clone.1 | convolution fusion | flops 39815040 | bytes 5020672 | tf_op jit(solution)/shard_map/while/body/eval_jaxpr/hqk,khd->qhd/dot_general | solution.py:83
  64.8 1.9 multiply_add_fusion.2
  66.7 0.8 fusion.180
  67.5 3.7 %fusion.181 = bf16[2,384,4,32]{1,3,2,0:T(8,128)(2,1)} fusion(bf16[2,384,4,32]{1,3,2,0:T(8,128)(2,1)} %get-tuple-element.292, s32[]{:T(128)} %get-tuple-element.291, f32[4,384]{1,0:T(4,128)S(1)} %fusion.180, bf16[2,384,4,32]{1,3,2,0:T(8,128)(2,1)} %get-tuple-element.305, bf16[2,384,4,32]{1,3,2,0:T(8,128)(2,1)} %get-tuple-element.301, ...), kind=kOutput, calls=%fused_computation.9.clone.1 | convolution fusion | flops 39815040 | bytes 5020672 | tf_op jit(solution)/shard_map/while/body/eval_jaxpr/hqk,khd->qhd/dot_general | solution.py:83
  71.2 1.2 fusion.113
  72.5 1.3 broadcast_in_dim.54
  73.8 6.0 %all-to-all-start.2 = ((f32[2,2,384,256]{3,2,1,0:T(8,128)}), f32[2,2,384,256]{3,2,1,0:T(8,128)S(1)}, u32[]{:S(2)}, u32[]{:S(2)}) async-start(f32[2,2,384,256]{3,2,1,0:T(8,128)} %broadcast_in_dim.54), calls=%async_computation.2 | async-start | bytes 3145728 | tf_op jit(solution)/shard_map/all_to_all | solution.py:17
  79.7 56.6 %all-to-all-done.2 = f32[2,2,384,256]{3,2,1,0:T(8,128)S(1)} async-done(((f32[2,2,384,256]{3,2,1,0:T(8,128)}), f32[2,2,384,256]{3,2,1,0:T(8,128)S(1)}, u32[]{:S(2)}, u32[]{:S(2)}) %all-to-all-start.2) | async-done | bytes 1572896 | tf_op jit(solution)/shard_map/all_to_all | solution.py:17
  136.7 1.2 copy.158
  137.8 6.2 %all-to-all-start.3 = ((bf16[2,384,256]{2,0,1:T(2,128)(2,1)}), bf16[2,384,256]{2,0,1:T(2,128)(2,1)S(1)}, u32[]{:S(2)}, u32[]{:S(2)}) async-start(bf16[2,384,256]{2,0,1:T(2,128)(2,1)} %copy.158), calls=%async_computation.3 | async-start | bytes 786432 | tf_op jit(solution)/shard_map/all_to_all | solution.py:130
  144.4 0.5 fusion.74
  144.9 0.5 fusion.84
  145.4 13.1 %all-to-all-done.3 = bf16[2,384,256]{2,0,1:T(2,128)(2,1)S(1)} async-done(((bf16[2,384,256]{2,0,1:T(2,128)(2,1)}), bf16[2,384,256]{2,0,1:T(2,128)(2,1)S(1)}, u32[]{:S(2)}, u32[]{:S(2)}) %all-to-all-start.3) | async-done | bytes 393248 | tf_op jit(solution)/shard_map/all_to_all | solution.py:130
  158.8 0.6 convert_reduce_fusion.1
  159.5 1.1 fusion.90
  160.7 1.0 fusion.91
  162.6 0.3 convolution_convert_fusion.3
  163.5 10.9 %while.25 = (s32[]{:T(128)}, bf16[3,256,4,32]{1,3,2,0:T(8,128)(2,1)S(1)}, s32[3]{0:T(128)S(1)}, bf16[256,3,4,32]{0,3,2,1:T(8,128)(2,1)S(1)}, bf16[256,3,4,32]{0,...) while((s32[]{:T(128)}, ...), condition=%wide.region_14.15_spmd, body=%wide.region_11.14_spmd.sunk | while | flops 52889092 | bytes 472223 | solution.py:152
  163.5 0.6 dynamic_slice.125
  165.9 0.5 fusion.187
  166.5 0.7 fusion.188
  167.1 0.6 dynamic_slice.125
  169.6 0.5 fusion.187
  170.1 0.6 fusion.188
  170.7 0.6 dynamic_slice.125
  173.2 0.5 fusion.187
  173.7 0.7 fusion.188
  174.4 0.3 fusion.66
  174.7 98.8 %all-gather.2.cloned.1.call-done = bf16[64,384,384]{2,0,1:T(8,128)(2,1)} async-done(((bf16[64,3,384]{2,0,1:T(8,128)(2,1)}), bf16[64,384,384]{2,0,1:T(8,128)(2,1)}) %all-gather.2.cloned.1.call-update) | async-done | bytes 18874384 | tf_op jit(solution)/shard_map/all_gather | solution.py:173
  273.5 39.0 %fusion.140 = (f32[3,384]{1,0:T(4,128)S(1)}, f32[3,384]{1,0:T(4,128)S(1)}, f32[64,3,384]{2,1,0:T(4,128)S(1)}) fusion(bf16[64,384,384]{2,0,1:T(8,128)(2,1)} %all-gather.2.cloned.1.call-done, bf16[64,3,384]{2,0,1:T(8,128)(2,1)S(1)} %fusion.84), kind=kOutput, calls=%fused_computation.161 | convolution fusion | flops 56841984 | bytes 19325952 | tf_op jit(solution)/shard_map/cik,cjk->cij/dot_general | solution.py:170
  312.5 0.6 broadcast_in_dim.57
  313.2 5.8 %all-to-all-start.5 = ((f32[2,1,2304]{2,1,0:T(1,128)}), f32[2,1,2304]{2,1,0:T(1,128)S(1)}, u32[]{:S(2)}, u32[]{:S(2)}) async-start(f32[2,1,2304]{2,1,0:T(1,128)} %broadcast_in_dim.57), calls=%async_computation.5 | async-start | bytes 36864 | tf_op jit(solution)/shard_map/all_to_all | solution.py:17
  319.0 0.8 copy.205
  319.9 6.8 %all-to-all-done.5 = f32[2,1,2304]{2,1,0:T(1,128)S(1)} async-done(((f32[2,1,2304]{2,1,0:T(1,128)}), f32[2,1,2304]{2,1,0:T(1,128)S(1)}, u32[]{:S(2)}, u32[]{:S(2)}) %all-to-all-start.5) | async-done | bytes 18464 | tf_op jit(solution)/shard_map/all_to_all | solution.py:17
  326.8 3.5 all-to-all-start.4
  330.7 0.7 copy.206
  331.5 11.4 %all-to-all-done.4 = bf16[2,256,3,128]{1,3,2,0:T(8,128)(2,1)S(1)} async-done(((bf16[2,256,3,128]{1,3,2,0:T(8,128)(2,1)}), bf16[2,256,3,128]{1,3,2,0:T(8,128)(2,1)S(1)}, u32[]{:S(2)}, u32[]{:S(2)}) %all-to-all-start.4) | async-done | bytes 393248 | tf_op jit(solution)/shard_map/all_to_all | solution.py:43
  342.9 3.4 all-to-all-start.6
  346.4 0.8 copy.174
  347.3 9.5 %all-to-all-done.6 = bf16[2,3,384,64]{2,3,1,0:T(8,128)(2,1)S(1)} async-done(((bf16[2,3,384,64]{2,3,1,0:T(8,128)(2,1)}), bf16[2,3,384,64]{2,3,1,0:T(8,128)(2,1)S(1)}, u32[]{:S(2)}, u32[]{:S(2)}) %all-to-all-start.6) | async-done | bytes 294944 | tf_op jit(solution)/shard_map/all_to_all | solution.py:43
  356.9 1.2 fusion.82
  (63 shorter events, 3.7 us)
Async XLA Ops:
  7.2 167.2 %copy-start = (bf16[128,256]{1,0:T(8,128)(2,1)S(1)}, bf16[128,256]{1,0:T(8,128)(2,1)}, u32[]{:S(2)}) copy-start(bf16[128,256]{1,0:T(8,128)(2,1)} %param.24) | copy-start | bytes 196612
  7.2 5.1 %copy-start.2 = (bf16[3,384,128]{2,1,0:T(8,128)(2,1)S(1)}, bf16[3,384,128]{2,1,0:T(8,128)(2,1)}, u32[]{:S(2)}) copy-start(bf16[3,384,128]{2,1,0:T(8,128)(2,1)} %param.17) | copy-start | bytes 884740
  7.2 7.0 %copy-start.10 = (bf16[128,4]{0,1:T(4,128)(2,1)S(1)}, bf16[128,4]{0,1:T(4,128)(2,1)}, u32[]{:S(2)}) copy-start(bf16[128,4]{0,1:T(4,128)(2,1)} %param.22) | copy-start | bytes 3076
  7.2 266.3 %all-gather.2.cloned.1.call-start = ((), (), s32[]{:S(2)}) async-start(), calls=%async_computation.7 | async-start | bytes 19021824 | tf_op jit(solution)/shard_map/all_gather | solution.py:173
  10.7 16.7 %copy-start.1 = (bf16[2,384,256]{2,1,0:T(8,128)(2,1)S(1)}, bf16[2,384,256]{2,1,0:T(8,128)(2,1)}, u32[]{:S(2)}) copy-start(bf16[2,384,256]{2,1,0:T(8,128)(2,1)} %param.16) | copy-start | bytes 1179652
  12.2 15.7 %copy-start.5 = (s32[384]{0:T(512)S(1)}, s32[384]{0:T(512)}, u32[]{:S(2)}) copy-start(s32[384]{0:T(512)} %param.19) | copy-start | bytes 4612
  12.2 15.7 %copy-start.7 = (bf16[4,256,128]{2,1,0:T(8,128)(2,1)S(1)}, bf16[4,256,128]{2,1,0:T(8,128)(2,1)}, u32[]{:S(2)}) copy-start(bf16[4,256,128]{2,1,0:T(8,128)(2,1)} %param.20) | copy-start | bytes 786436
  15.7 31.9 %all-to-all-start = ((bf16[64,4,3,384]{3,1,2,0:T(4,128)(2,1)}), bf16[64,4,3,384]{3,1,2,0:T(4,128)(2,1)S(1)}, u32[]{:S(2)}, u32[]{:S(2)}) async-start(bf16[64,4,3,384]{3,1,2,0:T(4,128)(2,1)} %broadcast_in_dim.32), calls=%async_computation | async-start | bytes 1179648 | tf_op jit(solution)/shard_map/all_to_all | solution.py:17
  73.8 62.6 %all-to-all-start.2 = ((f32[2,2,384,256]{3,2,1,0:T(8,128)}), f32[2,2,384,256]{3,2,1,0:T(8,128)S(1)}, u32[]{:S(2)}, u32[]{:S(2)}) async-start(f32[2,2,384,256]{3,2,1,0:T(8,128)} %broadcast_in_dim.54), calls=%async_computation.2 | async-start | bytes 3145728 | tf_op jit(solution)/shard_map/all_to_all | solution.py:17
  136.5 7.8 %copy-start.6 = (s32[256]{0:T(256)S(1)}, s32[256]{0:T(256)}, u32[]{:S(2)}) copy-start(s32[256]{0:T(256)} %param.18) | copy-start | bytes 3076
  136.5 7.8 %copy-start.8 = (bf16[4,128,64]{1,2,0:T(8,128)(2,1)S(1)}, bf16[4,128,64]{1,2,0:T(8,128)(2,1)}, u32[]{:S(2)}) copy-start(bf16[4,128,64]{1,2,0:T(8,128)(2,1)} %param.25) | copy-start | bytes 196612
  137.8 20.7 %all-to-all-start.3 = ((bf16[2,384,256]{2,0,1:T(2,128)(2,1)}), bf16[2,384,256]{2,0,1:T(2,128)(2,1)S(1)}, u32[]{:S(2)}, u32[]{:S(2)}) async-start(bf16[2,384,256]{2,0,1:T(2,128)(2,1)} %copy.158), calls=%async_computation.3 | async-start | bytes 786432 | tf_op jit(solution)/shard_map/all_to_all | solution.py:130
  159.5 2.8 copy-start.3
  312.5 18.0 %copy-start.4 = (bf16[64,128]{1,0:T(8,128)(2,1)S(1)}, bf16[64,128]{1,0:T(8,128)(2,1)}, u32[]{:S(2)}) copy-start(bf16[64,128]{1,0:T(8,128)(2,1)} %param.26) | copy-start | bytes 49156
  313.2 13.6 %all-to-all-start.5 = ((f32[2,1,2304]{2,1,0:T(1,128)}), f32[2,1,2304]{2,1,0:T(1,128)S(1)}, u32[]{:S(2)}, u32[]{:S(2)}) async-start(f32[2,1,2304]{2,1,0:T(1,128)} %broadcast_in_dim.57), calls=%async_computation.5 | async-start | bytes 36864 | tf_op jit(solution)/shard_map/all_to_all | solution.py:17
  326.8 16.1 %all-to-all-start.4 = ((bf16[2,256,3,128]{1,3,2,0:T(8,128)(2,1)}), bf16[2,256,3,128]{1,3,2,0:T(8,128)(2,1)S(1)}, u32[]{:S(2)}, u32[]{:S(2)}) async-start(bf16[2,256,3,128]{1,3,2,0:T(8,128)(2,1)} %bitcast.203), calls=%async_computation.4 | async-start | bytes 786432 | tf_op jit(solution)/shard_map/all_to_all | solution.py:43
  330.3 26.5 %copy-start.9 = (bf16[128,64]{0,1:T(8,128)(2,1)S(1)}, bf16[128,64]{0,1:T(8,128)(2,1)}, u32[]{:S(2)}) copy-start(bf16[128,64]{0,1:T(8,128)(2,1)} %param.27) | copy-start | bytes 49156
  342.9 13.9 %all-to-all-start.6 = ((bf16[2,3,384,64]{2,3,1,0:T(8,128)(2,1)}), bf16[2,3,384,64]{2,3,1,0:T(8,128)(2,1)S(1)}, u32[]{:S(2)}, u32[]{:S(2)}) async-start(bf16[2,3,384,64]{2,3,1,0:T(8,128)(2,1)} %bitcast.204), calls=%async_computation.6 | async-start | bytes 589824 | tf_op jit(solution)/shard_map/all_to_all | solution.py:43
Sparse Core Ops, SparseCore 0:
  14.3 259.0 all-gather.1
where the time goes:
time: 370 us; the launch traced here: 365 us
  waiting for transfers between devices  213 us (58%)
  matrix products  67.9 us (18%)
  starting transfers between devices  36.6 us (10%)
  between operations  14.7 us (4%)
  local copies, waits for them, and re-layouts  13.3 us (4%)
  other arithmetic  9.59 us (3%)
  loops' own time  5.53 us (1%)
  blocking collectives  4.73 us (1%)
    all_gather x1, waiting for transfers between devices, per_device(): lax.all_gather(right, DAP, axis=1, tiled=True)  98.8 us
    all_to_all x3, waiting for transfers between devices, sent_to_all(): return lax.all_to_all(copies, axis, split_axis=0, concat_axis=0, tiled=True)  79.9 us
    dot_general x1, matrix products, per_device(): jnp.einsum('cik,cjk->cij', left, lax.all_gather(right, DAP, axis=1, tiled...  39 us
    all_to_all x3, starting transfers between devices, sent_to_all(): return lax.all_to_all(copies, axis, split_axis=0, concat_axis=0, tiled=True)  23.5 us
    all_to_all x2, waiting for transfers between devices, sum_at_owner(): lax.all_to_all(in_blocks(value, dim, devices), axis, 0, 0, tiled=True)  20.9 us
    all_to_all x1, waiting for transfers between devices, per_device(): lax.all_to_all(homolog_stack_lone, DAP, split_axis=1, concat_axis=0, tile...  13.1 us
    dot_general x5, matrix products, attend(): jnp.einsum('hqk,khd->qhd', weights, values, preferred_element_type=jnp.fl...  9.38 us
  transfers between devices with their start and end apart: 7, of which 7 were waited for; matrix products, arithmetic and copies ran while one was open for 12% of the time, Pallas kernels for 0%

commit v1 on v0

v1 whole, which is shorter than its diff:
```python
import jax
import jax.numpy as jnp
from jax import lax
from jax.sharding import Mesh
from jax.sharding import PartitionSpec as P

GROUP_BREADTH = 32
CHIPS = ("dap_0", "dap_1", "dap_2")
CORE = "dap_3"
DAP = CHIPS + (CORE,)

EPS = 1e-05
NEG = 1000000000.0


def sent_to_all(value, axis):
    copies = jnp.broadcast_to(value, (lax.axis_size(axis), *value.shape))
    return lax.all_to_all(copies, axis, split_axis=0, concat_axis=0, tiled=True)


def standardize_features(values):
    values = values.astype(jnp.float32)
    center = jnp.mean(values, axis=-1, keepdims=True)
    spread = jnp.mean(jnp.square(values - center), axis=-1, keepdims=True)
    return (values - center) * lax.rsqrt(spread + EPS)


def from_other_rep(arrays):
    sizes = [a.size for a in arrays]
    packed = jnp.concatenate([a.reshape(-1) for a in arrays])
    deep = lax.axis_size("dap_0")
    pairs = []
    for z in range(deep):
        for r in range(2):
            pairs.append((z * 2 + r, (deep - 1 - z) * 2 + (1 - r)))
    got = lax.ppermute(packed, ("dap_0", "rep"), pairs)
    outs, at = [], 0
    for a, n in zip(arrays, sizes):
        outs.append(got[at : at + n].reshape(a.shape))
        at += n
    return outs


def attend(query, keys, values, gate, bias):
    heads = query.shape[-1] // GROUP_BREADTH

    def split(x):
        return x.reshape(x.shape[0], heads, GROUP_BREADTH)

    scores = (
        jnp.einsum("qhd,khd->hqk", split(query), split(keys), preferred_element_type=jnp.float32)
        / jnp.sqrt(jnp.float32(GROUP_BREADTH))
        + bias
    )
    weights = jax.nn.softmax(scores, axis=-1).astype(jnp.bfloat16)
    mixed = jnp.einsum("hqk,khd->qhd", weights, split(values), preferred_element_type=jnp.float32)
    gated = mixed * jax.nn.sigmoid(split(gate).astype(jnp.float32))
    return gated.astype(jnp.bfloat16).reshape(query.shape)


def per_device(
    msa,
    pair,
    homolog_present,
    amino_present,
    row_w,
    row_out,
    offset_w,
    col_w,
    col_out,
    side_w,
    final_w,
    sigmoid_w,
):
    rep = lax.axis_index("rep")
    rows_here, sites = pair.shape[0], pair.shape[1]
    seqs_here, embed = msa.shape[0], msa.shape[2]
    chips = lax.axis_size(CHIPS)
    devices = lax.axis_size(DAP)
    row_start = lax.axis_index(DAP) * rows_here
    res_float = amino_present.astype(jnp.float32)
    mask_rows = lax.dynamic_slice_in_dim(res_float, row_start, rows_here, 0)

    offset_o, side_o, final_o = from_other_rep([offset_w, side_w, final_w])
    row_w_o, row_out_o = from_other_rep([row_w, row_out])
    col_w_o, col_out_o = from_other_rep([col_w, col_out])
    offset_all = jnp.concatenate([offset_w, offset_o], 1)
    side_all = jnp.concatenate([side_w, side_o], 2)
    row_all = jnp.concatenate([row_w, row_w_o], 2)
    row_out_all = jnp.concatenate([row_out, row_out_o], 0)
    col_all = jnp.concatenate([col_w, col_w_o], 2)
    col_out_all = jnp.concatenate([col_out, col_out_o], 0)
    final_all = jnp.concatenate([final_w, final_o], 0)

    pair_ln = standardize_features(pair).astype(jnp.bfloat16)
    local_bias = jnp.einsum(
        "ijc,ch->hij", pair_ln, offset_all, preferred_element_type=jnp.float32
    ).astype(jnp.bfloat16)
    heads = local_bias.shape[0]
    near = lax.all_to_all(local_bias.reshape(2, heads // 2, rows_here, sites), CORE, 0, 0, tiled=True)
    mine = lax.dynamic_index_in_dim(near, rep, 0, keepdims=False)
    far = sent_to_all(mine, CHIPS)
    both = sent_to_all(far, CORE)
    pair_bias = both.transpose(0, 2, 1, 3, 4).reshape(heads, chips * rows_here, sites)
    row_bias = pair_bias.astype(jnp.float32) + NEG * (res_float - 1.0)[None, None, :]

    pair_mask = mask_rows[:, None] * res_float[None, :]

    def gated_side(gate_weight, value_weight):
        gate = jnp.einsum("ikd,dc->cik", pair_ln, gate_weight, preferred_element_type=jnp.float32)
        value = jnp.einsum("ikd,dc->cik", pair_ln, value_weight, preferred_element_type=jnp.float32)
        return (jax.nn.sigmoid(gate) * value * pair_mask[None]).astype(jnp.bfloat16)

    sides = jnp.stack([gated_side(side_all[0], side_all[1]), gated_side(side_all[2], side_all[3])], 1)
    sides = lax.all_to_all(sides, DAP, 0, 0, tiled=True)
    sides = sides.transpose(1, 0, 2, 3).reshape(2, devices * rows_here, sites)
    product = jnp.einsum("ik,jk->ij", sides[0], sides[1], preferred_element_type=jnp.float32)
    product = product.astype(jnp.bfloat16).reshape(devices, rows_here, sites)
    product = lax.all_to_all(product, DAP, 0, 0, tiled=True).astype(jnp.float32)

    normed = standardize_features(msa).astype(jnp.bfloat16)

    def of_rep(x):
        blocks = x.reshape(seqs_here, chips, 2, rows_here, embed)
        return lax.dynamic_index_in_dim(blocks, rep, 2, keepdims=False).reshape(
            seqs_here, chips * rows_here, embed
        )

    def project(x, weight):
        return jnp.dot(x, weight, preferred_element_type=jnp.float32).astype(jnp.bfloat16)

    normed_q = of_rep(normed)
    row_parts = (
        project(normed_q, row_all[0]),
        project(normed, row_all[1]),
        project(normed, row_all[2]),
        project(normed_q, row_all[3]),
    )
    row_mixed = lax.map(lambda parts: attend(*parts, row_bias), row_parts)
    msa_one = (
        of_rep(msa).astype(jnp.float32)
        + jnp.dot(row_mixed, row_out_all, preferred_element_type=jnp.float32)
    ).astype(jnp.bfloat16)

    blocks = msa_one.reshape(seqs_here, chips, rows_here, embed).transpose(1, 0, 2, 3)
    blocks = jnp.broadcast_to(blocks[:, None], (chips, 2, *blocks.shape[1:]))
    blocks = blocks.reshape(chips * 2, *blocks.shape[2:])
    blocks = lax.all_to_all(blocks, CHIPS + ("rep",), 0, 0, tiled=True)
    blocks = blocks.reshape(chips, 2, *blocks.shape[1:]).swapaxes(0, 1)
    blocks = lax.all_to_all(blocks, CORE, 0, 0, tiled=True)
    column = blocks.transpose(1, 0, 2, 3, 4).reshape(-1, rows_here, embed)

    column_normed = standardize_features(column).astype(jnp.bfloat16).swapaxes(0, 1)
    col_parts = tuple(project(column_normed, col_all[n]) for n in range(4))
    col_bias = (NEG * (homolog_present.astype(jnp.float32) - 1.0))[None, None, :]
    col_mixed = lax.map(lambda parts: attend(*parts, col_bias), col_parts)
    width = embed // 2
    col_half = lax.dynamic_slice_in_dim(col_out_all, rep * width, width, 1)
    column_delta = jnp.einsum("rsd,dz->srz", col_mixed, col_half, preferred_element_type=jnp.float32)
    retained = lax.dynamic_slice_in_dim(column, rep * width, width, 2)
    alignment_output = (retained.astype(jnp.float32) + column_delta).astype(jnp.bfloat16)

    mean = jnp.mean(product, axis=0)
    square = jnp.mean(product * product, axis=0)
    scaled = ((product - mean) * lax.rsqrt(square - mean * mean + EPS)).astype(jnp.bfloat16)
    half = pair.shape[2] // 2
    final_half = lax.dynamic_slice_in_dim(final_all, rep * half, half, 1)
    tri_update = jnp.einsum("cij,cz->ijz", scaled, final_half, preferred_element_type=jnp.float32)
    pair_half = lax.dynamic_slice_in_dim(pair, rep * half, half, 2)
    gate_out = jax.nn.sigmoid(jnp.dot(pair_ln, sigmoid_w, preferred_element_type=jnp.float32))
    pair_output = (pair_half.astype(jnp.float32) + gate_out * tri_update).astype(jnp.bfloat16)
    return (alignment_output, pair_output)


def solution(mesh):
    finer = Mesh(
        mesh.devices.reshape(4, 4, 4, 2, mesh.shape["rep"]),
        (*DAP, "rep"),
    )
    return jax.shard_map(
        per_device,
        mesh=finer,
        in_specs=(
            P(DAP, None, None),
            P(DAP, None, None),
            P(),
            P(),
            P(None, None, "rep"),
            P("rep", None),
            P(None, "rep"),
            P(None, None, "rep"),
            P("rep", None),
            P(None, None, "rep"),
            P("rep", None),
            P(None, "rep"),
        ),
        out_specs=(P(None, DAP, "rep"), P(DAP, None, "rep")),
        check_vma=False,
    )
```

time: 370 us -> 181 us (0.49)
  the two profiles are of different devices: /device:TPU:32 before, /device:TPU:1 now
where the time goes in v1:
time: 181 us; the launch traced here: 180 us
  starting transfers between devices  45.8 us (25%)
  local copies, waits for them, and re-layouts  41.5 us (23%)
  matrix products  29.7 us (16%)
  waiting for transfers between devices  28 us (15%)
  blocking collectives  17.6 us (10%)
  other arithmetic  15.8 us (9%)
    all_to_all x1, starting transfers between devices, per_device(): blocks = lax.all_to_all(blocks, CHIPS + ('rep',), 0, 0, tiled=True)  12.3 us
    all_to_all x1, waiting for transfers between devices, per_device(): blocks = lax.all_to_all(blocks, CHIPS + ('rep',), 0, 0, tiled=True)  11.7 us
    all_to_all x1, starting transfers between devices, sent_to_all(): return lax.all_to_all(copies, axis, split_axis=0, concat_axis=0, tiled=True)  11.2 us
    all_to_all x1, waiting for transfers between devices, sent_to_all(): return lax.all_to_all(copies, axis, split_axis=0, concat_axis=0, tiled=True)  10.3 us
    ppermute x3, starting transfers between devices, from_other_rep(): got = lax.ppermute(packed, ('dap_0', 'rep'), pairs)  9.16 us
    dot_general x5, matrix products, attend(): jnp.einsum('hqk,khd->qhd', weights, split(values), preferred_element_type...  8.81 us
    unnamed x54, local copies, waits for them, and re-layouts  8.11 us
    all_to_all x1, starting transfers between devices, per_device(): product = lax.all_to_all(product, DAP, 0, 0, tiled=True).astype(jnp.float32)  7.42 us
  transfers between devices with their start and end apart: 7, of which 3 were waited for; matrix products, arithmetic and copies ran while one was open for 34% of the time, Pallas kernels for 0%

profile of v1, /device:TPU:1, one launch (start us, length us, event | category | flops | bytes accessed | tf_op | source)
XLA Modules:
  0.0 180.0 jit_solution(16347737203349939827)
XLA Ops:
  0.7 1.0 copy.126
  1.8 0.8 copy.125
  3.5 6.5 %collective-permute-start.1 = (bf16[41472]{0:T(1024)(128)(2,1)S(1)}, bf16[41472]{0:T(1024)(128)(2,1)S(1)}, u32[]{:S(2)}, u32[]{:S(2)}) collective-permute-start(bf16[41472]{0:T(1024)(128)(2,1)S(1)} %pad_maximum_fusion.5), channel_id=1, source_target_pairs={{0,193},{1,192},{64,129},{65,128},{128,65},{129,64},{192,1},{193,0... | collective-permute-start | bytes 248840 | tf_op jit(solution)/shard_map/ppermute | solution.py:36
  10.0 0.9 copy.176
  10.9 1.7 pad_maximum_fusion.1
  12.6 0.9 copy.177
  13.5 1.7 pad_maximum_fusion.2
  15.2 2.7 %collective-permute-start.2 = (bf16[163840]{0:T(1024)(128)(2,1)}, bf16[163840]{0:T(1024)(128)(2,1)S(1)}, u32[]{:S(2)}, u32[]{:S(2)}) collective-permute-start(bf16[163840]{0:T(1024)(128)(2,1)} %pad_maximum_fusion.2), channel_id=1, source_target_pairs={{0,193},{1,192},{64,129},{65,128},{128,65},{129,64},{192,1},{193,0... | collective-permute-start | bytes 983048 | tf_op jit(solution)/shard_map/ppermute | solution.py:36
  17.9 1.4 copy.157
  20.0 1.3 add_multiply_fusion
  24.1 0.9 bitcast_convert_fusion
  25.6 1.3 fusion.34
  27.0 0.8 copy.175
  28.9 4.9 %all_to_all.35 = bf16[2,4,3,384]{3,1,2,0:T(4,128)(2,1)S(1)} all-to-all(bf16[2,4,3,384]{3,1,2,0:T(4,128)(2,1)S(1)} %copy.128), channel_id=1, replica_groups=mesh['dap_0'=4,'dap_1'=4,'dap_2'=4,'dap_3'=2,'rep'=2] {'dap_3'}, dimensions={0} | all-to-all | bytes 36864 | tf_op jit(solution)/shard_map/all_to_all | solution.py:100
  33.8 1.0 broadcast_in_dim.22
  34.7 11.2 %all-to-all-start.1 = ((bf16[64,4,3,384]{3,1,2,0:T(4,128)(2,1)}), bf16[64,4,3,384]{3,1,2,0:T(4,128)(2,1)S(1)}, u32[]{:S(2)}, u32[]{:S(2)}) async-start(bf16[64,4,3,384]{3,1,2,0:T(4,128)(2,1)} %broadcast_in_dim.22), calls=%async_computation.1 | async-start | bytes 1179648 | tf_op jit(solution)/shard_map/all_to_all | solution.py:18
  47.2 1.3 fusion.25
  49.2 1.4 copy.156
  52.0 1.0 slice.152
  53.0 0.9 convolution_convert_fusion.7
  53.9 10.3 %all-to-all-done.1 = bf16[64,4,3,384]{3,1,2,0:T(4,128)(2,1)S(1)} async-done(((bf16[64,4,3,384]{3,1,2,0:T(4,128)(2,1)}), bf16[64,4,3,384]{3,1,2,0:T(4,128)(2,1)S(1)}, u32[]{:S(2)}, u32[]{:S(2)}) %all-to-all-start.1) | async-done | bytes 589856 | tf_op jit(solution)/shard_map/all_to_all | solution.py:18
  64.5 6.5 %all_to_all.36 = bf16[2,64,4,3,384]{4,2,3,1,0:T(4,128)(2,1)S(1)} all-to-all(bf16[2,64,4,3,384]{4,2,3,1,0:T(4,128)(2,1)S(1)} %broadcast_in_dim.23), channel_id=1, replica_groups=mesh['dap_0'=4,'dap_1'=4,'dap_2'=4,'dap_3'=2,'rep'=2] {'dap_3'}, dimensions={0} | all-to-all | bytes 2359296 | tf_op jit(solution)/shard_map/all_to_all | solution.py:18
  71.0 5.7 %all-to-all-start.5 = ((bf16[128,2,3,384]{3,1,2,0:T(2,128)(2,1)}), bf16[128,2,3,384]{3,1,2,0:T(2,128)(2,1)S(1)}, u32[]{:S(2)}, u32[]{:S(2)}) async-start(bf16[128,2,3,384]{3,1,2,0:T(2,128)(2,1)} %copy.156), calls=%async_computation.5 | async-start | bytes 1179648 | tf_op jit(solution)/shard_map/all_to_all | solution.py:115
  76.7 0.9 convolution_convert_fusion.8
  77.6 0.8 slice.160
  80.5 1.0 slice.162
  81.5 1.0 convolution_convert_fusion.4
  82.5 1.0 convolution_convert_fusion.5
  83.8 1.8 %copy.129 = f32[2,4,64,3,384]{4,1,0,3,2:T(4,128)} copy(f32[2,4,64,3,384]{4,1,3,2,0:T(4,128)S(1)} %convert_bitcast_fusion) | data formatting | bytes 4718592 | tf_op jit(solution)/shard_map/convert_element_type | solution.py:105
  85.7 2.7 %reshape.285 = f32[8,192,384]{2,0,1:T(8,128)S(1)} reshape(f32[2,4,64,3,384]{4,1,0,3,2:T(4,128)} %copy.129) | data formatting | bytes 4718592 | tf_op jit(solution)/shard_map/convert_element_type | solution.py:105
  88.5 1.8 %copy.134 = f32[8,192,384]{2,1,0:T(8,128)} copy(f32[8,192,384]{2,0,1:T(8,128)S(1)} %broadcast_add_fusion) | data formatting | bytes 4718592 | tf_op jit(solution)/shard_map/while | solution.py:139
  90.3 6.1 %all-to-all-done.5 = bf16[128,2,3,384]{3,1,2,0:T(2,128)(2,1)S(1)} async-done(((bf16[128,2,3,384]{3,1,2,0:T(2,128)(2,1)}), bf16[128,2,3,384]{3,1,2,0:T(2,128)(2,1)S(1)}, u32[]{:S(2)}, u32[]{:S(2)}) %all-to-all-start.5) | async-done | bytes 589856 | tf_op jit(solution)/shard_map/all_to_all | solution.py:115
  96.4 3.3 %slice_reduce_fusion = (bf16[128,3,384]{2,1,0:T(4,128)(2,1)S(1)}, bf16[128,3,384]{2,1,0:T(4,128)(2,1)S(1)}) fusion(bf16[2,128,3,384]{3,0,2,1:T(2,128)(2,1)S(1)} %bitcast.223), kind=kLoop, calls=%fused_computation.110 | loop fusion | bytes 1179648 | tf_op jit(solution)/shard_map/slice | solution.py:117
  100.6 0.9 reshape.279
  101.4 7.4 %all-to-all-start.6 = ((bf16[128,3,384]{2,1,0:T(4,128)(2,1)}), bf16[128,3,384]{2,1,0:T(4,128)(2,1)}, u32[]{:S(2)}, u32[]{:S(2)}) async-start(bf16[128,3,384]{2,1,0:T(4,128)(2,1)} %reshape.279), calls=%async_computation.6 | async-start | bytes 786432 | tf_op jit(solution)/shard_map/all_to_all | solution.py:119
  108.9 18.6 %while.20 = (s32[]{:T(128)}, bf16[2,192,256]{1,2,0:T(8,128)(2,1)}, bf16[2,384,256]{2,1,0:T(8,128)(2,1)}, bf16[2,192,256]{2,1,0:T(8,128)(2,1)}, bf16[2,384,256]{2...) while((s32[]{:T(128)}, bf16[2,192,256]{1,2,0:T(8,128)(2,1)}, ...), condition=%wide.region_7.8_spmd, body=%wide.region_4.7_spmd.sunk | while | flops 79923456 | bytes 13120093 | solution.py:139
  108.9 1.1 constant_dynamic-slice_fusion.17
  110.1 1.0 constant_dynamic-slice_fusion.16
  111.2 2.2 %multiply_add_fusion.9 = f32[8,192,384]{2,1,0:T(8,128)S(1)} fusion(f32[8,192,384]{2,1,0:T(8,128)} %get-tuple-element.304, bf16[192,8,32]{0,2,1:T(8,128)(2,1)S(1)} %bitcast.209, bf16[384,8,32]{0,2,1:T(8,128)(2,1)S(1)} %bitcast.208), kind=kOutput, calls=%fused_computation.3.clone.1 | convolution fusion | flops 38928384 | bytes 5013504 | tf_op jit(solution)/shard_map/while/body/eval_jaxpr/qhd,khd->hqk/dot_general | solution.py:51
  113.4 0.9 fusion.167
  114.6 2.8 %fusion.168 = bf16[192,8,32]{0,2,1:T(8,128)(2,1)S(1)} fusion(f32[192,8,32]{0,2,1:T(8,128)S(1)} %bitcast.221, bf16[384,8,32]{0,2,1:T(8,128)(2,1)S(1)} %bitcast.224, f32[8,192]{1,0:T(8,128)S(1)} %fusion.167, f32[8,192,384]{2,1,0:T(8,128)S(1)} %multiply_add_fusion.9), kind=kOutput, calls=%fused_computation.7.clone.1 | convolution fusion | flops 39618432 | bytes 2856960 | tf_op jit(solution)/shard_map/while/body/eval_jaxpr/hqk,khd->qhd/dot_general | solution.py:56
  118.2 1.0 constant_dynamic-slice_fusion.17
  119.4 1.0 constant_dynamic-slice_fusion.16
  120.5 2.2 %multiply_add_fusion.9 = f32[8,192,384]{2,1,0:T(8,128)S(1)} fusion(f32[8,192,384]{2,1,0:T(8,128)} %get-tuple-element.304, bf16[192,8,32]{0,2,1:T(8,128)(2,1)S(1)} %bitcast.209, bf16[384,8,32]{0,2,1:T(8,128)(2,1)S(1)} %bitcast.208), kind=kOutput, calls=%fused_computation.3.clone.1 | convolution fusion | flops 38928384 | bytes 5013504 | tf_op jit(solution)/shard_map/while/body/eval_jaxpr/qhd,khd->hqk/dot_general | solution.py:51
  122.7 0.9 fusion.167
  123.9 2.8 %fusion.168 = bf16[192,8,32]{0,2,1:T(8,128)(2,1)S(1)} fusion(f32[192,8,32]{0,2,1:T(8,128)S(1)} %bitcast.221, bf16[384,8,32]{0,2,1:T(8,128)(2,1)S(1)} %bitcast.224, f32[8,192]{1,0:T(8,128)S(1)} %fusion.167, f32[8,192,384]{2,1,0:T(8,128)S(1)} %multiply_add_fusion.9), kind=kOutput, calls=%fused_computation.7.clone.1 | convolution fusion | flops 39618432 | bytes 2856960 | tf_op jit(solution)/shard_map/while/body/eval_jaxpr/hqk,khd->qhd/dot_general | solution.py:56
  127.5 1.4 fusion.29
  129.2 0.9 broadcast_in_dim.24
  130.1 12.3 %all-to-all-start.3 = ((bf16[128,2,3,256]{3,1,2,0:T(2,128)(2,1)}), bf16[128,2,3,256]{3,1,2,0:T(2,128)(2,1)S(1)}, u32[]{:S(2)}, u32[]{:S(2)}) async-start(bf16[128,2,3,256]{3,1,2,0:T(2,128)(2,1)} %bitcast.34), calls=%async_computation.3 | async-start | bytes 786432 | tf_op jit(solution)/shard_map/all_to_all | solution.py:148
  142.4 1.3 convert_reduce_fusion
  143.7 1.2 fusion.45
  145.0 0.9 fusion.37
  145.9 11.7 %all-to-all-done.3 = bf16[128,2,3,256]{3,1,2,0:T(2,128)(2,1)S(1)} async-done(((bf16[128,2,3,256]{3,1,2,0:T(2,128)(2,1)}), bf16[128,2,3,256]{3,1,2,0:T(2,128)(2,1)S(1)}, u32[]{:S(2)}, u32[]{:S(2)}) %all-to-all-start.3) | async-done | bytes 393248 | tf_op jit(solution)/shard_map/all_to_all | solution.py:148
  157.8 6.2 %all_to_all.37 = bf16[2,64,2,3,256]{4,2,1,3,0:T(2,128)(2,1)S(1)} all-to-all(bf16[2,64,2,3,256]{4,2,1,3,0:T(2,128)(2,1)S(1)} %bitcast.235), channel_id=1, replica_groups=mesh['dap_0'=4,'dap_1'=4,'dap_2'=4,'dap_3'=2,'rep'=2] {'dap_3'}, dimensions={0} | all-to-all | bytes 786432 | tf_op jit(solution)/shard_map/all_to_all | solution.py:150
  164.7 0.9 fusion.43
  168.4 9.4 %while.21 = (s32[]{:T(128)}, bf16[3,256,256]{1,2,0:T(8,128)(2,1)}, bf16[3,256,256]{2,1,0:T(8,128)(2,1)S(1)}, bf16[3,256,256]{2,1,0:T(8,128)(2,1)S(1)}, bf16[3,25...) while((s32[]{:T(128)}, bf16[3,256,256]{1,2,0:T(8,128)(2,1)}, ...), condition=%wide.region_13.14_spmd, body=%wide.region_10.13_spmd.sunk | while | flops 105777664 | bytes 3820125 | solution.py:156
  168.7 0.8 fusion.174
  169.8 1.0 fusion.175
  171.8 0.8 fusion.174
  172.9 1.0 fusion.175
  174.9 0.8 fusion.174
  176.1 1.0 fusion.175
  178.0 1.2 fusion.30
  179.2 0.8 copy.160
  (152 shorter events, 23.2 us)
Async XLA Ops:
  0.6 25.0 %copy-start = (bf16[128,64]{0,1:T(8,128)(2,1)S(1)}, bf16[128,64]{0,1:T(8,128)(2,1)}, u32[]{:S(2)}) copy-start(bf16[128,64]{0,1:T(8,128)(2,1)} %param.27) | copy-start | bytes 49156
  0.6 21.2 %copy-start.10 = (bf16[128,256]{1,0:T(8,128)(2,1)S(1)}, bf16[128,256]{1,0:T(8,128)(2,1)}, u32[]{:S(2)}) copy-start(bf16[128,256]{1,0:T(8,128)(2,1)} %param.24) | copy-start | bytes 196612
  0.7 20.6 %copy-start.4 = (bf16[2,384,256]{2,1,0:T(8,128)(2,1)S(1)}, bf16[2,384,256]{2,1,0:T(8,128)(2,1)}, u32[]{:S(2)}) copy-start(bf16[2,384,256]{2,1,0:T(8,128)(2,1)} %param.16) | copy-start | bytes 1179652
  0.7 21.5 %copy-start.1 = (bf16[3,384,128]{2,1,0:T(8,128)(2,1)S(1)}, bf16[3,384,128]{2,1,0:T(8,128)(2,1)}, u32[]{:S(2)}) copy-start(bf16[3,384,128]{2,1,0:T(8,128)(2,1)} %param.17) | copy-start | bytes 884740
  3.5 24.4 %collective-permute-start.1 = (bf16[41472]{0:T(1024)(128)(2,1)S(1)}, bf16[41472]{0:T(1024)(128)(2,1)S(1)}, u32[]{:S(2)}, u32[]{:S(2)}) collective-permute-start(bf16[41472]{0:T(1024)(128)(2,1)S(1)} %pad_maximum_fusion.5), channel_id=1, source_target_pairs={{0,193},{1,192},{64,129},{65,128},{128,65},{129,64},{192,1},{193,0... | collective-permute-start | bytes 248840 | tf_op jit(solution)/shard_map/ppermute | solution.py:36
  12.6 39.4 %collective-permute-start = (bf16[163840]{0:T(1024)(128)(2,1)}, bf16[163840]{0:T(1024)(128)(2,1)}, u32[]{:S(2)}, u32[]{:S(2)}) collective-permute-start(bf16[163840]{0:T(1024)(128)(2,1)} %pad_maximum_fusion.1), channel_id=1, source_target_pairs={{0,193},{1,192},{64,129},{65,128},{128,65},{129,64},{192,1},{193,0... | collective-permute-start | bytes 983048 | tf_op jit(solution)/shard_map/ppermute | solution.py:36
  15.2 63.9 %collective-permute-start.2 = (bf16[163840]{0:T(1024)(128)(2,1)}, bf16[163840]{0:T(1024)(128)(2,1)S(1)}, u32[]{:S(2)}, u32[]{:S(2)}) collective-permute-start(bf16[163840]{0:T(1024)(128)(2,1)} %pad_maximum_fusion.2), channel_id=1, source_target_pairs={{0,193},{1,192},{64,129},{65,128},{128,65},{129,64},{192,1},{193,0... | collective-permute-start | bytes 983048 | tf_op jit(solution)/shard_map/ppermute | solution.py:36
  21.4 3.6 %copy-start.20 = (s32[256]{0:T(256)S(1)}, s32[256]{0:T(256)}, u32[]{:S(2)}) copy-start(s32[256]{0:T(256)} %param.18) | copy-start | bytes 3076
  22.2 24.4 %copy-start.16 = (f32[3,384]{1,0:T(4,128)}, f32[3,384]{1,0:T(4,128)S(1)}, u32[]{:S(2)}) copy-start(f32[3,384]{1,0:T(4,128)S(1)} %broadcast_multiply_fusion.1) | copy-start | bytes 13828
  22.8 23.8 %copy-start.14 = (f32[3,384]{1,0:T(4,128)}, f32[3,384]{1,0:T(4,128)S(1)}, u32[]{:S(2)}) copy-start(f32[3,384]{1,0:T(4,128)S(1)} %add_rsqrt_fusion.2) | copy-start | bytes 13828
  23.8 4.5 %copy-start.19 = (bf16[128,4]{0,1:T(4,128)(2,1)S(1)}, bf16[128,4]{0,1:T(4,128)(2,1)}, u32[]{:S(2)}) copy-start(bf16[128,4]{0,1:T(4,128)(2,1)} %param.22) | copy-start | bytes 3076
  26.9 19.1 %copy-start.6 = (bf16[4,128,64]{1,2,0:T(8,128)(2,1)S(1)}, bf16[4,128,64]{1,2,0:T(8,128)(2,1)}, u32[]{:S(2)}) copy-start(bf16[4,128,64]{1,2,0:T(8,128)(2,1)} %param.25) | copy-start | bytes 196612
  27.9 18.1 %copy-start.13 = (bf16[41472]{0:T(1024)(128)(2,1)}, bf16[41472]{0:T(1024)(128)(2,1)S(1)}, u32[]{:S(2)}) copy-start(bf16[41472]{0:T(1024)(128)(2,1)S(1)} %collective-permute-done.1) | copy-start | bytes 248836
  34.7 29.4 %all-to-all-start.1 = ((bf16[64,4,3,384]{3,1,2,0:T(4,128)(2,1)}), bf16[64,4,3,384]{3,1,2,0:T(4,128)(2,1)S(1)}, u32[]{:S(2)}, u32[]{:S(2)}) async-start(bf16[64,4,3,384]{3,1,2,0:T(4,128)(2,1)} %broadcast_in_dim.22), calls=%async_computation.1 | async-start | bytes 1179648 | tf_op jit(solution)/shard_map/all_to_all | solution.py:18
  47.2 1.4 copy-start.15
  47.2 1.4 copy-start.17
  48.5 4.5 %copy-start.2 = (bf16[4,256,128]{2,1,0:T(8,128)(2,1)S(1)}, bf16[4,256,128]{2,1,0:T(8,128)(2,1)}, u32[]{:S(2)}) copy-start(bf16[4,256,128]{2,1,0:T(8,128)(2,1)} %param.20) | copy-start | bytes 786436
  71.0 25.4 %all-to-all-start.5 = ((bf16[128,2,3,384]{3,1,2,0:T(2,128)(2,1)}), bf16[128,2,3,384]{3,1,2,0:T(2,128)(2,1)S(1)}, u32[]{:S(2)}, u32[]{:S(2)}) async-start(bf16[128,2,3,384]{3,1,2,0:T(2,128)(2,1)} %copy.156), calls=%async_computation.5 | async-start | bytes 1179648 | tf_op jit(solution)/shard_map/all_to_all | solution.py:115
  79.1 0.7 copy-start.7
  85.7 2.7 %copy-start.18 = (f32[384]{0:T(512)S(1)}, f32[384]{0:T(512)}, u32[]{:S(2)}) copy-start(f32[384]{0:T(512)} %add_multiply_fusion) | copy-start | bytes 4612
  101.4 27.7 %all-to-all-start.6 = ((bf16[128,3,384]{2,1,0:T(4,128)(2,1)}), bf16[128,3,384]{2,1,0:T(4,128)(2,1)}, u32[]{:S(2)}, u32[]{:S(2)}) async-start(bf16[128,3,384]{2,1,0:T(4,128)(2,1)} %reshape.279), calls=%async_computation.6 | async-start | bytes 786432 | tf_op jit(solution)/shard_map/all_to_all | solution.py:119
  127.5 17.4 %copy-start.5 = (bf16[3,384,64]{1,2,0:T(8,128)(2,1)S(1)}, bf16[3,384,64]{1,2,0:T(8,128)(2,1)}, u32[]{:S(2)}) copy-start(bf16[3,384,64]{1,2,0:T(8,128)(2,1)} %copy.175) | copy-start | bytes 442372
  127.5 17.5 %copy-start.8 = (f32[3,384,64]{1,2,0:T(8,128)S(1)}, f32[3,384,64]{1,2,0:T(8,128)}, u32[]{:S(2)}) copy-start(f32[3,384,64]{1,2,0:T(8,128)} %fusion.34) | copy-start | bytes 884740
  127.5 17.5 %copy-start.11 = (bf16[64,128]{0,1:T(8,128)(2,1)S(1)}, bf16[64,128]{0,1:T(8,128)(2,1)}, u32[]{:S(2)}) copy-start(bf16[64,128]{0,1:T(8,128)(2,1)} %copy.157) | copy-start | bytes 49156
  127.5 17.5 %copy-start.12 = (bf16[64,128]{0,1:T(8,128)(2,1)S(1)}, bf16[64,128]{0,1:T(8,128)(2,1)}, u32[]{:S(2)}) copy-start(bf16[64,128]{0,1:T(8,128)(2,1)} %copy.158) | copy-start | bytes 49156
  130.1 27.5 %all-to-all-start.3 = ((bf16[128,2,3,256]{3,1,2,0:T(2,128)(2,1)}), bf16[128,2,3,256]{3,1,2,0:T(2,128)(2,1)S(1)}, u32[]{:S(2)}, u32[]{:S(2)}) async-start(bf16[128,2,3,256]{3,1,2,0:T(2,128)(2,1)} %bitcast.34), calls=%async_computation.3 | async-start | bytes 786432 | tf_op jit(solution)/shard_map/all_to_all | solution.py:148
  164.0 2.8 %copy-start.3 = (bf16[4,256,128]{2,1,0:T(8,128)(2,1)S(1)}, bf16[4,256,128]{2,1,0:T(8,128)(2,1)}, u32[]{:S(2)}) copy-start(bf16[4,256,128]{2,1,0:T(8,128)(2,1)} %param.23) | copy-start | bytes 786436
  166.8 1.6 copy-start.21
  168.4 9.6 %copy-start.9 = (bf16[128,256]{0,1:T(8,128)(2,1)S(1)}, bf16[128,256]{0,1:T(8,128)(2,1)}, u32[]{:S(2)}) copy-start(bf16[128,256]{0,1:T(8,128)(2,1)} %copy.143) | copy-start | bytes 196612

commit v2 on v1

v2 whole, which is shorter than its diff:
```python
import functools

import jax
import jax.numpy as jnp
from jax import lax
from jax.experimental import pallas as pl
from jax.experimental.pallas import tpu as pltpu
from jax.sharding import Mesh
from jax.sharding import PartitionSpec as P

GROUP_BREADTH = 32
CHIPS = ("dap_0", "dap_1", "dap_2")
CORE = "dap_3"
DAP = CHIPS + (CORE,)
MESH = pl.DeviceIdType.MESH
VMEM = pl.BlockSpec(memory_space=pltpu.VMEM)

EPS = 1e-05
NEG = 1000000000.0


def standardize_features(values):
    values = values.astype(jnp.float32)
    center = jnp.mean(values, axis=-1, keepdims=True)
    spread = jnp.mean(jnp.square(values - center), axis=-1, keepdims=True)
    return (values - center) * lax.rsqrt(spread + EPS)


def place():
    z, x, y = (lax.axis_index(a) for a in CHIPS)
    return z, x, y, lax.axis_index(CORE), lax.axis_index("rep")


def send(src, dst, sent, came, device):
    pltpu.make_async_remote_copy(
        src_ref=src, dst_ref=dst, send_sem=sent, recv_sem=came, device_id=device, device_id_type=MESH
    ).start()


def wait_bytes(ref, sem):
    pltpu.make_async_copy(ref, ref, sem).wait()


def first_exchange(
    bias,
    sides,
    row_w,
    col_w,
    row_o,
    col_o,
    final,
    bias_all,
    sides_all,
    row_wx,
    col_wx,
    row_ox,
    col_ox,
    final_x,
    s_sent,
    s_came,
    line_sent,
    line_came,
    plane_sent,
    plane_came,
    core_sent,
    core_came,
):
    z, x, y, c, r = place()
    deep, wide, high = 4, 4, 4
    plane = wide * high
    xy = x * high + y
    chip = z * plane + xy
    chunk = row_w.shape[0] // (2 * plane)
    mine = pl.ds(pl.multiple_of((c * plane + xy) * chunk, chunk), chunk)
    half = pl.ds(pl.multiple_of(c * plane * chunk, plane * chunk), plane * chunk)
    mirror = (deep - 1 - z, x, y, c, 1 - r)
    partner = (z, x, y, 1 - c, r)

    for dz in range(deep):
        zt = lax.rem(z + dz, deep)
        if dz == 0:

            @pl.when(c != r)
            def _():
                send(bias, bias_all.at[r, xy, z], line_sent.at[0], line_came.at[0], (zt, x, y, r, c))

            @pl.when(c == r)
            def _():
                bias_all[r, xy, z] = bias[...]

        else:
            send(bias, bias_all.at[r, xy, z], line_sent.at[0], line_came.at[0], (zt, x, y, r, c))
    send(row_w.at[mine], row_wx.at[mine], line_sent.at[1], line_came.at[1], mirror)
    send(col_w.at[mine], col_wx.at[mine], line_sent.at[2], line_came.at[2], mirror)
    o_half = pl.ds(pl.multiple_of(c * (row_o.shape[0] // 2), row_o.shape[0] // 2), row_o.shape[0] // 2)
    send(row_o.at[o_half], row_ox.at[o_half], line_sent.at[3], line_came.at[3], mirror)
    send(col_o.at[o_half], col_ox.at[o_half], line_sent.at[4], line_came.at[4], mirror)
    send(final, final_x, line_sent.at[5], line_came.at[5], mirror)

    me = chip * 2 + c
    chips = deep * plane
    sides_all[me] = sides[chip]
    send(sides.at[chip], sides_all.at[me], s_sent, s_came, partner)

    def to_owner(i, carry):
        to = lax.rem(chip + i, chips)
        zt, xt, yt = to // plane, lax.rem(to // high, wide), lax.rem(to, high)
        send(sides.at[to], sides_all.at[me], s_sent, s_came, (zt, xt, yt, 0, r))
        send(sides.at[to], sides_all.at[me], s_sent, s_came, (zt, xt, yt, 1, r))
        return carry

    lax.fori_loop(1, chips // 2, to_owner, 0)

    @pl.when(c == r)
    def _():
        wait_bytes(bias_all.at[0, 0, pl.ds(0, deep - 1)], line_came.at[0])

    @pl.when(c != r)
    def _():
        wait_bytes(bias_all.at[0, 0], line_came.at[0])

    wait_bytes(row_wx.at[mine], line_came.at[1])
    wait_bytes(col_wx.at[mine], line_came.at[2])

    def over_plane(i, carry):
        to = lax.rem(xy + i, plane)
        device = (z, to // high, lax.rem(to, high), c, r)
        send(bias_all.at[c, xy], bias_all.at[c, xy], plane_sent.at[0], plane_came.at[0], device)
        send(row_wx.at[mine], row_wx.at[mine], plane_sent.at[1], plane_came.at[1], device)
        send(col_wx.at[mine], col_wx.at[mine], plane_sent.at[2], plane_came.at[2], device)
        return carry

    lax.fori_loop(1, plane, over_plane, 0)
    lax.fori_loop(chips // 2, chips, to_owner, 0)

    rest = pl.ds(0, (plane - 1) * chunk)
    wait_bytes(row_ox.at[o_half], line_came.at[3])
    send(row_ox.at[o_half], row_ox.at[o_half], core_sent.at[3], core_came.at[3], partner)
    wait_bytes(col_ox.at[o_half], line_came.at[4])
    send(col_ox.at[o_half], col_ox.at[o_half], core_sent.at[4], core_came.at[4], partner)
    wait_bytes(bias_all.at[0, pl.ds(0, plane - 1)], plane_came.at[0])
    send(bias_all.at[c], bias_all.at[c], core_sent.at[0], core_came.at[0], partner)
    wait_bytes(row_wx.at[rest], plane_came.at[1])
    send(row_wx.at[half], row_wx.at[half], core_sent.at[1], core_came.at[1], partner)
    wait_bytes(col_wx.at[rest], plane_came.at[2])
    send(col_wx.at[half], col_wx.at[half], core_sent.at[2], core_came.at[2], partner)

    wait_bytes(final_x, line_came.at[5])
    wait_bytes(bias_all.at[0], core_came.at[0])
    wait_bytes(row_wx.at[half], core_came.at[1])
    wait_bytes(col_wx.at[half], core_came.at[2])
    wait_bytes(row_ox.at[o_half], core_came.at[3])
    wait_bytes(col_ox.at[o_half], core_came.at[4])
    wait_bytes(sides_all.at[pl.ds(0, 2 * chips - 1)], s_came)

    @pl.when(c == r)
    def _():
        wait_bytes(bias_all.at[0, 0, pl.ds(0, deep - 1)], line_sent.at[0])

    @pl.when(c != r)
    def _():
        wait_bytes(bias_all.at[0, 0], line_sent.at[0])

    wait_bytes(row_wx.at[mine], line_sent.at[1])
    wait_bytes(col_wx.at[mine], line_sent.at[2])
    wait_bytes(row_ox.at[o_half], line_sent.at[3])
    wait_bytes(col_ox.at[o_half], line_sent.at[4])
    wait_bytes(final_x, line_sent.at[5])
    wait_bytes(bias_all.at[0, pl.ds(0, plane - 1)], plane_sent.at[0])
    wait_bytes(row_wx.at[rest], plane_sent.at[1])
    wait_bytes(col_wx.at[rest], plane_sent.at[2])
    wait_bytes(bias_all.at[0], core_sent.at[0])
    wait_bytes(row_wx.at[half], core_sent.at[1])
    wait_bytes(col_wx.at[half], core_sent.at[2])
    wait_bytes(row_ox.at[o_half], core_sent.at[3])
    wait_bytes(col_ox.at[o_half], core_sent.at[4])
    wait_bytes(sides_all.at[pl.ds(0, 2 * chips - 1)], s_sent)


def second_exchange(seqs, rows, column, product, m_sent, m_came, p_sent, p_came):
    z, x, y, c, r = place()
    wide, high = 4, 4
    plane = wide * high
    chips = seqs.shape[0]
    chip = z * plane + x * high + y
    me = chip * 2 + c
    channel = r * chips + chip

    @pl.when(c == r)
    def _():
        column[me] = seqs[chip]

    @pl.when(c != r)
    def _():
        send(seqs.at[chip], column.at[me], m_sent, m_came, (z, x, y, r, r))

    send(seqs.at[chip], column.at[me], m_sent, m_came, (z, x, y, r, 1 - r))
    product[channel] = rows[chip]
    send(rows.at[chip], product.at[channel], p_sent, p_came, (z, x, y, c, 1 - r))

    def to_owner(i, carry):
        to = lax.rem(chip + i, chips)
        zt, xt, yt = to // plane, lax.rem(to // high, wide), lax.rem(to, high)
        for rt in range(2):
            send(seqs.at[to], column.at[me], m_sent, m_came, (zt, xt, yt, r, rt))
        return carry

    def to_rows(i, carry):
        to = lax.rem(chip + i, chips)
        zt, xt, yt = to // plane, lax.rem(to // high, wide), lax.rem(to, high)
        for rt in range(2):
            send(rows.at[to], product.at[channel], p_sent, p_came, (zt, xt, yt, c, rt))
        return carry

    lax.fori_loop(1, chips, to_owner, 0)
    lax.fori_loop(1, chips, to_rows, 0)

    for sem in (m_came, m_sent):


        @pl.when(c == r)
        def _():
            wait_bytes(column.at[pl.ds(0, 2 * chips - 1)], sem)

        @pl.when(c != r)
        def _():
            wait_bytes(column, sem)

    for sem in (p_came, p_sent):
        wait_bytes(product.at[pl.ds(0, 2 * chips - 1)], sem)


def exchange(kernel, outs, semaphores, *operands):
    return pl.pallas_call(
        kernel,
        out_shape=[jax.ShapeDtypeStruct(s, jnp.bfloat16) for s in outs],
        in_specs=[VMEM] * len(operands),
        out_specs=[VMEM] * len(outs),
        scratch_shapes=[
            pltpu.SemaphoreType.DMA if n == 0 else pltpu.SemaphoreType.DMA((n,)) for n in semaphores
        ],
        compiler_params=pltpu.CompilerParams(has_side_effects=True, vmem_limit_bytes=40 << 20),
    )(*operands)


def dot_last(a, b):
    return lax.dot_general(a, b, (((1,), (1,)), ((), ())), preferred_element_type=jnp.float32)


def dot(a, b):
    return jnp.dot(a, b, preferred_element_type=jnp.float32)


def project(x, own, other):
    return jnp.concatenate([dot(x, own), dot(x, other)], 1).astype(jnp.bfloat16)


def attend_rows(q, k, v, g, bias, mixed, block, heads):
    embed = q.shape[1]
    queries = q.shape[0]
    lane = lax.broadcasted_iota(jnp.int32, (heads, embed), 1) // GROUP_BREADTH
    head = lax.broadcasted_iota(jnp.int32, (heads, embed), 0)
    own = (lane == head).astype(jnp.float32)[None]
    scale = 1.0 / jnp.sqrt(jnp.float32(GROUP_BREADTH))

    for n in range(queries // block):
        part = slice(n * block, (n + 1) * block)
        wide = q[part].astype(jnp.float32)[:, None, :] * own
        wide = wide.reshape(block * heads, embed).astype(jnp.bfloat16)
        scores = dot_last(wide, k) * scale + bias(n)
        scores = jnp.exp(scores - jnp.max(scores, axis=1, keepdims=True))
        weights = (scores * (1.0 / jnp.sum(scores, axis=1, keepdims=True))).astype(jnp.bfloat16)
        out = dot(weights, v).reshape(block, heads, embed) * own
        out = jnp.sum(out, axis=1)
        gate = 1.0 / (1.0 + jnp.exp(-g[part].astype(jnp.float32)))
        mixed[part, :] = (out * gate).astype(jnp.bfloat16)


def row_kernel(
    msa, msa_q, bias_all, hidden, w, wx, wo, wox, out, bias_rows, mixed, *, heads, block
):
    r = lax.axis_index("rep")
    planes, deep = bias_all.shape[1], bias_all.shape[2]
    rows = bias_rows.shape[0] // (planes * deep)
    sites = bias_rows.shape[2]
    away = hidden[...]

    def place_bias(p, carry):
        at, level = lax.rem(p, planes), p // planes
        both = jnp.concatenate(
            [
                bias_all[r, at, level].astype(jnp.float32),
                bias_all[1 - r, at, level].astype(jnp.float32),
            ],
            0,
        )
        for t in range(rows):
            bias_rows[p * rows + t] = both[:, t * sites : (t + 1) * sites] + away
        return carry

    lax.fori_loop(0, planes * deep, place_bias, 0)

    def one(s, carry):
        x = standardize_features(msa[s]).astype(jnp.bfloat16)
        xq = standardize_features(msa_q[s]).astype(jnp.bfloat16)
        q = project(xq, w[0], wx[0])
        k = project(x, w[1], wx[1])
        v = project(x, w[2], wx[2])
        g = project(xq, w[3], wx[3])

        def bias(n):
            return bias_rows[n * block : (n + 1) * block].reshape(block * heads, sites)

        attend_rows(q, k, v, g, bias, mixed, block, heads)
        half = wo.shape[0]
        delta = dot(mixed[:, :half], wo[...]) + dot(mixed[:, half:], wox[...])
        out[s] = (msa_q[s].astype(jnp.float32) + delta).astype(jnp.bfloat16)
        return carry

    lax.fori_loop(0, msa.shape[0], one, 0)


def col_kernel(column, hidden, w, wx, wo, wox, out, mixed, *, heads, block):
    r = lax.axis_index("rep")
    embed = w.shape[1]
    width = embed // 2
    at = pl.ds(pl.multiple_of(r * width, width), width)
    away = hidden[...]
    for t in range(column.shape[1] // embed):
        x = standardize_features(column[:, t * embed : (t + 1) * embed]).astype(jnp.bfloat16)
        q, k, v, g = [project(x, w[n], wx[n]) for n in range(4)]
        attend_rows(q, k, v, g, lambda n: away, mixed, block, heads)
        half = wo.shape[0]
        delta = dot(mixed[:, :half], wo[:, at]) + dot(mixed[:, half:], wox[:, at])
        keep = column[:, pl.ds(pl.multiple_of(t * embed + r * width, width), width)]
        out[:, t * width : (t + 1) * width] = (keep.astype(jnp.float32) + delta).astype(jnp.bfloat16)


def local_call(kernel, out, scratch, flops, *operands):
    return pl.pallas_call(
        kernel,
        out_shape=jax.ShapeDtypeStruct(out, jnp.bfloat16),
        in_specs=[VMEM] * len(operands),
        out_specs=VMEM,
        scratch_shapes=[pltpu.VMEM(*s) for s in scratch],
        compiler_params=pltpu.CompilerParams(vmem_limit_bytes=40 << 20),
        cost_estimate=pl.CostEstimate(flops=flops, bytes_accessed=4 << 20, transcendentals=0),
    )(*operands)


def per_device(
    msa,
    pair,
    homolog_present,
    amino_present,
    row_w,
    row_out,
    offset_w,
    col_w,
    col_out,
    side_w,
    final_w,
    sigmoid_w,
):
    rep = lax.axis_index("rep")
    core = lax.axis_index(CORE)
    rows_here, sites, channels = pair.shape
    seqs_here, embed = msa.shape[0], msa.shape[2]
    chips = lax.axis_size(CHIPS)
    devices = lax.axis_size(DAP)
    heads_here = offset_w.shape[1]
    heads = 2 * heads_here
    row_start = lax.axis_index(DAP) * rows_here
    res_float = amino_present.astype(jnp.float32)
    mask_rows = lax.dynamic_slice_in_dim(res_float, row_start, rows_here, 0)
    flat = rows_here * sites

    pair_ln = standardize_features(pair).astype(jnp.bfloat16).reshape(flat, channels)
    bias = jnp.einsum("nc,ch->hn", pair_ln, offset_w, preferred_element_type=jnp.float32).astype(
        jnp.bfloat16
    )
    pair_mask = (mask_rows[:, None] * res_float[None, :]).reshape(1, flat)

    def gated_side(gate_weight, value_weight):
        gate = jnp.einsum("nd,dc->cn", pair_ln, gate_weight, preferred_element_type=jnp.float32)
        value = jnp.einsum("nd,dc->cn", pair_ln, value_weight, preferred_element_type=jnp.float32)
        return (jax.nn.sigmoid(gate) * value * pair_mask).astype(jnp.bfloat16)

    sides = jnp.stack([gated_side(side_w[0], side_w[1]), gated_side(side_w[2], side_w[3])], 1)

    weight_rows = row_w.shape[0] * row_w.shape[1]
    flat_w = (weight_rows, row_w.shape[2])
    bias_all, sides_all, row_wx, col_wx, row_ox, col_ox, final_x = exchange(
        first_exchange,
        [
            (2, 16, chips // 16, heads_here, flat),
            (devices, 2, flat),
            flat_w,
            flat_w,
            row_out.shape,
            col_out.shape,
            final_w.shape,
        ],
        [0, 0, 6, 6, 3, 3, 5, 5],
        bias,
        sides,
        row_w.reshape(flat_w),
        col_w.reshape(flat_w),
        row_out,
        col_out,
        final_w,
    )

    lefts = lax.dynamic_index_in_dim(sides_all[:, 0].reshape(chips, 2, flat), core, 1, keepdims=False)
    product = jnp.einsum(
        "ik,jk->ij",
        lefts.reshape(chips * rows_here, sites),
        sides_all[:, 1].reshape(devices * rows_here, sites),
        preferred_element_type=jnp.float32,
    )
    product = product.astype(jnp.bfloat16).reshape(chips, rows_here, sites)

    blocks = msa.reshape(seqs_here, chips, 2, rows_here, embed)
    msa_q = lax.dynamic_index_in_dim(blocks, rep, 2, keepdims=False)
    queries = chips * rows_here
    msa_q = msa_q.reshape(seqs_here, queries, embed)
    hidden = (NEG * (res_float - 1.0))[None, :]
    msa_one = local_call(
        functools.partial(row_kernel, heads=heads, block=24),
        (seqs_here, queries, embed),
        [((queries, heads, sites), jnp.float32), ((queries, embed), jnp.bfloat16)],
        3 << 30,
        msa,
        msa_q,
        bias_all,
        hidden,
        row_w,
        row_wx.reshape(row_w.shape),
        row_out,
        row_ox,
    )

    seq_blocks = msa_one.reshape(seqs_here, chips, rows_here * embed).swapaxes(0, 1)
    column, product = exchange(
        second_exchange,
        [(devices, seqs_here, rows_here * embed), (devices, rows_here, sites)],
        [0, 0, 0, 0],
        seq_blocks,
        product,
    )

    column = column.reshape(devices * seqs_here, rows_here * embed)
    away = (NEG * (homolog_present.astype(jnp.float32) - 1.0))[None, :]
    width = embed // 2
    alignment_output = local_call(
        functools.partial(col_kernel, heads=heads, block=32),
        (devices * seqs_here, rows_here * width),
        [((devices * seqs_here, embed), jnp.bfloat16)],
        3 << 30,
        column,
        away,
        col_w,
        col_wx.reshape(col_w.shape),
        col_out,
        col_ox,
    ).reshape(devices * seqs_here, rows_here, width)

    product = product.astype(jnp.float32)
    mean = jnp.mean(product, axis=0)
    square = jnp.mean(product * product, axis=0)
    scaled = ((product - mean) * lax.rsqrt(square - mean * mean + EPS)).astype(jnp.bfloat16)
    half = channels // 2
    first = jnp.where(rep == 0, final_w, final_x)
    second = jnp.where(rep == 0, final_x, final_w)
    final_all = jnp.concatenate([first, second], 0)
    final_half = lax.dynamic_slice_in_dim(final_all, rep * half, half, 1)
    tri_update = jnp.einsum("cij,cz->ijz", scaled, final_half, preferred_element_type=jnp.float32)
    pair_half = lax.dynamic_slice_in_dim(pair, rep * half, half, 2)
    gate_out = jax.nn.sigmoid(dot(pair_ln, sigmoid_w)).reshape(rows_here, sites, half)
    pair_output = (pair_half.astype(jnp.float32) + gate_out * tri_update).astype(jnp.bfloat16)
    return (alignment_output, pair_output)


def solution(mesh):
    finer = Mesh(
        mesh.devices.reshape(4, 4, 4, 2, mesh.shape["rep"]),
        (*DAP, "rep"),
    )
    return jax.shard_map(
        per_device,
        mesh=finer,
        in_specs=(
            P(DAP, None, None),
            P(DAP, None, None),
            P(),
            P(),
            P(None, None, "rep"),
            P("rep", None),
            P(None, "rep"),
            P(None, None, "rep"),
            P("rep", None),
            P(None, None, "rep"),
            P("rep", None),
            P(None, "rep"),
        ),
        out_specs=(P(None, DAP, "rep"), P(DAP, None, "rep")),
        check_vma=False,
    )
```

time: 181 us -> 107 us (0.59)
  Pallas kernels: 0 us -> 92.2 us
  starting transfers between devices: 45.8 us -> 0 us
  local copies, waits for them, and re-layouts: 41.5 us -> 7.84 us
  waiting for transfers between devices: 28 us -> 0 us
  matrix products: 29.7 us -> 2.7 us
  blocking collectives: 17.6 us -> 0 us
  other arithmetic: 15.8 us -> 2.31 us
    pallas_call x0 -> x4, Pallas kernels: none -> 92.2 us  [the longest x2 77.7 us: exchange(): pl.pallas_call(kernel, out_shape=[jax.ShapeDtypeStruct(s, jnp.bfloat16) f...]
    all_to_all x4 -> x0, starting transfers between devices: 36.7 us -> none  [the longest x1 12.3 us: per_device(): blocks = lax.all_to_all(blocks, CHIPS + ('rep',), 0, 0, tiled=True)]
    all_to_all x4 -> x0, waiting for transfers between devices: 28 us -> none  [the longest x1 11.7 us: per_device(): blocks = lax.all_to_all(blocks, CHIPS + ('rep',), 0, 0, tiled=True)]
    dot_general x24 -> x7, matrix products: 26.3 us -> 1.72 us  [the longest x2 0.54 us: gated_side(): jnp.einsum('nd,dc->cn', pair_ln, gate_weight, preferred_element_type=jnp....]
    all_to_all x3 -> x0, blocking collectives: 17.6 us -> none  [the longest x1 6.47 us: sent_to_all(): return lax.all_to_all(copies, axis, split_axis=0, concat_axis=0, tiled=True)]
    ppermute x3 -> x0, starting transfers between devices: 9.16 us -> none  [from_other_rep(): got = lax.ppermute(packed, ('dap_0', 'rep'), pairs)]
    slice x14 -> x1, local copies, waits for them, and re-layouts: 9.11 us -> 2.59 us  [per_device(): sides_all[:, 1].reshape(devices * rows_here, sites)]
    dynamic_slice x32 -> x2, local copies, waits for them, and re-layouts: 6.72 us -> 1.02 us  [the longest x1 0.87 us: per_device(): lax.dynamic_index_in_dim(sides_all[:, 0].reshape(chips, 2, flat), core, 1...]
  transfers between devices with their start and end apart: 7 -> 0, of which waited for: 3 -> 0; matrix products, arithmetic and copies ran while one was open for 34% -> 0% of each run, Pallas kernels for 0% -> 0%
where the time goes in v2:
time: 107 us; the launch traced here: 106 us
  Pallas kernels  92.2 us (86%)
  local copies, waits for them, and re-layouts  7.84 us (7%)
  matrix products  2.7 us (3%)
  other arithmetic  2.31 us (2%)
    pallas_call x2, Pallas kernels, exchange(): pl.pallas_call(kernel, out_shape=[jax.ShapeDtypeStruct(s, jnp.bfloat16) f...  77.7 us
    pallas_call x2, Pallas kernels, local_call(): pl.pallas_call(kernel, out_shape=jax.ShapeDtypeStruct(out, jnp.bfloat16),...  14.5 us
    slice x1, local copies, waits for them, and re-layouts, per_device(): sides_all[:, 1].reshape(devices * rows_here, sites)  2.59 us
    unnamed x27, local copies, waits for them, and re-layouts  2.51 us

profile of v2, /device:TPU:1, one launch (start us, length us, event | category | flops | bytes accessed | tf_op | source)
XLA Modules:
  0.0 106.1 jit_solution(13127752056770910408)
XLA Ops:
  0.6 0.0 copy-start
  0.6 0.0 copy-start.7
  0.7 1.4 %copy.31 = bf16[2,384,256]{2,0,1:T(2,128)(2,1)S(1)} copy(bf16[2,384,256]{2,1,0:T(8,128)(2,1)} %msa.1) | data formatting | bytes 786432 | tf_op args[0]
  2.1 0.0 copy-start.10
  2.1 0.0 copy-start.8
  2.1 0.1 constant_dynamic-slice_fusion.1
  2.3 0.0 copy-done.7
  2.3 0.2 convert_reduce_fusion.1
  2.5 0.4 fusion.23
  2.9 0.0 copy-start.9
  3.0 0.4 fusion.24
  3.3 0.0 copy-done.10
  3.3 0.2 fusion.15.bias
  3.5 0.0 copy-done.8
  3.5 0.3 fusion.7
  3.8 0.0 copy-done.9
  3.9 0.1 dynamic_slice.18
  3.9 0.1 broadcast_multiply_fusion
  4.0 0.2 fusion.13
  4.3 0.2 copy.33
  4.5 0.3 fusion.10
  4.8 0.0 copy-start.2
  4.8 0.0 copy-start.3
  4.8 0.0 copy-start.4
  4.8 0.0 copy-start.5
  4.8 0.0 copy-start.6
  4.8 0.2 fusion.14
  5.1 0.0 copy-start.1
  5.1 0.2 copy.32
  5.3 0.7 pad_maximum_fusion.sides
  6.0 0.0 copy-done.2
  6.0 0.0 copy-done.3
  6.0 0.0 copy-done.4
  6.0 0.0 copy-done.5
  6.0 0.0 copy-done.6
  6.0 48.7 %shard_map.131 = (bf16[2,16,4,4,1152]{4,3,2,1,0:T(4,128)(2,1)S(1)}, bf16[128,2,1152]{2,1,0:T(2,128)(2,1)S(1)}, bf16[1024,128]{1,0:T(8,128)(2,1)S(1)}, bf16[1024,...) custom-call(bf16[4,1152]{1,0:T(4,128)(2,1)S(1)} %fusion.15.bias, ...), custom_call_target="tpu_custom_call" | custom-call | tf_op jit(solution)/shard_map/pallas_call | solution.py:234
  54.8 0.0 copy-done.1
  54.8 8.5 %shard_map.132 = bf16[2,192,256]{2,1,0:T(8,128)(2,1)S(1)} custom-call(bf16[2,384,256]{2,1,0:T(8,128)(2,1)S(1)} %copy-done.1, bf16[2,192,256]{2,1,0:T(8,128)(2,1)S(1)} %copy.34.msa_q, bf16[2,16,4,4,1152]{4,3,2,1,0:T(4,128)(2,1)S(1)} %get-tuple-element.11.bias_all, f32[1,384]{1,0:T(1,128)S(1)} %broadcast_in_dim.4.hidden, bf16[4,256,128]{2,1,0:T(8,128)(2,1)S(1)} %copy-done.2, ...), custom_call_target="tpu_custom_call" | custom-call | flops 3221225472 | bytes 4194304 | tf_op jit(solution)/shard_map/pallas_call | solution.py:340
  63.3 0.1 reshape.92
  63.4 0.2 copy.51
  63.6 2.6 %slice_reduce_fusion = (bf16[128,1152]{1,0:T(8,128)(2,1)S(1)}, bf16[128,1152]{1,0:T(8,128)(2,1)S(1)}) fusion(bf16[128,2,1152]{2,1,0:T(2,128)(2,1)S(1)} %get-tuple-element.14), kind=kLoop, calls=%fused_computation.38 | loop fusion | bytes 1179648 | tf_op jit(solution)/shard_map/slice | solution.py:418
  66.2 0.1 reshape_squeeze.6
  66.4 0.9 dynamic-slice_reduce_fusion
  67.2 0.1 reshape.93
  67.3 0.1 reshape_squeeze.7
  67.5 0.0 copy-start.11
  67.5 0.3 convolution_convert_fusion.1
  67.8 0.1 reshape.94.rows
  67.8 29.0 %shard_map.133 = (bf16[128,2,768]{2,1,0:T(2,128)(2,1)S(1)}, bf16[128,3,384]{2,1,0:T(4,128)(2,1)S(1)}) custom-call(bf16[64,2,768]{2,1,0:T(2,128)(2,1)S(1)} %bitcast.50, bf16[64,3,384]{2,1,0:T(4,128)(2,1)S(1)} %reshape.94.rows), custom_call_target="tpu_custom_call" | custom-call | tf_op jit(solution)/shard_map/pallas_call | solution.py:234
  96.8 0.1 reshape.95.column
  97.0 0.0 copy-done.11
  97.0 6.0 %shard_map.134 = bf16[256,384]{1,0:T(8,128)(2,1)S(1)} custom-call(bf16[256,768]{1,0:T(8,128)(2,1)S(1)} %reshape.95.column, f32[1,256]{1,0:T(1,128)S(1)} %bitcast.53, bf16[4,256,128]{2,1,0:T(8,128)(2,1)S(1)} %copy-done.3, bf16[4,256,128]{2,1,0:T(8,128)(2,1)S(1)} %bitcast.54, bf16[128,256]{1,0:T(8,128)(2,1)S(1)} %copy-done.6, ...), custom_call_target="tpu_custom_call" | custom-call | flops 3221225472 | bytes 4194304 | tf_op jit(solution)/shard_map/pallas_call | solution.py:340
  103.0 0.1 copy.36
  103.1 0.8 copy.41
  104.0 0.0 copy-done
  104.0 0.3 fusion.4
  104.2 0.3 convert_reduce_fusion
  104.6 0.2 fusion.19
  104.8 0.1 constant_dynamic-slice_fusion
  104.9 0.2 copy.45
  105.1 1.0 fusion.17
  (10 shorter events, 0.1 us)
Async XLA Ops:
  0.6 103.3 %copy-start = (bf16[128,64]{0,1:T(8,128)(2,1)S(1)}, bf16[128,64]{0,1:T(8,128)(2,1)}, u32[]{:S(2)}) copy-start(bf16[128,64]{0,1:T(8,128)(2,1)} %param.23) | copy-start | bytes 49156
  0.6 1.7 %copy-start.7 = (bf16[3,384,128]{2,1,0:T(8,128)(2,1)S(1)}, bf16[3,384,128]{2,1,0:T(8,128)(2,1)}, u32[]{:S(2)}) copy-start(bf16[3,384,128]{2,1,0:T(8,128)(2,1)} %param.13) | copy-start | bytes 884740
  2.1 1.2 %copy-start.10 = (bf16[128,4]{0,1:T(4,128)(2,1)S(1)}, bf16[128,4]{0,1:T(4,128)(2,1)}, u32[]{:S(2)}) copy-start(bf16[128,4]{0,1:T(4,128)(2,1)} %param.18) | copy-start | bytes 3076
  2.1 1.4 %copy-start.8 = (bf16[4,128,64]{1,2,0:T(8,128)(2,1)S(1)}, bf16[4,128,64]{1,2,0:T(8,128)(2,1)}, u32[]{:S(2)}) copy-start(bf16[4,128,64]{1,2,0:T(8,128)(2,1)} %param.21) | copy-start | bytes 196612
  2.9 0.9 copy-start.9
  4.8 1.2 %copy-start.2 = (bf16[4,256,128]{2,1,0:T(8,128)(2,1)S(1)}, bf16[4,256,128]{2,1,0:T(8,128)(2,1)}, u32[]{:S(2)}) copy-start(bf16[4,256,128]{2,1,0:T(8,128)(2,1)} %w.2) | copy-start | bytes 786436
  4.8 1.2 %copy-start.3 = (bf16[4,256,128]{2,1,0:T(8,128)(2,1)S(1)}, bf16[4,256,128]{2,1,0:T(8,128)(2,1)}, u32[]{:S(2)}) copy-start(bf16[4,256,128]{2,1,0:T(8,128)(2,1)} %w.3) | copy-start | bytes 786436
  4.8 1.2 %copy-start.4 = (bf16[64,128]{1,0:T(8,128)(2,1)S(1)}, bf16[64,128]{1,0:T(8,128)(2,1)}, u32[]{:S(2)}) copy-start(bf16[64,128]{1,0:T(8,128)(2,1)} %final.1) | copy-start | bytes 49156
  4.8 1.2 %copy-start.5 = (bf16[128,256]{1,0:T(8,128)(2,1)S(1)}, bf16[128,256]{1,0:T(8,128)(2,1)}, u32[]{:S(2)}) copy-start(bf16[128,256]{1,0:T(8,128)(2,1)} %wo.2) | copy-start | bytes 196612
  4.8 1.2 %copy-start.6 = (bf16[128,256]{1,0:T(8,128)(2,1)S(1)}, bf16[128,256]{1,0:T(8,128)(2,1)}, u32[]{:S(2)}) copy-start(bf16[128,256]{1,0:T(8,128)(2,1)} %wo.3) | copy-start | bytes 196612
  5.1 49.7 %copy-start.1 = (bf16[2,384,256]{2,1,0:T(8,128)(2,1)S(1)}, bf16[2,384,256]{2,1,0:T(8,128)(2,1)}, u32[]{:S(2)}) copy-start(bf16[2,384,256]{2,1,0:T(8,128)(2,1)} %msa.1) | copy-start | bytes 1179652
  67.5 29.5 %copy-start.11 = (s32[256]{0:T(256)S(1)}, s32[256]{0:T(256)}, u32[]{:S(2)}) copy-start(s32[256]{0:T(256)} %param.14) | copy-start | bytes 3076

commit v3 on v2

--- a/solution.py
+++ b/solution.py
@@ -39,6 +39,15 @@
 
 def wait_bytes(ref, sem):
     pltpu.make_async_copy(ref, ref, sem).wait()
+
+
+def greet(device):
+    pl.semaphore_signal(pltpu.get_barrier_semaphore(), inc=1, device_id=device, device_id_type=MESH)
+
+
+def chip_at(to):
+    plane, high = 16, 4
+    return to // plane, lax.rem(to // high, high), lax.rem(to, high)
 
 
 def first_exchange(
@@ -60,21 +69,53 @@
     s_came,
     line_sent,
     line_came,
-    plane_sent,
-    plane_came,
+    bias_sent,
+    bias_came,
+    row_sent,
+    row_came,
+    col_sent,
+    col_came,
     core_sent,
     core_came,
 ):
     z, x, y, c, r = place()
-    deep, wide, high = 4, 4, 4
-    plane = wide * high
+    deep, high = 4, 4
+    plane = high * high
+    chips = deep * plane
     xy = x * high + y
     chip = z * plane + xy
     chunk = row_w.shape[0] // (2 * plane)
-    mine = pl.ds(pl.multiple_of((c * plane + xy) * chunk, chunk), chunk)
-    half = pl.ds(pl.multiple_of(c * plane * chunk, plane * chunk), plane * chunk)
     mirror = (deep - 1 - z, x, y, c, 1 - r)
     partner = (z, x, y, 1 - c, r)
+
+    def rows_of(at):
+        return pl.ds(pl.multiple_of((c * plane + at) * chunk, chunk), chunk)
+
+    mine = rows_of(xy)
+
+    def greet_group(i, carry):
+        greet((*chip_at(lax.rem(chip + i, chips)), c, r))
+        return carry
+
+    lax.fori_loop(1, chips, greet_group, 0)
+    greet(mirror)
+    greet(partner)
+    for zt in range(deep):
+
+        @pl.when(c != r)
+        def _():
+            greet((zt, x, y, r, c))
+
+    sides_all[c, chip] = sides[chip]
+
+    @pl.when(c == r)
+    def _():
+        bias_all[r, xy, z] = bias[...]
+        pl.semaphore_wait(pltpu.get_barrier_semaphore(), chips + 1)
+
+    @pl.when(c != r)
+    def _():
+        pl.semaphore_wait(pltpu.get_barrier_semaphore(), chips + 1 + deep)
 
     for dz in range(deep):
         zt = lax.rem(z + dz, deep)
@@ -83,10 +124,6 @@
             @pl.when(c != r)
             def _():
                 send(bias, bias_all.at[r, xy, z], line_sent.at[0], line_came.at[0], (zt, x, y, r, c))
-
-            @pl.when(c == r)
-            def _():
-                bias_all[r, xy, z] = bias[...]
 
         else:
             send(bias, bias_all.at[r, xy, z], line_sent.at[0], line_came.at[0], (zt, x, y, r, c))
@@ -97,19 +134,12 @@
     send(col_o.at[o_half], col_ox.at[o_half], line_sent.at[4], line_came.at[4], mirror)
     send(final, final_x, line_sent.at[5], line_came.at[5], mirror)
 
-    me = chip * 2 + c
-    chips = deep * plane
-    sides_all[me] = sides[chip]
-    send(sides.at[chip], sides_all.at[me], s_sent, s_came, partner)
-
     def to_owner(i, carry):
         to = lax.rem(chip + i, chips)
-        zt, xt, yt = to // plane, lax.rem(to // high, wide), lax.rem(to, high)
-        send(sides.at[to], sides_all.at[me], s_sent, s_came, (zt, xt, yt, 0, r))
-        send(sides.at[to], sides_all.at[me], s_sent, s_came, (zt, xt, yt, 1, r))
-        return carry
-
-    lax.fori_loop(1, chips // 2, to_owner, 0)
+        send(sides.at[to], sides_all.at[c, chip], s_sent, s_came.at[z], (*chip_at(to), c, r))
+        return carry
+
+    lax.fori_loop(1, plane, to_owner, 0)
 
     @pl.when(c == r)
     def _():
@@ -119,39 +149,76 @@
     def _():
         wait_bytes(bias_all.at[0, 0], line_came.at[0])
 
+    def plane_device(i):
+        to = lax.rem(xy + i, plane)
+        return (z, to // high, lax.rem(to, high), c, r)
+
+    def bias_plane(i, carry):
+        send(bias_all.at[c, xy], bias_all.at[c, xy], bias_sent, bias_came.at[xy], plane_device(i))
+        return carry
+
+    lax.fori_loop(1, plane, bias_plane, 0)
     wait_bytes(row_wx.at[mine], line_came.at[1])
     wait_bytes(col_wx.at[mine], line_came.at[2])
 
-    def over_plane(i, carry):
-        to = lax.rem(xy + i, plane)
-        device = (z, to // high, lax.rem(to, high), c, r)
-        send(bias_all.at[c, xy], bias_all.at[c, xy], plane_sent.at[0], plane_came.at[0], device)
-        send(row_wx.at[mine], row_wx.at[mine], plane_sent.at[1], plane_came.at[1], device)
-        send(col_wx.at[mine], col_wx.at[mine], plane_sent.at[2], plane_came.at[2], device)
-        return carry
-
-    lax.fori_loop(1, plane, over_plane, 0)
-    lax.fori_loop(chips // 2, chips, to_owner, 0)
-
-    rest = pl.ds(0, (plane - 1) * chunk)
+    def weight_plane(i, carry):
+        device = plane_device(i)
+        send(row_wx.at[mine], row_wx.at[mine], row_sent, row_came.at[xy], device)
+        send(col_wx.at[mine], col_wx.at[mine], col_sent, col_came.at[xy], device)
+        return carry
+
+    lax.fori_loop(1, plane, weight_plane, 0)
+    lax.fori_loop(plane, chips, to_owner, 0)
+
+    send(bias_all.at[c, xy], bias_all.at[c, xy], core_sent.at[0], core_came.at[0], partner)
+    send(row_wx.at[mine], row_wx.at[mine], core_sent.at[1], core_came.at[1], partner)
+    send(col_wx.at[mine], col_wx.at[mine], core_sent.at[2], core_came.at[2], partner)
     wait_bytes(row_ox.at[o_half], line_came.at[3])
     send(row_ox.at[o_half], row_ox.at[o_half], core_sent.at[3], core_came.at[3], partner)
     wait_bytes(col_ox.at[o_half], line_came.at[4])
     send(col_ox.at[o_half], col_ox.at[o_half], core_sent.at[4], core_came.at[4], partner)
-    wait_bytes(bias_all.at[0, pl.ds(0, plane - 1)], plane_came.at[0])
-    send(bias_all.at[c], bias_all.at[c], core_sent.at[0], core_came.at[0], partner)
-    wait_bytes(row_wx.at[rest], plane_came.at[1])
-    send(row_wx.at[half], row_wx.at[half], core_sent.at[1], core_came.at[1], partner)
-    wait_bytes(col_wx.at[rest], plane_came.at[2])
-    send(col_wx.at[half], col_wx.at[half], core_sent.at[2], core_came.at[2], partner)
-
+
+    def bias_core(i, carry):
+        at = lax.rem(xy + i, plane)
+        wait_bytes(bias_all.at[c, at], bias_came.at[at])
+        send(bias_all.at[c, at], bias_all.at[c, at], core_sent.at[0], core_came.at[0], partner)
+        return carry
+
+    lax.fori_loop(1, plane, bias_core, 0)
+
+    def weight_core(i, carry):
+        at = lax.rem(xy + i, plane)
+        rows = rows_of(at)
+        wait_bytes(row_wx.at[rows], row_came.at[at])
+        send(row_wx.at[rows], row_wx.at[rows], core_sent.at[1], core_came.at[1], partner)
+        wait_bytes(col_wx.at[rows], col_came.at[at])
+        send(col_wx.at[rows], col_wx.at[rows], core_sent.at[2], core_came.at[2], partner)
+        return carry
+
+    lax.fori_loop(1, plane, weight_core, 0)
+
+    def pass_sides(level):
+        for n in range(4):
+            part = pl.ds(pl.multiple_of(level * plane + n * high, high), high)
+            send(sides_all.at[c, part], sides_all.at[c, part], core_sent.at[5], core_came.at[5], partner)
+
+    wait_bytes(sides_all.at[0, pl.ds(0, plane - 1)], s_came.at[z])
+    pass_sides(z)
+    for dz in range(1, deep):
+        level = lax.rem(z + dz, deep)
+        wait_bytes(sides_all.at[0, pl.ds(0, plane)], s_came.at[level])
+        pass_sides(level)
+
+    half = pl.ds(0, plane * chunk)
+    rest = pl.ds(0, (plane - 1) * chunk)
     wait_bytes(final_x, line_came.at[5])
-    wait_bytes(bias_all.at[0], core_came.at[0])
-    wait_bytes(row_wx.at[half], core_came.at[1])
-    wait_bytes(col_wx.at[half], core_came.at[2])
-    wait_bytes(row_ox.at[o_half], core_came.at[3])
-    wait_bytes(col_ox.at[o_half], core_came.at[4])
-    wait_bytes(sides_all.at[pl.ds(0, 2 * chips - 1)], s_came)
+    for sems in (core_came, core_sent):
+        wait_bytes(bias_all.at[0], sems.at[0])
+        wait_bytes(row_wx.at[half], sems.at[1])
+        wait_bytes(col_wx.at[half], sems.at[2])
+        wait_bytes(row_ox.at[o_half], sems.at[3])
+        wait_bytes(col_ox.at[o_half], sems.at[4])
+        wait_bytes(sides_all.at[0], sems.at[5])
 
     @pl.when(c == r)
     def _():
@@ -166,57 +233,63 @@
     wait_bytes(row_ox.at[o_half], line_sent.at[3])
     wait_bytes(col_ox.at[o_half], line_sent.at[4])
     wait_bytes(final_x, line_sent.at[5])
-    wait_bytes(bias_all.at[0, pl.ds(0, plane - 1)], plane_sent.at[0])
-    wait_bytes(row_wx.at[rest], plane_sent.at[1])
-    wait_bytes(col_wx.at[rest], plane_sent.at[2])
-    wait_bytes(bias_all.at[0], core_sent.at[0])
-    wait_bytes(row_wx.at[half], core_sent.at[1])
-    wait_bytes(col_wx.at[half], core_sent.at[2])
-    wait_bytes(row_ox.at[o_half], core_sent.at[3])
-    wait_bytes(col_ox.at[o_half], core_sent.at[4])
-    wait_bytes(sides_all.at[pl.ds(0, 2 * chips - 1)], s_sent)
+    wait_bytes(bias_all.at[0, pl.ds(0, plane - 1)], bias_sent)
+    wait_bytes(row_wx.at[rest], row_sent)
+    wait_bytes(col_wx.at[rest], col_sent)
+    wait_bytes(sides_all.at[0, pl.ds(0, chips - 1)], s_sent)
 
 
 def second_exchange(seqs, rows, column, product, m_sent, m_came, p_sent, p_came):
     z, x, y, c, r = place()
-    wide, high = 4, 4
-    plane = wide * high
     chips = seqs.shape[0]
-    chip = z * plane + x * high + y
+    chip = z * 16 + x * 4 + y
     me = chip * 2 + c
     channel = r * chips + chip
+    here = (z, x, y)
+    barrier = pltpu.get_barrier_semaphore()
+
+    def greet_chip(i, carry):
+        there = chip_at(lax.rem(chip + i, chips))
+        for ct in range(2):
+            for rt in range(2):
+                greet((*there, ct, rt))
+        return carry
+
+    greet((*here, 1 - c, r))
+    greet((*here, c, 1 - r))
+    greet((*here, 1 - c, 1 - r))
+    lax.fori_loop(1, chips, greet_chip, 0)
+    product[channel] = rows[chip]
 
     @pl.when(c == r)
     def _():
         column[me] = seqs[chip]
 
+    pl.semaphore_wait(barrier, 4 * chips - 1)
+
     @pl.when(c != r)
     def _():
-        send(seqs.at[chip], column.at[me], m_sent, m_came, (z, x, y, r, r))
-
-    send(seqs.at[chip], column.at[me], m_sent, m_came, (z, x, y, r, 1 - r))
-    product[channel] = rows[chip]
-    send(rows.at[chip], product.at[channel], p_sent, p_came, (z, x, y, c, 1 - r))
+        send(seqs.at[chip], column.at[me], m_sent, m_came, (*here, r, r))
+
+    send(seqs.at[chip], column.at[me], m_sent, m_came, (*here, r, 1 - r))
 
     def to_owner(i, carry):
         to = lax.rem(chip + i, chips)
-        zt, xt, yt = to // plane, lax.rem(to // high, wide), lax.rem(to, high)
         for rt in range(2):
-            send(seqs.at[to], column.at[me], m_sent, m_came, (zt, xt, yt, r, rt))
+            send(seqs.at[to], column.at[me], m_sent, m_came, (*chip_at(to), r, rt))
         return carry
 
     def to_rows(i, carry):
         to = lax.rem(chip + i, chips)
-        zt, xt, yt = to // plane, lax.rem(to // high, wide), lax.rem(to, high)
         for rt in range(2):
-            send(rows.at[to], product.at[channel], p_sent, p_came, (zt, xt, yt, c, rt))
+            send(rows.at[to], product.at[channel], p_sent, p_came, (*chip_at(to), c, rt))
         return carry
 
     lax.fori_loop(1, chips, to_owner, 0)
+    send(rows.at[chip], product.at[channel], p_sent, p_came, (*here, c, 1 - r))
     lax.fori_loop(1, chips, to_rows, 0)
 
     for sem in (m_came, m_sent):
-
 
         @pl.when(c == r)
         def _():
@@ -230,7 +303,7 @@
         wait_bytes(product.at[pl.ds(0, 2 * chips - 1)], sem)
 
 
-def exchange(kernel, outs, semaphores, *operands):
+def exchange(kernel, number, outs, semaphores, *operands):
     return pl.pallas_call(
         kernel,
         out_shape=[jax.ShapeDtypeStruct(s, jnp.bfloat16) for s in outs],
@@ -239,7 +312,9 @@
         scratch_shapes=[
             pltpu.SemaphoreType.DMA if n == 0 else pltpu.SemaphoreType.DMA((n,)) for n in semaphores
         ],
-        compiler_params=pltpu.CompilerParams(has_side_effects=True, vmem_limit_bytes=40 << 20),
+        compiler_params=pltpu.CompilerParams(
+            collective_id=number, has_side_effects=True, vmem_limit_bytes=40 << 20
+        ),
     )(*operands)
 
 
@@ -392,16 +467,17 @@
     flat_w = (weight_rows, row_w.shape[2])
     bias_all, sides_all, row_wx, col_wx, row_ox, col_ox, final_x = exchange(
         first_exchange,
+        0,
         [
             (2, 16, chips // 16, heads_here, flat),
-            (devices, 2, flat),
+            (2, chips, 2, flat),
             flat_w,
             flat_w,
             row_out.shape,
             col_out.shape,
             final_w.shape,
         ],
-        [0, 0, 6, 6, 3, 3, 5, 5],
+        [0, 4, 6, 6, 0, 16, 0, 16, 0, 16, 6, 6],
         bias,
         sides,
         row_w.reshape(flat_w),
@@ -411,11 +487,12 @@
         final_w,
     )
 
-    lefts = lax.dynamic_index_in_dim(sides_all[:, 0].reshape(chips, 2, flat), core, 1, keepdims=False)
+    lefts = lax.dynamic_index_in_dim(sides_all, core, 0, keepdims=False)[:, 0]
+    rights = sides_all[:, :, 1].swapaxes(0, 1)
     product = jnp.einsum(
         "ik,jk->ij",
         lefts.reshape(chips * rows_here, sites),
-        sides_all[:, 1].reshape(devices * rows_here, sites),
+        rights.reshape(devices * rows_here, sites),
         preferred_element_type=jnp.float32,
     )
     product = product.astype(jnp.bfloat16).reshape(chips, rows_here, sites)
@@ -443,6 +520,7 @@
     seq_blocks = msa_one.reshape(seqs_here, chips, rows_here * embed).swapaxes(0, 1)
     column, product = exchange(
         second_exchange,
+        1,
         [(devices, seqs_here, rows_here * embed), (devices, rows_here, sites)],
         [0, 0, 0, 0],
         seq_blocks,

time: 107 us -> 89.6 us (0.84)
  Pallas kernels: 92.2 us -> 77.9 us
  local copies, waits for them, and re-layouts: 7.84 us -> 5.55 us
    pallas_call x2, Pallas kernels: 77.7 us -> 63.4 us  [exchange(): pl.pallas_call(kernel, out_shape=[jax.ShapeDtypeStruct(s, jnp.bfloat16) f...]
    slice x1 -> x2, local copies, waits for them, and re-layouts: 2.59 us -> 0.65 us  [the longest x1 0.63 us: per_device(): rights = sides_all[:, :, 1].swapaxes(0, 1)]
    unnamed x27 -> x28, local copies, waits for them, and re-layouts: 2.51 us -> 2.55 us
where the time goes in v3:
time: 89.6 us; the launch traced here: 89.5 us
  Pallas kernels  77.9 us (87%)
  local copies, waits for them, and re-layouts  5.55 us (6%)
  matrix products  2.69 us (3%)
  other arithmetic  2.31 us (3%)
  between operations  1.09 us (1%)
    pallas_call x2, Pallas kernels, exchange(): pl.pallas_call(kernel, out_shape=[jax.ShapeDtypeStruct(s, jnp.bfloat16) f...  63.4 us
    pallas_call x2, Pallas kernels, local_call(): pl.pallas_call(kernel, out_shape=jax.ShapeDtypeStruct(out, jnp.bfloat16),...  14.5 us
    unnamed x28, local copies, waits for them, and re-layouts  2.55 us

profile of v3, /device:TPU:1, one launch (start us, length us, event | category | flops | bytes accessed | tf_op | source)
XLA Modules:
  0.0 89.5 jit_solution(9771444530970384808)
XLA Ops:
  0.6 0.0 copy-start
  0.6 0.0 copy-start.7
  0.7 1.4 %copy.32 = bf16[2,384,256]{2,0,1:T(2,128)(2,1)S(1)} copy(bf16[2,384,256]{2,1,0:T(8,128)(2,1)} %msa.1) | data formatting | bytes 786432 | tf_op args[0]
  2.1 0.0 copy-start.10
  2.1 0.0 copy-start.8
  2.1 0.1 constant_dynamic-slice_fusion.2
  2.3 0.0 copy-done.7
  2.3 0.2 convert_reduce_fusion.1
  2.5 0.4 fusion.23
  2.9 0.0 copy-start.9
  3.0 0.4 fusion.24
  3.3 0.0 copy-done.10
  3.3 0.2 fusion.15.bias
  3.5 0.0 copy-done.8
  3.5 0.3 fusion.7
  3.8 0.0 copy-done.9
  3.9 0.1 dynamic_slice.18
  3.9 0.1 broadcast_multiply_fusion
  4.0 0.2 fusion.13
  4.3 0.2 copy.34
  4.5 0.3 fusion.10
  4.8 0.0 copy-start.2
  4.8 0.0 copy-start.3
  4.8 0.0 copy-start.4
  4.8 0.0 copy-start.5
  4.8 0.0 copy-start.6
  4.8 0.2 fusion.14
  5.1 0.0 copy-start.1
  5.1 0.2 copy.33
  5.3 0.7 pad_maximum_fusion.sides
  6.0 0.0 copy-done.2
  6.0 0.0 copy-done.3
  6.0 0.0 copy-done.4
  6.0 0.0 copy-done.5
  6.0 0.0 copy-done.6
  6.0 34.3 %shard_map.131 = (bf16[2,16,4,4,1152]{4,3,2,1,0:T(4,128)(2,1)S(1)}, bf16[2,64,2,1152]{3,2,1,0:T(2,128)(2,1)S(1)}, bf16[1024,128]{1,0:T(8,128)(2,1)S(1)}, bf16[10...) custom-call(bf16[4,1152]{1,0:T(4,128)(2,1)S(1)} %fusion.15.bias, ...), custom_call_target="tpu_custom_call" | custom-call | tf_op jit(solution)/shard_map/pallas_call | solution.py:307
  40.4 0.0 copy-done.1
  40.4 8.5 %shard_map.132 = bf16[2,192,256]{2,1,0:T(8,128)(2,1)S(1)} custom-call(bf16[2,384,256]{2,1,0:T(8,128)(2,1)S(1)} %copy-done.1, bf16[2,192,256]{2,1,0:T(8,128)(2,1)S(1)} %copy.35.msa_q, bf16[2,16,4,4,1152]{4,3,2,1,0:T(4,128)(2,1)S(1)} %get-tuple-element.11.bias_all, f32[1,384]{1,0:T(1,128)S(1)} %broadcast_in_dim.4.hidden, bf16[4,256,128]{2,1,0:T(8,128)(2,1)S(1)} %copy-done.2, ...), custom_call_target="tpu_custom_call" | custom-call | flops 3221225472 | bytes 4194304 | tf_op jit(solution)/shard_map/pallas_call | solution.py:415
  49.0 0.1 reshape.91
  49.1 0.2 copy.58
  49.3 0.2 constant_dynamic-slice_fusion.1
  49.6 0.1 reshape_squeeze.3
  49.6 0.6 slice.23
  50.3 0.3 copy.38
  50.6 0.2 reshape.92
  50.8 0.0 copy-start.11
  50.8 0.3 convolution_convert_fusion.1
  51.1 0.1 reshape.93.rows
  51.2 29.0 %shard_map.133 = (bf16[128,2,768]{2,1,0:T(2,128)(2,1)S(1)}, bf16[128,3,384]{2,1,0:T(4,128)(2,1)S(1)}) custom-call(bf16[64,2,768]{2,1,0:T(2,128)(2,1)S(1)} %bitcast.60, bf16[64,3,384]{2,1,0:T(4,128)(2,1)S(1)} %reshape.93.rows), custom_call_target="tpu_custom_call" | custom-call | tf_op jit(solution)/shard_map/pallas_call | solution.py:307
  80.2 0.1 reshape.94.column
  80.4 0.0 copy-done.11
  80.4 6.0 %shard_map.134 = bf16[256,384]{1,0:T(8,128)(2,1)S(1)} custom-call(bf16[256,768]{1,0:T(8,128)(2,1)S(1)} %reshape.94.column, f32[1,256]{1,0:T(1,128)S(1)} %bitcast.63, bf16[4,256,128]{2,1,0:T(8,128)(2,1)S(1)} %copy-done.3, bf16[4,256,128]{2,1,0:T(8,128)(2,1)S(1)} %bitcast.64, bf16[128,256]{1,0:T(8,128)(2,1)S(1)} %copy-done.6, ...), custom_call_target="tpu_custom_call" | custom-call | flops 3221225472 | bytes 4194304 | tf_op jit(solution)/shard_map/pallas_call | solution.py:415
  86.4 0.1 copy.39
  86.5 0.8 copy.44
  87.3 0.0 copy-done
  87.4 0.3 fusion.4
  87.6 0.3 convert_reduce_fusion
  88.0 0.2 fusion.19
  88.2 0.1 constant_dynamic-slice_fusion
  88.3 0.2 copy.48
  88.5 1.0 %fusion.17 = bf16[3,384,64]{1,2,0:T(8,128)(2,1)} fusion(f32[8,3,8,384]{3,2,1,0:T(8,128)S(1)} %bitcast.77, bf16[128,3,384]{2,1,0:T(4,128)(2,1)S(1)} %fusion.19, bf16[3,384,64]{1,2,0:T(8,128)(2,1)S(1)} %copy.48, s32[]{:T(128)S(6)} %select_n.30, bf16[64,128]{1,0:T(8,128)(2,1)S(1)} %get-tuple-element.29, bf16[64,128]{1,0:T(8,128)(2,1)S(1)} %get-tuple-element.28), kind=kOutput, calls=%fused_computation.27 | convolution fusion | flops 19202048 | bytes 917508 | tf_op jit(solution)/shard_map/cij,cz->ijz/dot_general | solution.py:555
  (13 shorter events, 0.2 us)
Async XLA Ops:
  0.6 86.7 %copy-start = (bf16[128,64]{0,1:T(8,128)(2,1)S(1)}, bf16[128,64]{0,1:T(8,128)(2,1)}, u32[]{:S(2)}) copy-start(bf16[128,64]{0,1:T(8,128)(2,1)} %param.23) | copy-start | bytes 49156
  0.6 1.7 %copy-start.7 = (bf16[3,384,128]{2,1,0:T(8,128)(2,1)S(1)}, bf16[3,384,128]{2,1,0:T(8,128)(2,1)}, u32[]{:S(2)}) copy-start(bf16[3,384,128]{2,1,0:T(8,128)(2,1)} %param.13) | copy-start | bytes 884740
  2.1 1.2 %copy-start.10 = (bf16[128,4]{0,1:T(4,128)(2,1)S(1)}, bf16[128,4]{0,1:T(4,128)(2,1)}, u32[]{:S(2)}) copy-start(bf16[128,4]{0,1:T(4,128)(2,1)} %param.18) | copy-start | bytes 3076
  2.1 1.4 %copy-start.8 = (bf16[4,128,64]{1,2,0:T(8,128)(2,1)S(1)}, bf16[4,128,64]{1,2,0:T(8,128)(2,1)}, u32[]{:S(2)}) copy-start(bf16[4,128,64]{1,2,0:T(8,128)(2,1)} %param.21) | copy-start | bytes 196612
  2.9 0.9 copy-start.9
  4.8 1.2 %copy-start.2 = (bf16[4,256,128]{2,1,0:T(8,128)(2,1)S(1)}, bf16[4,256,128]{2,1,0:T(8,128)(2,1)}, u32[]{:S(2)}) copy-start(bf16[4,256,128]{2,1,0:T(8,128)(2,1)} %w.2) | copy-start | bytes 786436
  4.8 1.2 %copy-start.3 = (bf16[4,256,128]{2,1,0:T(8,128)(2,1)S(1)}, bf16[4,256,128]{2,1,0:T(8,128)(2,1)}, u32[]{:S(2)}) copy-start(bf16[4,256,128]{2,1,0:T(8,128)(2,1)} %w.3) | copy-start | bytes 786436
  4.8 1.2 %copy-start.4 = (bf16[64,128]{1,0:T(8,128)(2,1)S(1)}, bf16[64,128]{1,0:T(8,128)(2,1)}, u32[]{:S(2)}) copy-start(bf16[64,128]{1,0:T(8,128)(2,1)} %final.1) | copy-start | bytes 49156
  4.8 1.2 %copy-start.5 = (bf16[128,256]{1,0:T(8,128)(2,1)S(1)}, bf16[128,256]{1,0:T(8,128)(2,1)}, u32[]{:S(2)}) copy-start(bf16[128,256]{1,0:T(8,128)(2,1)} %wo.2) | copy-start | bytes 196612
  4.8 1.2 %copy-start.6 = (bf16[128,256]{1,0:T(8,128)(2,1)S(1)}, bf16[128,256]{1,0:T(8,128)(2,1)}, u32[]{:S(2)}) copy-start(bf16[128,256]{1,0:T(8,128)(2,1)} %wo.3) | copy-start | bytes 196612
  5.1 35.3 %copy-start.1 = (bf16[2,384,256]{2,1,0:T(8,128)(2,1)S(1)}, bf16[2,384,256]{2,1,0:T(8,128)(2,1)}, u32[]{:S(2)}) copy-start(bf16[2,384,256]{2,1,0:T(8,128)(2,1)} %msa.1) | copy-start | bytes 1179652
  50.8 29.6 %copy-start.11 = (s32[256]{0:T(256)S(1)}, s32[256]{0:T(256)}, u32[]{:S(2)}) copy-start(s32[256]{0:T(256)} %param.14) | copy-start | bytes 3076

commit v4 on v3

--- a/solution.py
+++ b/solution.py
@@ -239,55 +239,56 @@
     wait_bytes(sides_all.at[0, pl.ds(0, chips - 1)], s_sent)
 
 
-def second_exchange(seqs, rows, column, product, m_sent, m_came, p_sent, p_came):
+def second_exchange(seqs, column, m_sent, m_came):
     z, x, y, c, r = place()
     chips = seqs.shape[0]
     chip = z * 16 + x * 4 + y
     me = chip * 2 + c
-    channel = r * chips + chip
     here = (z, x, y)
-    barrier = pltpu.get_barrier_semaphore()
 
     def greet_chip(i, carry):
         there = chip_at(lax.rem(chip + i, chips))
-        for ct in range(2):
-            for rt in range(2):
-                greet((*there, ct, rt))
-        return carry
-
-    greet((*here, 1 - c, r))
-    greet((*here, c, 1 - r))
-    greet((*here, 1 - c, 1 - r))
+        greet((*there, r, 1 - r))
+
+        @pl.when(c == r)
+        def _():
+            greet((*there, r, r))
+            greet((*there, 1 - r, r))
+
+        @pl.when(c != r)
+        def _():
+            greet((*there, r, r))
+            greet((*there, 1 - r, 1 - r))
+
+        return carry
+
     lax.fori_loop(1, chips, greet_chip, 0)
-    product[channel] = rows[chip]
+    greet((*here, r, 1 - r))
 
     @pl.when(c == r)
     def _():
+        greet((*here, 1 - r, r))
         column[me] = seqs[chip]
-
-    pl.semaphore_wait(barrier, 4 * chips - 1)
+        pl.semaphore_wait(pltpu.get_barrier_semaphore(), 3 * chips - 1)
 
     @pl.when(c != r)
     def _():
+        greet((*here, r, r))
+        greet((*here, 1 - r, 1 - r))
+        pl.semaphore_wait(pltpu.get_barrier_semaphore(), 3 * chips)
+
+    @pl.when(c != r)
+    def _():
         send(seqs.at[chip], column.at[me], m_sent, m_came, (*here, r, r))
-
-    send(seqs.at[chip], column.at[me], m_sent, m_came, (*here, r, 1 - r))
 
     def to_owner(i, carry):
         to = lax.rem(chip + i, chips)
-        for rt in range(2):
-            send(seqs.at[to], column.at[me], m_sent, m_came, (*chip_at(to), r, rt))
-        return carry
-
-    def to_rows(i, carry):
-        to = lax.rem(chip + i, chips)
-        for rt in range(2):
-            send(rows.at[to], product.at[channel], p_sent, p_came, (*chip_at(to), c, rt))
+        send(seqs.at[to], column.at[me], m_sent, m_came, (*chip_at(to), r, 1 - r))
+        send(seqs.at[to], column.at[me], m_sent, m_came, (*chip_at(to), r, r))
         return carry
 
     lax.fori_loop(1, chips, to_owner, 0)
-    send(rows.at[chip], product.at[channel], p_sent, p_came, (*here, c, 1 - r))
-    lax.fori_loop(1, chips, to_rows, 0)
+    send(seqs.at[chip], column.at[me], m_sent, m_came, (*here, r, 1 - r))
 
     for sem in (m_came, m_sent):
 
@@ -298,9 +299,6 @@
         @pl.when(c != r)
         def _():
             wait_bytes(column, sem)
-
-    for sem in (p_came, p_sent):
-        wait_bytes(product.at[pl.ds(0, 2 * chips - 1)], sem)
 
 
 def exchange(kernel, number, outs, semaphores, *operands):
@@ -352,11 +350,42 @@
 
 
 def row_kernel(
-    msa, msa_q, bias_all, hidden, w, wx, wo, wox, out, bias_rows, mixed, *, heads, block
+    rows,
+    msa,
+    pick,
+    bias_all,
+    hidden,
+    w,
+    wx,
+    wo,
+    wox,
+    out,
+    product,
+    bias_rows,
+    mixed,
+    p_sent,
+    p_came,
+    *,
+    heads,
+    block,
 ):
-    r = lax.axis_index("rep")
-    planes, deep = bias_all.shape[1], bias_all.shape[2]
-    rows = bias_rows.shape[0] // (planes * deep)
+    z, x, y, c, r = place()
+    chips = rows.shape[0]
+    chip = z * 16 + x * 4 + y
+    channel = r * chips + chip
+
+    def greet_rows(i, carry):
+        there = chip_at(lax.rem(chip + i, chips))
+        greet((*there, c, 1 - r))
+        greet((*there, c, r))
+        return carry
+
+    lax.fori_loop(1, chips, greet_rows, 0)
+    greet((z, x, y, c, 1 - r))
+    product[channel] = rows[chip]
+
+    planes = bias_all.shape[1]
+    rows_each = bias_rows.shape[0] // chips
     sites = bias_rows.shape[2]
     away = hidden[...]
 
@@ -369,15 +398,26 @@
             ],
             0,
         )
-        for t in range(rows):
-            bias_rows[p * rows + t] = both[:, t * sites : (t + 1) * sites] + away
-        return carry
-
-    lax.fori_loop(0, planes * deep, place_bias, 0)
+        for t in range(rows_each):
+            bias_rows[p * rows_each + t] = both[:, t * sites : (t + 1) * sites] + away
+        return carry
+
+    lax.fori_loop(0, chips, place_bias, 0)
+
+    pl.semaphore_wait(pltpu.get_barrier_semaphore(), 2 * chips - 1)
+
+    def to_rows(i, carry):
+        to = lax.rem(chip + i, chips)
+        send(rows.at[to], product.at[channel], p_sent, p_came, (*chip_at(to), c, 1 - r))
+        send(rows.at[to], product.at[channel], p_sent, p_came, (*chip_at(to), c, r))
+        return carry
+
+    lax.fori_loop(1, chips, to_rows, 0)
+    send(rows.at[chip], product.at[channel], p_sent, p_came, (z, x, y, c, 1 - r))
 
     def one(s, carry):
         x = standardize_features(msa[s]).astype(jnp.bfloat16)
-        xq = standardize_features(msa_q[s]).astype(jnp.bfloat16)
+        xq = dot(pick[...], x).astype(jnp.bfloat16)
         q = project(xq, w[0], wx[0])
         k = project(x, w[1], wx[1])
         v = project(x, w[2], wx[2])
@@ -389,10 +429,12 @@
         attend_rows(q, k, v, g, bias, mixed, block, heads)
         half = wo.shape[0]
         delta = dot(mixed[:, :half], wo[...]) + dot(mixed[:, half:], wox[...])
-        out[s] = (msa_q[s].astype(jnp.float32) + delta).astype(jnp.bfloat16)
+        out[s] = (dot(pick[...], msa[s]) + delta).astype(jnp.bfloat16)
         return carry
 
     lax.fori_loop(0, msa.shape[0], one, 0)
+    for sem in (p_came, p_sent):
+        wait_bytes(product.at[pl.ds(0, 2 * chips - 1)], sem)
 
 
 def col_kernel(column, hidden, w, wx, wo, wox, out, mixed, *, heads, block):
@@ -497,18 +539,16 @@
     )
     product = product.astype(jnp.bfloat16).reshape(chips, rows_here, sites)
 
-    blocks = msa.reshape(seqs_here, chips, 2, rows_here, embed)
-    msa_q = lax.dynamic_index_in_dim(blocks, rep, 2, keepdims=False)
     queries = chips * rows_here
-    msa_q = msa_q.reshape(seqs_here, queries, embed)
+    query = lax.broadcasted_iota(jnp.int32, (queries, sites), 0)
+    site = lax.broadcasted_iota(jnp.int32, (queries, sites), 1)
+    picked = 2 * rows_here * (query // rows_here) + rows_here * rep + query % rows_here
+    pick = (site == picked).astype(jnp.bfloat16)
     hidden = (NEG * (res_float - 1.0))[None, :]
-    msa_one = local_call(
-        functools.partial(row_kernel, heads=heads, block=24),
-        (seqs_here, queries, embed),
-        [((queries, heads, sites), jnp.float32), ((queries, embed), jnp.bfloat16)],
-        3 << 30,
+    operands = (
+        product,
         msa,
-        msa_q,
+        pick,
         bias_all,
         hidden,
         row_w,
@@ -516,15 +556,32 @@
         row_out,
         row_ox,
     )
+    msa_one, product = pl.pallas_call(
+        functools.partial(row_kernel, heads=heads, block=24),
+        out_shape=[
+            jax.ShapeDtypeStruct((seqs_here, queries, embed), jnp.bfloat16),
+            jax.ShapeDtypeStruct((devices, rows_here, sites), jnp.bfloat16),
+        ],
+        in_specs=[VMEM] * len(operands),
+        out_specs=[VMEM] * 2,
+        scratch_shapes=[
+            pltpu.VMEM((queries, heads, sites), jnp.float32),
+            pltpu.VMEM((queries, embed), jnp.bfloat16),
+            pltpu.SemaphoreType.DMA,
+            pltpu.SemaphoreType.DMA,
+        ],
+        compiler_params=pltpu.CompilerParams(
+            collective_id=2, has_side_effects=True, vmem_limit_bytes=40 << 20
+        ),
+    )(*operands)
 
     seq_blocks = msa_one.reshape(seqs_here, chips, rows_here * embed).swapaxes(0, 1)
-    column, product = exchange(
+    (column,) = exchange(
         second_exchange,
         1,
-        [(devices, seqs_here, rows_here * embed), (devices, rows_here, sites)],
-        [0, 0, 0, 0],
+        [(devices, seqs_here, rows_here * embed)],
+        [0, 0],
         seq_blocks,
-        product,
     )
 
     column = column.reshape(devices * seqs_here, rows_here * embed)

time: 89.6 us -> 95.4 us (1.065)
  other arithmetic: 2.31 us -> 5.47 us
  Pallas kernels: 77.9 us -> 80.8 us
    pallas_call x0 -> x1, Pallas kernels: none -> 19.8 us  [per_device(): pl.pallas_call(functools.partial(row_kernel, heads=heads, block=24), out_...]
    pallas_call x2 -> x1, Pallas kernels: 14.5 us -> 5.97 us  [local_call(): pl.pallas_call(kernel, out_shape=jax.ShapeDtypeStruct(out, jnp.bfloat16),...]
    pallas_call x2, Pallas kernels: 63.4 us -> 55 us  [exchange(): pl.pallas_call(kernel, out_shape=[jax.ShapeDtypeStruct(s, jnp.bfloat16) f...]
    reduce_sum x1, other arithmetic: 0.18 us -> 1.18 us  [standardize_features(): center = jnp.mean(values, axis=-1, keepdims=True)]
    convert_element_type x1, other arithmetic: 0.37 us -> 1.33 us  [per_device(): standardize_features(pair).astype(jnp.bfloat16).reshape(flat, channels)]
    unnamed x28 -> x37, local copies, waits for them, and re-layouts: 2.55 us -> 1.59 us
    reduce_sum x1, other arithmetic: 0.42 us -> 1.37 us  [standardize_features(): spread = jnp.mean(jnp.square(values - center), axis=-1, keepdims=True)]
where the time goes in v4:
time: 95.4 us; the launch traced here: 95.2 us
  Pallas kernels  80.8 us (85%)
  other arithmetic  5.47 us (6%)
  local copies, waits for them, and re-layouts  5.08 us (5%)
  matrix products  2.7 us (3%)
  between operations  1.14 us (1%)
    pallas_call x2, Pallas kernels, exchange(): pl.pallas_call(kernel, out_shape=[jax.ShapeDtypeStruct(s, jnp.bfloat16) f...  55 us
    pallas_call x1, Pallas kernels, per_device(): pl.pallas_call(functools.partial(row_kernel, heads=heads, block=24), out_...  19.8 us
    pallas_call x1, Pallas kernels, local_call(): pl.pallas_call(kernel, out_shape=jax.ShapeDtypeStruct(out, jnp.bfloat16),...  5.97 us

profile of v4, /device:TPU:1, one launch (start us, length us, event | category | flops | bytes accessed | tf_op | source)
XLA Modules:
  0.0 95.2 jit_solution(46062863223348656)
XLA Ops:
  0.6 0.0 copy-start
  0.6 0.0 copy-start.15
  0.7 0.0 copy-start.13
  0.7 1.2 %convert_reduce_fusion.1 = f32[3,384]{1,0:T(4,128)S(1)} fusion(bf16[3,384,128]{2,1,0:T(8,128)(2,1)} %param.13), kind=kLoop, calls=%fused_computation.33 | loop fusion | flops 293760 | bytes 299520 | tf_op jit(solution)/shard_map/reduce_sum | solution.py:24
  1.8 1.4 %fusion.23 = f32[3,384]{1,0:T(4,128)S(1)} fusion(bf16[3,384,128]{2,1,0:T(8,128)(2,1)} %param.13, f32[3,384]{1,0:T(4,128)S(1)} %broadcast_multiply_fusion.2), kind=kLoop, calls=%fused_computation.36 | loop fusion | flops 588672 | bytes 304128 | tf_op jit(solution)/shard_map/reduce_sum | solution.py:25
  3.2 1.3 %fusion.24 = bf16[3,384,128]{2,1,0:T(8,128)(2,1)S(1)} fusion(bf16[3,384,128]{2,1,0:T(8,128)(2,1)} %param.13, f32[3,384]{1,0:T(4,128)S(1)} %add_rsqrt_fusion.1, f32[3,384]{1,0:T(4,128)S(1)} %broadcast_multiply_fusion.2), kind=kLoop, calls=%fused_computation.37 | loop fusion | flops 589824 | bytes 599040 | tf_op jit(solution)/shard_map/convert_element_type | solution.py:495
  4.6 0.0 copy-start.10
  4.6 0.0 copy-done.15
  4.6 0.2 fusion.15.bias
  4.8 0.0 copy-done.13
  4.8 0.3 fusion.7
  5.1 0.0 copy-done.14
  5.1 0.1 dynamic_slice.13
  5.2 0.1 broadcast_multiply_fusion
  5.3 0.2 fusion.13
  5.5 0.2 copy.30
  5.8 0.3 fusion.10
  6.0 0.0 copy-done.10
  6.0 0.0 copy-start.1
  6.0 0.0 copy-start.3
  6.1 0.0 copy-start.4
  6.1 0.0 copy-start.5
  6.1 0.0 copy-start.6
  6.1 0.2 fusion.14
  6.3 0.2 copy.29
  6.6 0.7 pad_maximum_fusion.sides
  7.2 0.0 copy-done.1
  7.3 0.0 copy-done.3
  7.3 0.0 copy-done.4
  7.3 0.0 copy-done.5
  7.3 0.0 copy-done.6
  7.3 34.1 %shard_map.131 = (bf16[2,16,4,4,1152]{4,3,2,1,0:T(4,128)(2,1)S(1)}, bf16[2,64,2,1152]{3,2,1,0:T(2,128)(2,1)S(1)}, bf16[1024,128]{1,0:T(8,128)(2,1)S(1)}, bf16[10...) custom-call(bf16[4,1152]{1,0:T(4,128)(2,1)S(1)} %fusion.15.bias, ...), custom_call_target="tpu_custom_call" | custom-call | tf_op jit(solution)/shard_map/pallas_call | solution.py:305
  41.4 0.0 copy-start.7
  41.4 0.2 constant_dynamic-slice_fusion.1
  41.7 0.7 reshape_squeeze.3
  42.4 0.6 slice.23
  43.1 0.0 copy-done.7
  43.1 0.0 copy-start.12
  43.1 0.0 copy-start.2
  43.1 0.3 copy.32
  43.5 0.2 reshape.81
  43.6 0.3 copy-done.12
  44.0 0.3 convolution_convert_fusion.1
  44.3 0.1 reshape.82.rows
  44.4 0.2 fusion.26.pick
  44.6 0.0 copy-done.2
  44.6 19.8 %shard_map.132 = (bf16[2,192,256]{2,1,0:T(8,128)(2,1)S(1)}, bf16[128,3,384]{2,1,0:T(4,128)(2,1)S(1)}) custom-call(bf16[64,3,384]{2,1,0:T(4,128)(2,1)S(1)} %reshape.82.rows, bf16[2,384,256]{2,1,0:T(8,128)(2,1)S(1)} %copy-done.2, bf16[192,384]{1,0:T(8,128)(2,1)S(1)} %fusion.26.pick, bf16[2,16,4,4,1152]{4,3,2,1,0:T(4,128)(2,1)S(1)} %get-tuple-element.12.bias_all, ...), custom_call_target="tpu_custom_call" | custom-call | tf_op jit(solution)/shard_map/pallas_call | solution.py:559
  64.5 0.0 copy-start.16
  64.5 0.1 reshape.84
  64.6 0.2 copy.53
  64.8 20.9 %shard_map.133 = bf16[128,2,768]{2,1,0:T(2,128)(2,1)S(1)} custom-call(bf16[64,2,768]{2,1,0:T(2,128)(2,1)S(1)} %bitcast.59), custom_call_target="tpu_custom_call" | custom-call | tf_op jit(solution)/shard_map/pallas_call | solution.py:305
  85.7 0.1 reshape.85.column
  85.9 0.0 copy-done.8
  85.9 0.0 copy-start.11
  85.9 6.0 %shard_map.134 = bf16[256,384]{1,0:T(8,128)(2,1)S(1)} custom-call(bf16[256,768]{1,0:T(8,128)(2,1)S(1)} %reshape.85.column, f32[1,256]{1,0:T(1,128)S(1)} %bitcast.62, bf16[4,256,128]{2,1,0:T(8,128)(2,1)S(1)} %copy-done.3, bf16[4,256,128]{2,1,0:T(8,128)(2,1)S(1)} %bitcast.63, bf16[128,256]{1,0:T(8,128)(2,1)S(1)} %copy-done.6, ...), custom_call_target="tpu_custom_call" | custom-call | flops 3221225472 | bytes 4194304 | tf_op jit(solution)/shard_map/pallas_call | solution.py:457
  91.9 0.1 copy.34
  92.1 0.8 copy.39
  92.9 0.3 fusion.4
  93.1 0.3 convert_reduce_fusion
  93.5 0.2 fusion.19
  93.7 0.1 copy-done.9
  93.8 0.1 constant_dynamic-slice_fusion
  94.0 0.2 copy.43
  94.2 1.0 %fusion.17 = bf16[3,384,64]{1,2,0:T(8,128)(2,1)} fusion(f32[8,3,8,384]{3,2,1,0:T(8,128)S(1)} %bitcast.73, bf16[128,3,384]{2,1,0:T(4,128)(2,1)S(1)} %fusion.19, bf16[3,384,64]{1,2,0:T(8,128)(2,1)S(1)} %copy.43, s32[]{:T(128)S(6)} %select_n.39, bf16[64,128]{1,0:T(8,128)(2,1)S(1)} %get-tuple-element.29, bf16[64,128]{1,0:T(8,128)(2,1)S(1)} %get-tuple-element.28), kind=kOutput, calls=%fused_computation.27 | convolution fusion | flops 19202048 | bytes 917508 | tf_op jit(solution)/shard_map/cij,cz->ijz/dot_general | solution.py:612
  (21 shorter events, 0.2 us)
Async XLA Ops:
  0.6 92.2 %copy-start = (bf16[128,64]{0,1:T(8,128)(2,1)S(1)}, bf16[128,64]{0,1:T(8,128)(2,1)}, u32[]{:S(2)}) copy-start(bf16[128,64]{0,1:T(8,128)(2,1)} %param.23) | copy-start | bytes 49156
  0.6 4.0 %copy-start.15 = (bf16[128,4]{0,1:T(4,128)(2,1)S(1)}, bf16[128,4]{0,1:T(4,128)(2,1)}, u32[]{:S(2)}) copy-start(bf16[128,4]{0,1:T(4,128)(2,1)} %param.18) | copy-start | bytes 3076
  0.7 4.1 %copy-start.13 = (bf16[4,128,64]{1,2,0:T(8,128)(2,1)S(1)}, bf16[4,128,64]{1,2,0:T(8,128)(2,1)}, u32[]{:S(2)}) copy-start(bf16[4,128,64]{1,2,0:T(8,128)(2,1)} %param.21) | copy-start | bytes 196612
  3.2 1.9 %copy-start.14 = (s32[384]{0:T(512)S(1)}, s32[384]{0:T(512)}, u32[]{:S(2)}) copy-start(s32[384]{0:T(512)} %param.15) | copy-start | bytes 4612
  4.6 1.4 %copy-start.10 = (bf16[3,384,128]{2,1,0:T(8,128)(2,1)}, bf16[3,384,128]{2,1,0:T(8,128)(2,1)S(1)}, u32[]{:S(2)}) copy-start(bf16[3,384,128]{2,1,0:T(8,128)(2,1)S(1)} %fusion.24) | copy-start | bytes 884740
  6.0 1.2 %copy-start.1 = (bf16[4,256,128]{2,1,0:T(8,128)(2,1)S(1)}, bf16[4,256,128]{2,1,0:T(8,128)(2,1)}, u32[]{:S(2)}) copy-start(bf16[4,256,128]{2,1,0:T(8,128)(2,1)} %w.2) | copy-start | bytes 786436
  6.0 1.2 %copy-start.3 = (bf16[4,256,128]{2,1,0:T(8,128)(2,1)S(1)}, bf16[4,256,128]{2,1,0:T(8,128)(2,1)}, u32[]{:S(2)}) copy-start(bf16[4,256,128]{2,1,0:T(8,128)(2,1)} %w.3) | copy-start | bytes 786436
  6.1 1.2 %copy-start.4 = (bf16[128,256]{1,0:T(8,128)(2,1)S(1)}, bf16[128,256]{1,0:T(8,128)(2,1)}, u32[]{:S(2)}) copy-start(bf16[128,256]{1,0:T(8,128)(2,1)} %wo.2) | copy-start | bytes 196612
  6.1 1.2 %copy-start.5 = (bf16[64,128]{1,0:T(8,128)(2,1)S(1)}, bf16[64,128]{1,0:T(8,128)(2,1)}, u32[]{:S(2)}) copy-start(bf16[64,128]{1,0:T(8,128)(2,1)} %final.1) | copy-start | bytes 49156
  6.1 1.2 %copy-start.6 = (bf16[128,256]{1,0:T(8,128)(2,1)S(1)}, bf16[128,256]{1,0:T(8,128)(2,1)}, u32[]{:S(2)}) copy-start(bf16[128,256]{1,0:T(8,128)(2,1)} %wo.3) | copy-start | bytes 196612
  41.4 1.7 %copy-start.7 = (bf16[1024,128]{1,0:T(8,128)(2,1)}, bf16[1024,128]{1,0:T(8,128)(2,1)S(1)}, u32[]{:S(2)}) copy-start(bf16[1024,128]{1,0:T(8,128)(2,1)S(1)} %get-tuple-element.16) | copy-start | bytes 786436
  43.1 0.9 copy-start.12
  43.1 1.5 %copy-start.2 = (bf16[2,384,256]{2,1,0:T(8,128)(2,1)S(1)}, bf16[2,384,256]{2,1,0:T(8,128)(2,1)}, u32[]{:S(2)}) copy-start(bf16[2,384,256]{2,1,0:T(8,128)(2,1)} %msa.1) | copy-start | bytes 1179652
  64.5 21.4 %copy-start.16 = (s32[256]{0:T(256)S(1)}, s32[256]{0:T(256)}, u32[]{:S(2)}) copy-start(s32[256]{0:T(256)} %param.14) | copy-start | bytes 3076
  64.5 21.4 %copy-start.8 = (bf16[1024,128]{1,0:T(8,128)(2,1)S(1)}, bf16[1024,128]{1,0:T(8,128)(2,1)}, u32[]{:S(2)}) copy-start(bf16[1024,128]{1,0:T(8,128)(2,1)} %copy-done.7) | copy-start | bytes 786436
  85.9 7.0 %copy-start.11 = (bf16[3,384,128]{2,1,0:T(8,128)(2,1)S(1)}, bf16[3,384,128]{2,1,0:T(8,128)(2,1)}, u32[]{:S(2)}) copy-start(bf16[3,384,128]{2,1,0:T(8,128)(2,1)} %copy-done.10) | copy-start | bytes 884740
  92.9 1.0 %copy-start.9 = (bf16[3,384,128]{2,1,0:T(8,128)(2,1)S(1)}, bf16[3,384,128]{2,1,0:T(8,128)(2,1)}, u32[]{:S(2)}) copy-start(bf16[3,384,128]{2,1,0:T(8,128)(2,1)} %param.13) | copy-start | bytes 884740

commit v5 on v4

--- a/solution.py
+++ b/solution.py
@@ -239,68 +239,6 @@
     wait_bytes(sides_all.at[0, pl.ds(0, chips - 1)], s_sent)
 
 
-def second_exchange(seqs, column, m_sent, m_came):
-    z, x, y, c, r = place()
-    chips = seqs.shape[0]
-    chip = z * 16 + x * 4 + y
-    me = chip * 2 + c
-    here = (z, x, y)
-
-    def greet_chip(i, carry):
-        there = chip_at(lax.rem(chip + i, chips))
-        greet((*there, r, 1 - r))
-
-        @pl.when(c == r)
-        def _():
-            greet((*there, r, r))
-            greet((*there, 1 - r, r))
-
-        @pl.when(c != r)
-        def _():
-            greet((*there, r, r))
-            greet((*there, 1 - r, 1 - r))
-
-        return carry
-
-    lax.fori_loop(1, chips, greet_chip, 0)
-    greet((*here, r, 1 - r))
-
-    @pl.when(c == r)
-    def _():
-        greet((*here, 1 - r, r))
-        column[me] = seqs[chip]
-        pl.semaphore_wait(pltpu.get_barrier_semaphore(), 3 * chips - 1)
-
-    @pl.when(c != r)
-    def _():
-        greet((*here, r, r))
-        greet((*here, 1 - r, 1 - r))
-        pl.semaphore_wait(pltpu.get_barrier_semaphore(), 3 * chips)
-
-    @pl.when(c != r)
-    def _():
-        send(seqs.at[chip], column.at[me], m_sent, m_came, (*here, r, r))
-
-    def to_owner(i, carry):
-        to = lax.rem(chip + i, chips)
-        send(seqs.at[to], column.at[me], m_sent, m_came, (*chip_at(to), r, 1 - r))
-        send(seqs.at[to], column.at[me], m_sent, m_came, (*chip_at(to), r, r))
-        return carry
-
-    lax.fori_loop(1, chips, to_owner, 0)
-    send(seqs.at[chip], column.at[me], m_sent, m_came, (*here, r, 1 - r))
-
-    for sem in (m_came, m_sent):
-
-        @pl.when(c == r)
-        def _():
-            wait_bytes(column.at[pl.ds(0, 2 * chips - 1)], sem)
-
-        @pl.when(c != r)
-        def _():
-            wait_bytes(column, sem)
-
-
 def exchange(kernel, number, outs, semaphores, *operands):
     return pl.pallas_call(
         kernel,
@@ -359,12 +297,16 @@
     wx,
     wo,
     wox,
-    out,
+    column,
     product,
     bias_rows,
     mixed,
+    done,
+    seqs,
     p_sent,
     p_came,
+    m_sent,
+    m_came,
     *,
     heads,
     block,
@@ -372,16 +314,22 @@
     z, x, y, c, r = place()
     chips = rows.shape[0]
     chip = z * 16 + x * 4 + y
+    me = chip * 2 + c
     channel = r * chips + chip
-
-    def greet_rows(i, carry):
+    here = (z, x, y)
+    embed = w.shape[1]
+
+    def greet_chip(i, carry):
         there = chip_at(lax.rem(chip + i, chips))
-        greet((*there, c, 1 - r))
-        greet((*there, c, r))
-        return carry
-
-    lax.fori_loop(1, chips, greet_rows, 0)
-    greet((z, x, y, c, 1 - r))
+        for ct in range(2):
+            for rt in range(2):
+                greet((*there, ct, rt))
+        return carry
+
+    lax.fori_loop(1, chips, greet_chip, 0)
+    greet((*here, 1 - c, r))
+    greet((*here, c, 1 - r))
+    greet((*here, 1 - c, 1 - r))
     product[channel] = rows[chip]
 
     planes = bias_all.shape[1]
@@ -399,12 +347,10 @@
             0,
         )
         for t in range(rows_each):
-            bias_rows[p * rows_each + t] = both[:, t * sites : (t + 1) * sites] + away
+            bias_rows[t * chips + p] = both[:, t * sites : (t + 1) * sites] + away
         return carry
 
     lax.fori_loop(0, chips, place_bias, 0)
-
-    pl.semaphore_wait(pltpu.get_barrier_semaphore(), 2 * chips - 1)
 
     def to_rows(i, carry):
         to = lax.rem(chip + i, chips)
@@ -412,10 +358,13 @@
         send(rows.at[to], product.at[channel], p_sent, p_came, (*chip_at(to), c, r))
         return carry
 
-    lax.fori_loop(1, chips, to_rows, 0)
-    send(rows.at[chip], product.at[channel], p_sent, p_came, (z, x, y, c, 1 - r))
-
     def one(s, carry):
+        @pl.when(s == 1)
+        def _():
+            pl.semaphore_wait(pltpu.get_barrier_semaphore(), 4 * chips - 1)
+            lax.fori_loop(1, chips, to_rows, 0)
+            send(rows.at[chip], product.at[channel], p_sent, p_came, (*here, c, 1 - r))
+
         x = standardize_features(msa[s]).astype(jnp.bfloat16)
         xq = dot(pick[...], x).astype(jnp.bfloat16)
         q = project(xq, w[0], wx[0])
@@ -429,10 +378,44 @@
         attend_rows(q, k, v, g, bias, mixed, block, heads)
         half = wo.shape[0]
         delta = dot(mixed[:, :half], wo[...]) + dot(mixed[:, half:], wox[...])
-        out[s] = (dot(pick[...], msa[s]) + delta).astype(jnp.bfloat16)
+        done[s] = dot(pick[...], msa[s]) + delta
         return carry
 
     lax.fori_loop(0, msa.shape[0], one, 0)
+
+    for t in range(rows_each):
+        part = slice(t * chips, (t + 1) * chips)
+        both = jnp.concatenate([done[0, part, :][:, None, :], done[1, part, :][:, None, :]], 1)
+        seqs[:, :, t * embed : (t + 1) * embed] = both.astype(jnp.bfloat16)
+
+    @pl.when(c == r)
+    def _():
+        column[me] = seqs[chip]
+
+    def to_owner(i, carry):
+        to = lax.rem(chip + i, chips)
+        send(seqs.at[to], column.at[me], m_sent, m_came, (*chip_at(to), r, 1 - r))
+        send(seqs.at[to], column.at[me], m_sent, m_came, (*chip_at(to), r, r))
+        return carry
+
+    lax.fori_loop(1, chips, to_owner, 0)
+
+    @pl.when(c != r)
+    def _():
+        send(seqs.at[chip], column.at[me], m_sent, m_came, (*here, r, r))
+
+    send(seqs.at[chip], column.at[me], m_sent, m_came, (*here, r, 1 - r))
+
+    for sem in (m_came, m_sent):
+
+        @pl.when(c == r)
+        def _():
+            wait_bytes(column.at[pl.ds(0, 2 * chips - 1)], sem)
+
+        @pl.when(c != r)
+        def _():
+            wait_bytes(column, sem)
+
     for sem in (p_came, p_sent):
         wait_bytes(product.at[pl.ds(0, 2 * chips - 1)], sem)
 
@@ -542,7 +525,7 @@
     queries = chips * rows_here
     query = lax.broadcasted_iota(jnp.int32, (queries, sites), 0)
     site = lax.broadcasted_iota(jnp.int32, (queries, sites), 1)
-    picked = 2 * rows_here * (query // rows_here) + rows_here * rep + query % rows_here
+    picked = 2 * rows_here * (query % chips) + rows_here * rep + query // chips
     pick = (site == picked).astype(jnp.bfloat16)
     hidden = (NEG * (res_float - 1.0))[None, :]
     operands = (
@@ -556,10 +539,10 @@
         row_out,
         row_ox,
     )
-    msa_one, product = pl.pallas_call(
+    column, product = pl.pallas_call(
         functools.partial(row_kernel, heads=heads, block=24),
         out_shape=[
-            jax.ShapeDtypeStruct((seqs_here, queries, embed), jnp.bfloat16),
+            jax.ShapeDtypeStruct((devices, seqs_here, rows_here * embed), jnp.bfloat16),
             jax.ShapeDtypeStruct((devices, rows_here, sites), jnp.bfloat16),
         ],
         in_specs=[VMEM] * len(operands),
@@ -567,22 +550,17 @@
         scratch_shapes=[
             pltpu.VMEM((queries, heads, sites), jnp.float32),
             pltpu.VMEM((queries, embed), jnp.bfloat16),
+            pltpu.VMEM((seqs_here, queries, embed), jnp.float32),
+            pltpu.VMEM((chips, seqs_here, rows_here * embed), jnp.bfloat16),
+            pltpu.SemaphoreType.DMA,
+            pltpu.SemaphoreType.DMA,
             pltpu.SemaphoreType.DMA,
             pltpu.SemaphoreType.DMA,
         ],
         compiler_params=pltpu.CompilerParams(
-            collective_id=2, has_side_effects=True, vmem_limit_bytes=40 << 20
+            collective_id=1, has_side_effects=True, vmem_limit_bytes=40 << 20
         ),
     )(*operands)
-
-    seq_blocks = msa_one.reshape(seqs_here, chips, rows_here * embed).swapaxes(0, 1)
-    (column,) = exchange(
-        second_exchange,
-        1,
-        [(devices, seqs_here, rows_here * embed)],
-        [0, 0],
-        seq_blocks,
-    )
 
     column = column.reshape(devices * seqs_here, rows_here * embed)
     away = (NEG * (homolog_present.astype(jnp.float32) - 1.0))[None, :]

time: 95.4 us -> 86.3 us (0.905)
  Pallas kernels: 80.8 us -> 69.8 us
  local copies, waits for them, and re-layouts: 5.08 us -> 7 us
    pallas_call x2 -> x1, Pallas kernels: 55 us -> 34.3 us  [exchange(): pl.pallas_call(kernel, out_shape=[jax.ShapeDtypeStruct(s, jnp.bfloat16) f...]
    pallas_call x1, Pallas kernels: 19.8 us -> 29.4 us  [per_device(): pl.pallas_call(functools.partial(row_kernel, heads=heads, block=24), out_...]
    unnamed x37 -> x43, local copies, waits for them, and re-layouts: 1.59 us -> 4.48 us
where the time goes in v5:
time: 86.3 us; the launch traced here: 86 us
  Pallas kernels  69.8 us (81%)
  local copies, waits for them, and re-layouts  7 us (8%)
  other arithmetic  5.46 us (6%)
  matrix products  2.69 us (3%)
  between operations  1.12 us (1%)
    pallas_call x1, Pallas kernels, exchange(): pl.pallas_call(kernel, out_shape=[jax.ShapeDtypeStruct(s, jnp.bfloat16) f...  34.3 us
    pallas_call x1, Pallas kernels, per_device(): pl.pallas_call(functools.partial(row_kernel, heads=heads, block=24), out_...  29.4 us
    pallas_call x1, Pallas kernels, local_call(): pl.pallas_call(kernel, out_shape=jax.ShapeDtypeStruct(out, jnp.bfloat16),...  5.97 us
    unnamed x43, local copies, waits for them, and re-layouts  4.48 us

profile of v5, /device:TPU:1, one launch (start us, length us, event | category | flops | bytes accessed | tf_op | source)
XLA Modules:
  0.0 86.0 jit_solution(2067140317049777589)
XLA Ops:
  0.6 0.0 copy-start
  0.6 0.0 copy-start.18
  0.7 0.0 copy-start.16
  0.7 1.2 %convert_reduce_fusion.1 = f32[3,384]{1,0:T(4,128)S(1)} fusion(bf16[3,384,128]{2,1,0:T(8,128)(2,1)} %param.13), kind=kLoop, calls=%fused_computation.33 | loop fusion | flops 293760 | bytes 299520 | tf_op jit(solution)/shard_map/reduce_sum | solution.py:24
  1.8 1.4 %fusion.23 = f32[3,384]{1,0:T(4,128)S(1)} fusion(bf16[3,384,128]{2,1,0:T(8,128)(2,1)} %param.13, f32[3,384]{1,0:T(4,128)S(1)} %broadcast_multiply_fusion.2), kind=kLoop, calls=%fused_computation.36 | loop fusion | flops 588672 | bytes 304128 | tf_op jit(solution)/shard_map/reduce_sum | solution.py:25
  3.2 1.3 %fusion.24 = bf16[3,384,128]{2,1,0:T(8,128)(2,1)S(1)} fusion(bf16[3,384,128]{2,1,0:T(8,128)(2,1)} %param.13, f32[3,384]{1,0:T(4,128)S(1)} %add_rsqrt_fusion.1, f32[3,384]{1,0:T(4,128)S(1)} %broadcast_multiply_fusion.2), kind=kLoop, calls=%fused_computation.37 | loop fusion | flops 589824 | bytes 599040 | tf_op jit(solution)/shard_map/convert_element_type | solution.py:478
  4.6 0.0 copy-start.14
  4.6 0.0 copy-done.18
  4.6 0.2 fusion.15.bias
  4.8 0.0 copy-done.16
  4.8 0.3 fusion.7
  5.1 0.0 copy-done.17
  5.1 0.1 dynamic_slice.13
  5.2 0.1 broadcast_multiply_fusion
  5.3 0.2 fusion.13
  5.5 0.2 copy.29
  5.8 0.3 fusion.10
  6.0 0.0 copy-done.14
  6.0 0.0 copy-start.1
  6.0 0.0 copy-start.3
  6.1 0.0 copy-start.4
  6.1 0.0 copy-start.5
  6.1 0.0 copy-start.6
  6.1 0.2 fusion.14
  6.3 0.2 copy.28
  6.6 0.7 pad_maximum_fusion.sides
  7.3 0.0 copy-done.1
  7.3 0.0 copy-done.3
  7.3 0.0 copy-done.4
  7.3 0.0 copy-done.5
  7.3 0.0 copy-done.6
  7.3 34.3 %shard_map.131 = (bf16[2,16,4,4,1152]{4,3,2,1,0:T(4,128)(2,1)S(1)}, bf16[2,64,2,1152]{3,2,1,0:T(2,128)(2,1)S(1)}, bf16[1024,128]{1,0:T(8,128)(2,1)S(1)}, bf16[10...) custom-call(bf16[4,1152]{1,0:T(4,128)(2,1)S(1)} %fusion.15.bias, ...), custom_call_target="tpu_custom_call" | custom-call | tf_op jit(solution)/shard_map/pallas_call | solution.py:243
  41.6 0.0 copy-start.7
  41.7 0.6 copy-done.7
  42.3 0.2 constant_dynamic-slice_fusion.1
  42.6 0.1 reshape_squeeze.3
  42.6 0.6 slice.23
  43.3 0.0 copy-done.9
  43.3 0.0 copy-done.11
  43.3 0.0 copy-start.2
  43.4 0.3 copy.31
  43.7 0.2 reshape.78
  43.9 0.3 convolution_convert_fusion.1
  44.1 0.1 reshape.79.rows
  44.2 0.2 fusion.26.pick
  44.5 0.0 copy-done.2
  44.5 0.0 copy-start.8
  44.5 0.8 copy-done.8
  45.4 29.4 %shard_map.132 = (bf16[128,2,768]{2,1,0:T(2,128)(2,1)S(1)}, bf16[128,3,384]{2,1,0:T(4,128)(2,1)S(1)}) custom-call(bf16[64,3,384]{2,1,0:T(4,128)(2,1)S(1)} %reshape.79.rows, bf16[2,384,256]{2,1,0:T(8,128)(2,1)S(1)} %copy-done.2, bf16[192,384]{1,0:T(8,128)(2,1)S(1)} %fusion.26.pick, bf16[2,16,4,4,1152]{4,3,2,1,0:T(4,128)(2,1)S(1)} %get-tuple-element.12.bias_all, ...), custom_call_target="tpu_custom_call" | custom-call | tf_op jit(solution)/shard_map/pallas_call | solution.py:542
  74.8 0.1 reshape.81.column
  75.0 0.0 copy-done.19
  75.0 0.0 copy-start.10
  75.0 0.9 %copy-done.10 = bf16[1024,128]{1,0:T(8,128)(2,1)S(1)} copy-done((bf16[1024,128]{1,0:T(8,128)(2,1)S(1)}, bf16[1024,128]{1,0:T(8,128)(2,1)}, u32[]{:S(2)}) %copy-start.10) | copy-done | bytes 262168
  75.9 0.8 copy-done.12
  76.8 6.0 %shard_map.133 = bf16[256,384]{1,0:T(8,128)(2,1)S(1)} custom-call(bf16[256,768]{1,0:T(8,128)(2,1)S(1)} %reshape.81.column, f32[1,256]{1,0:T(1,128)S(1)} %bitcast.58, bf16[4,256,128]{2,1,0:T(8,128)(2,1)S(1)} %copy-done.3, bf16[4,256,128]{2,1,0:T(8,128)(2,1)S(1)} %bitcast.59, bf16[128,256]{1,0:T(8,128)(2,1)S(1)} %copy-done.6, bf16[128,256]{1,0:T(8,128)(2,1)S(1)} %copy-done.12), custom_call_target="tpu_custom_call" | custom-call | flops 3221225472 | bytes 4194304 | tf_op jit(solution)/shard_map/pallas_call | solution.py:440
  82.8 0.1 copy.32
  82.9 0.8 copy.37
  83.7 0.3 fusion.4
  84.0 0.3 convert_reduce_fusion
  84.4 0.2 fusion.19
  84.6 0.1 copy-done.13
  84.7 0.1 constant_dynamic-slice_fusion
  84.9 0.2 copy.41
  85.1 1.0 %fusion.17 = bf16[3,384,64]{1,2,0:T(8,128)(2,1)} fusion(f32[8,3,8,384]{3,2,1,0:T(8,128)S(1)} %bitcast.69, bf16[128,3,384]{2,1,0:T(4,128)(2,1)S(1)} %fusion.19, bf16[3,384,64]{1,2,0:T(8,128)(2,1)S(1)} %copy.41, s32[]{:T(128)S(6)} %select_n.39, bf16[64,128]{1,0:T(8,128)(2,1)S(1)} %get-tuple-element.29, bf16[64,128]{1,0:T(8,128)(2,1)S(1)} %get-tuple-element.28), kind=kOutput, calls=%fused_computation.27 | convolution fusion | flops 19202048 | bytes 917508 | tf_op jit(solution)/shard_map/cij,cz->ijz/dot_general | solution.py:590
  (24 shorter events, 0.2 us)
Async XLA Ops:
  0.6 83.1 %copy-start = (bf16[128,64]{0,1:T(8,128)(2,1)S(1)}, bf16[128,64]{0,1:T(8,128)(2,1)}, u32[]{:S(2)}) copy-start(bf16[128,64]{0,1:T(8,128)(2,1)} %param.23) | copy-start | bytes 49156
  0.6 4.0 %copy-start.18 = (bf16[128,4]{0,1:T(4,128)(2,1)S(1)}, bf16[128,4]{0,1:T(4,128)(2,1)}, u32[]{:S(2)}) copy-start(bf16[128,4]{0,1:T(4,128)(2,1)} %param.18) | copy-start | bytes 3076
  0.7 4.1 %copy-start.16 = (bf16[4,128,64]{1,2,0:T(8,128)(2,1)S(1)}, bf16[4,128,64]{1,2,0:T(8,128)(2,1)}, u32[]{:S(2)}) copy-start(bf16[4,128,64]{1,2,0:T(8,128)(2,1)} %param.21) | copy-start | bytes 196612
  3.2 1.9 %copy-start.17 = (s32[384]{0:T(512)S(1)}, s32[384]{0:T(512)}, u32[]{:S(2)}) copy-start(s32[384]{0:T(512)} %param.15) | copy-start | bytes 4612
  4.6 1.4 %copy-start.14 = (bf16[3,384,128]{2,1,0:T(8,128)(2,1)}, bf16[3,384,128]{2,1,0:T(8,128)(2,1)S(1)}, u32[]{:S(2)}) copy-start(bf16[3,384,128]{2,1,0:T(8,128)(2,1)S(1)} %fusion.24) | copy-start | bytes 884740
  6.0 1.2 %copy-start.1 = (bf16[4,256,128]{2,1,0:T(8,128)(2,1)S(1)}, bf16[4,256,128]{2,1,0:T(8,128)(2,1)}, u32[]{:S(2)}) copy-start(bf16[4,256,128]{2,1,0:T(8,128)(2,1)} %w.2) | copy-start | bytes 786436
  6.0 1.2 %copy-start.3 = (bf16[4,256,128]{2,1,0:T(8,128)(2,1)S(1)}, bf16[4,256,128]{2,1,0:T(8,128)(2,1)}, u32[]{:S(2)}) copy-start(bf16[4,256,128]{2,1,0:T(8,128)(2,1)} %w.3) | copy-start | bytes 786436
  6.1 1.2 %copy-start.4 = (bf16[128,256]{1,0:T(8,128)(2,1)S(1)}, bf16[128,256]{1,0:T(8,128)(2,1)}, u32[]{:S(2)}) copy-start(bf16[128,256]{1,0:T(8,128)(2,1)} %wo.2) | copy-start | bytes 196612
  6.1 1.2 %copy-start.5 = (bf16[64,128]{1,0:T(8,128)(2,1)S(1)}, bf16[64,128]{1,0:T(8,128)(2,1)}, u32[]{:S(2)}) copy-start(bf16[64,128]{1,0:T(8,128)(2,1)} %final.1) | copy-start | bytes 49156
  6.1 1.2 %copy-start.6 = (bf16[128,256]{1,0:T(8,128)(2,1)S(1)}, bf16[128,256]{1,0:T(8,128)(2,1)}, u32[]{:S(2)}) copy-start(bf16[128,256]{1,0:T(8,128)(2,1)} %wo.3) | copy-start | bytes 196612
  41.6 0.6 copy-start.7
  42.3 1.0 %copy-start.9 = (bf16[1024,128]{1,0:T(8,128)(2,1)}, bf16[1024,128]{1,0:T(8,128)(2,1)S(1)}, u32[]{:S(2)}) copy-start(bf16[1024,128]{1,0:T(8,128)(2,1)S(1)} %get-tuple-element.16) | copy-start | bytes 786436
  42.3 1.0 %copy-start.11 = (bf16[128,256]{1,0:T(8,128)(2,1)}, bf16[128,256]{1,0:T(8,128)(2,1)S(1)}, u32[]{:S(2)}) copy-start(bf16[128,256]{1,0:T(8,128)(2,1)S(1)} %get-tuple-element.17.wox) | copy-start | bytes 196612
  43.3 1.2 %copy-start.2 = (bf16[2,384,256]{2,1,0:T(8,128)(2,1)S(1)}, bf16[2,384,256]{2,1,0:T(8,128)(2,1)}, u32[]{:S(2)}) copy-start(bf16[2,384,256]{2,1,0:T(8,128)(2,1)} %msa.1) | copy-start | bytes 1179652
  44.5 0.8 copy-start.8
  45.4 29.6 %copy-start.19 = (s32[256]{0:T(256)S(1)}, s32[256]{0:T(256)}, u32[]{:S(2)}) copy-start(s32[256]{0:T(256)} %param.14) | copy-start | bytes 3076
  75.0 1.0 %copy-start.10 = (bf16[1024,128]{1,0:T(8,128)(2,1)S(1)}, bf16[1024,128]{1,0:T(8,128)(2,1)}, u32[]{:S(2)}) copy-start(bf16[1024,128]{1,0:T(8,128)(2,1)} %copy-done.9) | copy-start | bytes 786436
  75.9 0.8 copy-start.12
  76.8 7.0 %copy-start.15 = (bf16[3,384,128]{2,1,0:T(8,128)(2,1)S(1)}, bf16[3,384,128]{2,1,0:T(8,128)(2,1)}, u32[]{:S(2)}) copy-start(bf16[3,384,128]{2,1,0:T(8,128)(2,1)} %copy-done.14) | copy-start | bytes 884740
  83.7 1.0 %copy-start.13 = (bf16[3,384,128]{2,1,0:T(8,128)(2,1)S(1)}, bf16[3,384,128]{2,1,0:T(8,128)(2,1)}, u32[]{:S(2)}) copy-start(bf16[3,384,128]{2,1,0:T(8,128)(2,1)} %param.13) | copy-start | bytes 884740

commit v6 on v5

v6 whole, which is shorter than its diff:
```python
import functools

import jax
import jax.numpy as jnp
from jax import lax
from jax.experimental import pallas as pl
from jax.experimental.pallas import tpu as pltpu
from jax.sharding import Mesh
from jax.sharding import PartitionSpec as P

GROUP_BREADTH = 32
CHIPS = ("dap_0", "dap_1", "dap_2")
CORE = "dap_3"
DAP = CHIPS + (CORE,)
MESH = pl.DeviceIdType.MESH
VMEM = pl.BlockSpec(memory_space=pltpu.VMEM)

EPS = 1e-05
NEG = 1000000000.0


def standardize_features(values):
    values = values.astype(jnp.float32)
    center = jnp.mean(values, axis=-1, keepdims=True)
    spread = jnp.mean(jnp.square(values - center), axis=-1, keepdims=True)
    return (values - center) * lax.rsqrt(spread + EPS)


def place():
    z, x, y = (lax.axis_index(a) for a in CHIPS)
    return z, x, y, lax.axis_index(CORE), lax.axis_index("rep")


def send(src, dst, sent, came, device):
    pltpu.make_async_remote_copy(
        src_ref=src, dst_ref=dst, send_sem=sent, recv_sem=came, device_id=device, device_id_type=MESH
    ).start()


def wait_bytes(ref, sem):
    pltpu.make_async_copy(ref, ref, sem).wait()


def greet(device):
    pl.semaphore_signal(pltpu.get_barrier_semaphore(), inc=1, device_id=device, device_id_type=MESH)


def chip_at(to):
    plane, high = 16, 4
    return to // plane, lax.rem(to // high, high), lax.rem(to, high)


def dot_last(a, b):
    return lax.dot_general(a, b, (((1,), (1,)), ((), ())), preferred_element_type=jnp.float32)


def dot(a, b):
    return jnp.dot(a, b, preferred_element_type=jnp.float32)


def project(x, own, other):
    return jnp.concatenate([dot(x, own), dot(x, other)], 1).astype(jnp.bfloat16)


def attend_rows(q, k, v, g, bias, mixed, block, heads):
    embed = q.shape[1]
    queries = q.shape[0]
    lane = lax.broadcasted_iota(jnp.int32, (heads, embed), 1) // GROUP_BREADTH
    head = lax.broadcasted_iota(jnp.int32, (heads, embed), 0)
    own = (lane == head).astype(jnp.float32)[None]
    scale = 1.0 / jnp.sqrt(jnp.float32(GROUP_BREADTH))

    for n in range(queries // block):
        part = slice(n * block, (n + 1) * block)
        wide = q[part].astype(jnp.float32)[:, None, :] * own
        wide = wide.reshape(block * heads, embed).astype(jnp.bfloat16)
        scores = dot_last(wide, k) * scale + bias(n)
        scores = jnp.exp(scores - jnp.max(scores, axis=1, keepdims=True))
        weights = (scores * (1.0 / jnp.sum(scores, axis=1, keepdims=True))).astype(jnp.bfloat16)
        out = dot(weights, v).reshape(block, heads, embed) * own
        out = jnp.sum(out, axis=1)
        gate = 1.0 / (1.0 + jnp.exp(-g[part].astype(jnp.float32)))
        mixed[part, :] = (out * gate).astype(jnp.bfloat16)


def main_kernel(
    pair,
    pair_mask,
    offset_w,
    side_w,
    row_w,
    col_w,
    row_o,
    col_o,
    final,
    msa,
    pick,
    hidden,
    pair_ln,
    column,
    product,
    col_wx,
    col_ox,
    final_x,
    bias,
    sides,
    bias_all,
    sides_all,
    row_wx,
    row_ox,
    rows,
    bias_rows,
    mixed,
    done,
    seqs,
    s_sent,
    s_came,
    line_sent,
    line_came,
    bias_sent,
    bias_came,
    row_sent,
    row_came,
    col_sent,
    col_came,
    core_sent,
    core_came,
    p_sent,
    p_came,
    m_sent,
    m_came,
    *,
    heads,
    block,
):
    z, x, y, c, r = place()
    deep, high = 4, 4
    plane = high * high
    chips = deep * plane
    xy = x * high + y
    chip = z * plane + xy
    me = chip * 2 + c
    channel = r * chips + chip
    here = (z, x, y)
    chunk = row_w.shape[0] // (2 * plane)
    mirror = (deep - 1 - z, x, y, c, 1 - r)
    partner = (z, x, y, 1 - c, r)
    rows_each, sites = pair.shape[0], pair.shape[1]
    embed = msa.shape[2]

    def rows_of(at):
        return pl.ds(pl.multiple_of((c * plane + at) * chunk, chunk), chunk)

    mine = rows_of(xy)

    def greet_chip(i, carry):
        there = chip_at(lax.rem(chip + i, chips))
        for ct in range(2):
            for rt in range(2):
                greet((*there, ct, rt))
        return carry

    lax.fori_loop(1, chips, greet_chip, 0)
    greet((*here, 1 - c, r))
    greet((*here, c, 1 - r))
    greet((*here, 1 - c, 1 - r))

    for t in range(rows_each):
        part = slice(t * sites, (t + 1) * sites)
        normed = standardize_features(pair[t]).astype(jnp.bfloat16)
        pair_ln[t] = normed
        bias[:, part] = dot_last(offset_w[...], normed).astype(jnp.bfloat16)
        both = []
        for n in range(2):
            gate = dot_last(side_w[2 * n], normed)
            value = dot_last(side_w[2 * n + 1], normed)
            side = value / (1.0 + jnp.exp(-gate)) * pair_mask[t : t + 1, :]
            both.append(side[:, None, :])
        sides[:, :, part] = jnp.concatenate(both, 1).astype(jnp.bfloat16)
    sides_all[c, chip] = sides[chip]

    @pl.when(c == r)
    def _():
        bias_all[r, xy, z] = bias[...]

    pl.semaphore_wait(pltpu.get_barrier_semaphore(), 4 * chips - 1)

    for dz in range(deep):
        zt = lax.rem(z + dz, deep)
        if dz == 0:

            @pl.when(c != r)
            def _():
                send(bias, bias_all.at[r, xy, z], line_sent.at[0], line_came.at[0], (zt, x, y, r, c))

        else:
            send(bias, bias_all.at[r, xy, z], line_sent.at[0], line_came.at[0], (zt, x, y, r, c))
    send(row_w.at[mine], row_wx.at[mine], line_sent.at[1], line_came.at[1], mirror)
    send(col_w.at[mine], col_wx.at[mine], line_sent.at[2], line_came.at[2], mirror)
    o_half = pl.ds(pl.multiple_of(c * (row_o.shape[0] // 2), row_o.shape[0] // 2), row_o.shape[0] // 2)
    send(row_o.at[o_half], row_ox.at[o_half], line_sent.at[3], line_came.at[3], mirror)
    send(col_o.at[o_half], col_ox.at[o_half], line_sent.at[4], line_came.at[4], mirror)
    send(final, final_x, line_sent.at[5], line_came.at[5], mirror)

    def to_owner(i, carry):
        to = lax.rem(chip + i, chips)
        send(sides.at[to], sides_all.at[c, chip], s_sent, s_came.at[z], (*chip_at(to), c, r))
        return carry

    lax.fori_loop(1, plane, to_owner, 0)

    @pl.when(c == r)
    def _():
        wait_bytes(bias_all.at[0, 0, pl.ds(0, deep - 1)], line_came.at[0])

    @pl.when(c != r)
    def _():
        wait_bytes(bias_all.at[0, 0], line_came.at[0])

    def plane_device(i):
        to = lax.rem(xy + i, plane)
        return (z, to // high, lax.rem(to, high), c, r)

    def bias_plane(i, carry):
        send(bias_all.at[c, xy], bias_all.at[c, xy], bias_sent, bias_came.at[xy], plane_device(i))
        return carry

    lax.fori_loop(1, plane, bias_plane, 0)
    wait_bytes(row_wx.at[mine], line_came.at[1])
    wait_bytes(col_wx.at[mine], line_came.at[2])

    def weight_plane(i, carry):
        device = plane_device(i)
        send(row_wx.at[mine], row_wx.at[mine], row_sent, row_came.at[xy], device)
        send(col_wx.at[mine], col_wx.at[mine], col_sent, col_came.at[xy], device)
        return carry

    lax.fori_loop(1, plane, weight_plane, 0)
    lax.fori_loop(plane, chips, to_owner, 0)

    send(bias_all.at[c, xy], bias_all.at[c, xy], core_sent.at[0], core_came.at[0], partner)
    send(row_wx.at[mine], row_wx.at[mine], core_sent.at[1], core_came.at[1], partner)
    send(col_wx.at[mine], col_wx.at[mine], core_sent.at[2], core_came.at[2], partner)
    wait_bytes(row_ox.at[o_half], line_came.at[3])
    send(row_ox.at[o_half], row_ox.at[o_half], core_sent.at[3], core_came.at[3], partner)
    wait_bytes(col_ox.at[o_half], line_came.at[4])
    send(col_ox.at[o_half], col_ox.at[o_half], core_sent.at[4], core_came.at[4], partner)

    def bias_core(i, carry):
        at = lax.rem(xy + i, plane)
        wait_bytes(bias_all.at[c, at], bias_came.at[at])
        send(bias_all.at[c, at], bias_all.at[c, at], core_sent.at[0], core_came.at[0], partner)
        return carry

    lax.fori_loop(1, plane, bias_core, 0)

    def weight_core(i, carry):
        at = lax.rem(xy + i, plane)
        rows = rows_of(at)
        wait_bytes(row_wx.at[rows], row_came.at[at])
        send(row_wx.at[rows], row_wx.at[rows], core_sent.at[1], core_came.at[1], partner)
        wait_bytes(col_wx.at[rows], col_came.at[at])
        send(col_wx.at[rows], col_wx.at[rows], core_sent.at[2], core_came.at[2], partner)
        return carry

    lax.fori_loop(1, plane, weight_core, 0)

    def pass_sides(level):
        for n in range(4):
            part = pl.ds(pl.multiple_of(level * plane + n * high, high), high)
            send(sides_all.at[c, part], sides_all.at[c, part], core_sent.at[5], core_came.at[5], partner)

    wait_bytes(sides_all.at[0, pl.ds(0, plane - 1)], s_came.at[z])
    pass_sides(z)
    for dz in range(1, deep):
        level = lax.rem(z + dz, deep)
        wait_bytes(sides_all.at[0, pl.ds(0, plane)], s_came.at[level])
        pass_sides(level)

    wait_bytes(sides_all.at[0], core_came.at[5])
    site = lax.broadcasted_iota(jnp.int32, (sites, chips), 0)
    owner = lax.broadcasted_iota(jnp.int32, (sites, chips), 1)

    def side_of(core, t, n):
        part = sides_all[core, :, :, t * sites : (t + 1) * sites].astype(jnp.float32)
        return part[:, n, :].astype(jnp.bfloat16)

    rights = jnp.zeros((sites, sites), jnp.float32)
    for core in range(2):
        for t in range(rows_each):
            put = site == owner * (2 * rows_each) + (core * rows_each + t)
            rights += dot(put.astype(jnp.float32).astype(jnp.bfloat16), side_of(core, t, 1))
    rights = rights.astype(jnp.bfloat16)
    parts = [dot_last(side_of(c, t, 0), rights)[:, None, :] for t in range(rows_each)]
    rows[...] = jnp.concatenate(parts, 1).astype(jnp.bfloat16)
    product[channel] = rows[chip]

    def to_rows(i, carry):
        to = lax.rem(chip + i, chips)
        send(rows.at[to], product.at[channel], p_sent, p_came, (*chip_at(to), c, 1 - r))
        send(rows.at[to], product.at[channel], p_sent, p_came, (*chip_at(to), c, r))
        return carry

    lax.fori_loop(1, chips, to_rows, 0)
    send(rows.at[chip], product.at[channel], p_sent, p_came, (*here, c, 1 - r))

    half_rows = pl.ds(0, plane * chunk)
    wait_bytes(bias_all.at[0], core_came.at[0])
    wait_bytes(row_wx.at[half_rows], core_came.at[1])
    wait_bytes(row_ox.at[o_half], core_came.at[3])
    away = hidden[...]

    def place_bias(p, carry):
        at, level = lax.rem(p, plane), p // plane
        both = jnp.concatenate(
            [
                bias_all[r, at, level].astype(jnp.float32),
                bias_all[1 - r, at, level].astype(jnp.float32),
            ],
            0,
        )
        for t in range(rows_each):
            bias_rows[t * chips + p] = both[:, t * sites : (t + 1) * sites] + away
        return carry

    lax.fori_loop(0, chips, place_bias, 0)

    def part_of(n):
        return slice(n * embed, (n + 1) * embed)

    def one(s, carry):
        x = standardize_features(msa[s]).astype(jnp.bfloat16)
        xq = dot(pick[...], x).astype(jnp.bfloat16)
        q = project(xq, row_w[part_of(0)], row_wx[part_of(0)])
        k = project(x, row_w[part_of(1)], row_wx[part_of(1)])
        v = project(x, row_w[part_of(2)], row_wx[part_of(2)])
        g = project(xq, row_w[part_of(3)], row_wx[part_of(3)])

        def bias_of(n):
            return bias_rows[n * block : (n + 1) * block].reshape(block * heads, sites)

        attend_rows(q, k, v, g, bias_of, mixed, block, heads)
        half = row_o.shape[0]
        delta = dot(mixed[:, :half], row_o[...]) + dot(mixed[:, half:], row_ox[...])
        done[s] = dot(pick[...], msa[s]) + delta
        return carry

    lax.fori_loop(0, msa.shape[0], one, 0)
    for t in range(rows_each):
        part = slice(t * chips, (t + 1) * chips)
        both = jnp.concatenate([done[0, part, :][:, None, :], done[1, part, :][:, None, :]], 1)
        seqs[:, :, t * embed : (t + 1) * embed] = both.astype(jnp.bfloat16)

    @pl.when(c == r)
    def _():
        column[me] = seqs[chip]

    def to_owner(i, carry):
        to = lax.rem(chip + i, chips)
        send(seqs.at[to], column.at[me], m_sent, m_came, (*chip_at(to), r, 1 - r))
        send(seqs.at[to], column.at[me], m_sent, m_came, (*chip_at(to), r, r))
        return carry

    lax.fori_loop(1, chips, to_owner, 0)

    @pl.when(c != r)
    def _():
        send(seqs.at[chip], column.at[me], m_sent, m_came, (*here, r, r))

    send(seqs.at[chip], column.at[me], m_sent, m_came, (*here, r, 1 - r))

    for sem in (m_came, m_sent):

        @pl.when(c == r)
        def _():
            wait_bytes(column.at[pl.ds(0, 2 * chips - 1)], sem)

        @pl.when(c != r)
        def _():
            wait_bytes(column, sem)

    for sem in (p_came, p_sent):
        wait_bytes(product.at[pl.ds(0, 2 * chips - 1)], sem)

    half = pl.ds(0, plane * chunk)
    rest = pl.ds(0, (plane - 1) * chunk)
    wait_bytes(final_x, line_came.at[5])
    for sems in (core_came, core_sent):
        wait_bytes(col_wx.at[half], sems.at[2])
        wait_bytes(col_ox.at[o_half], sems.at[4])

    wait_bytes(bias_all.at[0], core_sent.at[0])
    wait_bytes(row_wx.at[half], core_sent.at[1])
    wait_bytes(row_ox.at[o_half], core_sent.at[3])
    wait_bytes(sides_all.at[0], core_sent.at[5])

    @pl.when(c == r)
    def _():
        wait_bytes(bias_all.at[0, 0, pl.ds(0, deep - 1)], line_sent.at[0])

    @pl.when(c != r)
    def _():
        wait_bytes(bias_all.at[0, 0], line_sent.at[0])

    wait_bytes(row_wx.at[mine], line_sent.at[1])
    wait_bytes(col_wx.at[mine], line_sent.at[2])
    wait_bytes(row_ox.at[o_half], line_sent.at[3])
    wait_bytes(col_ox.at[o_half], line_sent.at[4])
    wait_bytes(final_x, line_sent.at[5])
    wait_bytes(bias_all.at[0, pl.ds(0, plane - 1)], bias_sent)
    wait_bytes(row_wx.at[rest], row_sent)
    wait_bytes(col_wx.at[rest], col_sent)
    wait_bytes(sides_all.at[0, pl.ds(0, chips - 1)], s_sent)


def col_kernel(column, hidden, w, wx, wo, wox, out, mixed, *, heads, block):
    r = lax.axis_index("rep")
    embed = w.shape[1]
    width = embed // 2
    at = pl.ds(pl.multiple_of(r * width, width), width)
    away = hidden[...]
    for t in range(column.shape[1] // embed):
        x = standardize_features(column[:, t * embed : (t + 1) * embed]).astype(jnp.bfloat16)
        q, k, v, g = [project(x, w[n], wx[n]) for n in range(4)]
        attend_rows(q, k, v, g, lambda n: away, mixed, block, heads)
        half = wo.shape[0]
        delta = dot(mixed[:, :half], wo[:, at]) + dot(mixed[:, half:], wox[:, at])
        keep = column[:, pl.ds(pl.multiple_of(t * embed + r * width, width), width)]
        out[:, t * width : (t + 1) * width] = (keep.astype(jnp.float32) + delta).astype(jnp.bfloat16)


def local_call(kernel, out, scratch, flops, *operands):
    return pl.pallas_call(
        kernel,
        out_shape=jax.ShapeDtypeStruct(out, jnp.bfloat16),
        in_specs=[VMEM] * len(operands),
        out_specs=VMEM,
        scratch_shapes=[pltpu.VMEM(*s) for s in scratch],
        compiler_params=pltpu.CompilerParams(vmem_limit_bytes=40 << 20),
        cost_estimate=pl.CostEstimate(flops=flops, bytes_accessed=4 << 20, transcendentals=0),
    )(*operands)


def per_device(
    msa,
    pair,
    homolog_present,
    amino_present,
    row_w,
    row_out,
    offset_w,
    col_w,
    col_out,
    side_w,
    final_w,
    sigmoid_w,
):
    rep = lax.axis_index("rep")
    rows_here, sites, channels = pair.shape
    seqs_here, embed = msa.shape[0], msa.shape[2]
    chips = lax.axis_size(CHIPS)
    devices = lax.axis_size(DAP)
    heads_here = offset_w.shape[1]
    heads = 2 * heads_here
    row_start = lax.axis_index(DAP) * rows_here
    res_float = amino_present.astype(jnp.float32)
    mask_rows = lax.dynamic_slice_in_dim(res_float, row_start, rows_here, 0)
    flat = rows_here * sites
    pair_mask = mask_rows[:, None] * res_float[None, :]
    flat_w = (row_w.shape[0] * row_w.shape[1], row_w.shape[2])
    queries = chips * rows_here
    query = lax.broadcasted_iota(jnp.int32, (queries, sites), 0)
    site = lax.broadcasted_iota(jnp.int32, (queries, sites), 1)
    picked = 2 * rows_here * (query % chips) + rows_here * rep + query // chips
    pick = (site == picked).astype(jnp.bfloat16)
    hidden = (NEG * (res_float - 1.0))[None, :]
    operands = (
        pair,
        pair_mask,
        offset_w.T,
        side_w.swapaxes(1, 2),
        row_w.reshape(flat_w),
        col_w.reshape(flat_w),
        row_out,
        col_out,
        final_w,
        msa,
        pick,
        hidden,
    )
    side_channels = side_w.shape[2]
    bf = jnp.bfloat16
    outs = [
        pair.shape,
        (devices, seqs_here, rows_here * embed),
        (devices, rows_here, sites),
        flat_w,
        col_out.shape,
        final_w.shape,
    ]
    scratch = [
        ((heads_here, flat), bf),
        ((side_channels, 2, flat), bf),
        ((2, 16, chips // 16, heads_here, flat), bf),
        ((2, chips, 2, flat), bf),
        (flat_w, bf),
        (row_out.shape, bf),
        ((chips, rows_here, sites), bf),
        ((queries, heads, sites), jnp.float32),
        ((queries, embed), bf),
        ((seqs_here, queries, embed), jnp.float32),
        ((chips, seqs_here, rows_here * embed), bf),
    ]
    semaphores = [0, 4, 6, 6, 0, 16, 0, 16, 0, 16, 6, 6, 0, 0, 0, 0]
    pair_ln, column, product, col_wx, col_ox, final_x = pl.pallas_call(
        functools.partial(main_kernel, heads=heads, block=24),
        out_shape=[jax.ShapeDtypeStruct(shape, bf) for shape in outs],
        in_specs=[VMEM] * len(operands),
        out_specs=[VMEM] * len(outs),
        scratch_shapes=[pltpu.VMEM(*one) for one in scratch]
        + [pltpu.SemaphoreType.DMA if n == 0 else pltpu.SemaphoreType.DMA((n,)) for n in semaphores],
        compiler_params=pltpu.CompilerParams(
            collective_id=0, has_side_effects=True, vmem_limit_bytes=48 << 20
        ),
    )(*operands)
    pair_ln = pair_ln.reshape(flat, channels)

    column = column.reshape(devices * seqs_here, rows_here * embed)
    away = (NEG * (homolog_present.astype(jnp.float32) - 1.0))[None, :]
    width = embed // 2
    alignment_output = local_call(
        functools.partial(col_kernel, heads=heads, block=32),
        (devices * seqs_here, rows_here * width),
        [((devices * seqs_here, embed), jnp.bfloat16)],
        3 << 30,
        column,
        away,
        col_w,
        col_wx.reshape(col_w.shape),
        col_out,
        col_ox,
    ).reshape(devices * seqs_here, rows_here, width)

    product = product.astype(jnp.float32)
    mean = jnp.mean(product, axis=0)
    square = jnp.mean(product * product, axis=0)
    scaled = ((product - mean) * lax.rsqrt(square - mean * mean + EPS)).astype(jnp.bfloat16)
    half = channels // 2
    first = jnp.where(rep == 0, final_w, final_x)
    second = jnp.where(rep == 0, final_x, final_w)
    final_all = jnp.concatenate([first, second], 0)
    final_half = lax.dynamic_slice_in_dim(final_all, rep * half, half, 1)
    tri_update = jnp.einsum("cij,cz->ijz", scaled, final_half, preferred_element_type=jnp.float32)
    pair_half = lax.dynamic_slice_in_dim(pair, rep * half, half, 2)
    gate_out = jax.nn.sigmoid(dot(pair_ln, sigmoid_w)).reshape(rows_here, sites, half)
    pair_output = (pair_half.astype(jnp.float32) + gate_out * tri_update).astype(jnp.bfloat16)
    return (alignment_output, pair_output)


def solution(mesh):
    finer = Mesh(
        mesh.devices.reshape(4, 4, 4, 2, mesh.shape["rep"]),
        (*DAP, "rep"),
    )
    return jax.shard_map(
        per_device,
        mesh=finer,
        in_specs=(
            P(DAP, None, None),
            P(DAP, None, None),
            P(),
            P(),
            P(None, None, "rep"),
            P("rep", None),
            P(None, "rep"),
            P(None, None, "rep"),
            P("rep", None),
            P(None, None, "rep"),
            P("rep", None),
            P(None, "rep"),
        ),
        out_specs=(P(None, DAP, "rep"), P(DAP, None, "rep")),
        check_vma=False,
    )
```

time: 86.3 us -> 79.7 us (0.924)
  other arithmetic: 5.46 us -> 1.58 us
  Pallas kernels: 69.8 us -> 67.7 us
  matrix products: 2.69 us -> 1.23 us
  local copies, waits for them, and re-layouts: 7 us -> 8.01 us
    unnamed x43 -> x30, local copies, waits for them, and re-layouts: 4.48 us -> 7.49 us
    reduce_sum x2 -> x0, other arithmetic: 2.55 us -> none  [the longest x1 1.37 us: standardize_features(): spread = jnp.mean(jnp.square(values - center), axis=-1, keepdims=True)]
    pallas_call x2 -> x1, Pallas kernels: 63.8 us -> 61.7 us  [per_device(): pl.pallas_call(functools.partial(main_kernel, heads=heads, block=24), out...]
    dot_general x6 -> x0, matrix products: 1.46 us -> none  [the longest x2 0.54 us: gated_side(): jnp.einsum('nd,dc->cn', pair_ln, gate_weight, preferred_element_type=jnp....]
    convert_element_type x1 -> x0, other arithmetic: 1.33 us -> none  [per_device(): standardize_features(pair).astype(jnp.bfloat16).reshape(flat, channels)]
where the time goes in v6:
time: 79.7 us; the launch traced here: 79.3 us
  Pallas kernels  67.7 us (85%)
  local copies, waits for them, and re-layouts  8.01 us (10%)
  other arithmetic  1.58 us (2%)
  matrix products  1.23 us (2%)
    pallas_call x1, Pallas kernels, per_device(): pl.pallas_call(functools.partial(main_kernel, heads=heads, block=24), out...  61.7 us
    unnamed x30, local copies, waits for them, and re-layouts  7.49 us
    pallas_call x1, Pallas kernels, local_call(): pl.pallas_call(kernel, out_shape=jax.ShapeDtypeStruct(out, jnp.bfloat16),...  5.96 us

profile of v6, /device:TPU:1, one launch (start us, length us, event | category | flops | bytes accessed | tf_op | source)
XLA Modules:
  0.0 79.3 jit_solution(7524037979345406726)
XLA Ops:
  0.6 0.0 copy-start
  0.6 0.7 convert_element_type.21
  1.3 0.0 copy-start.10
  1.3 0.1 dynamic_slice.9
  1.4 0.1 broadcast_multiply_fusion.1.pair_mask
  1.5 0.0 copy-start.12
  1.5 0.0 copy-start.7
  1.5 0.0 copy-start.8
  1.5 0.0 copy-start.9
  1.6 0.2 fusion.9.pick
  1.8 0.4 copy-done.12
  2.2 0.0 copy-start.11
  2.2 0.0 copy-done.10
  2.2 0.0 copy-done.7
  2.2 0.1 copy-done.8
  2.4 0.0 copy-done.9
  2.4 0.5 copy-done.11
  2.9 0.0 copy-start.1
  2.9 1.0 %copy-done.1 = bf16[3,384,128]{2,1,0:T(8,128)(2,1)S(1)} copy-done((bf16[3,384,128]{2,1,0:T(8,128)(2,1)S(1)}, bf16[3,384,128]{2,1,0:T(8,128)(2,1)}, u32[]{:S(2)}) %copy-start.1) | copy-done | bytes 294936
  3.9 0.0 copy-start.3
  3.9 1.0 %copy-done.3 = bf16[2,384,256]{2,1,0:T(8,128)(2,1)S(1)} copy-done((bf16[2,384,256]{2,1,0:T(8,128)(2,1)S(1)}, bf16[2,384,256]{2,1,0:T(8,128)(2,1)}, u32[]{:S(2)}) %copy-start.3) | copy-done | bytes 393240
  4.8 0.0 copy-start.4
  4.8 0.9 %copy-done.4 = bf16[4,256,128]{2,1,0:T(8,128)(2,1)S(1)} copy-done((bf16[4,256,128]{2,1,0:T(8,128)(2,1)S(1)}, bf16[4,256,128]{2,1,0:T(8,128)(2,1)}, u32[]{:S(2)}) %copy-start.4) | copy-done | bytes 262168
  5.8 0.0 copy-start.5
  5.8 0.9 %copy-done.5 = bf16[4,256,128]{2,1,0:T(8,128)(2,1)S(1)} copy-done((bf16[4,256,128]{2,1,0:T(8,128)(2,1)S(1)}, bf16[4,256,128]{2,1,0:T(8,128)(2,1)}, u32[]{:S(2)}) %copy-start.5) | copy-done | bytes 262168
  6.7 61.7 %shard_map.131 = (bf16[3,384,128]{2,1,0:T(8,128)(2,1)S(1)}, bf16[128,2,768]{2,1,0:T(2,128)(2,1)S(1)}, bf16[128,3,384]{2,1,0:T(4,128)(2,1)S(1)}, bf16[1024,128]{1...) custom-call(bf16[3,384,128]{2,1,0:T(8,128)(2,1)S(1)} %copy-done.1, ...), custom_call_target="tpu_custom_call" | custom-call | tf_op jit(solution)/shard_map/pallas_call | solution.py:515
  68.5 0.0 copy-start.13
  68.5 0.0 copy-start.6
  68.5 0.1 reshape.41.column
  68.7 0.5 copy-done.13
  69.2 0.3 copy-done.6
  69.5 6.0 %shard_map.132 = bf16[256,384]{1,0:T(8,128)(2,1)S(1)} custom-call(bf16[256,768]{1,0:T(8,128)(2,1)S(1)} %reshape.41.column, f32[1,256]{1,0:T(1,128)S(1)} %bitcast.19, bf16[4,256,128]{2,1,0:T(8,128)(2,1)S(1)} %copy-done.6, bf16[4,256,128]{2,1,0:T(8,128)(2,1)S(1)} %bitcast.22, bf16[128,256]{1,0:T(8,128)(2,1)S(1)} %copy-done.10, ...), custom_call_target="tpu_custom_call" | custom-call | flops 3221225472 | bytes 4194304 | tf_op jit(solution)/shard_map/pallas_call | solution.py:433
  75.4 0.1 copy.19
  75.6 0.8 %copy.24 = bf16[256,3,128]{2,0,1:T(8,128)(2,1)} copy(bf16[256,3,128]{0,2,1:T(8,128)(2,1)S(1)} %bitcast.23) | data formatting | bytes 393216
  76.4 0.0 copy-done
  76.4 0.3 fusion.2
  76.7 0.3 convert_reduce_fusion
  77.0 0.0 copy-start.2
  77.0 0.2 fusion.6
  77.2 0.7 copy-done.2
  78.0 0.1 constant_dynamic-slice_fusion
  78.1 0.2 copy.27
  78.3 1.0 %fusion.4 = bf16[3,384,64]{1,2,0:T(8,128)(2,1)} fusion(f32[8,3,8,384]{3,2,1,0:T(8,128)S(1)} %bitcast.24, bf16[128,3,384]{2,1,0:T(4,128)(2,1)S(1)} %fusion.6, bf16[3,384,64]{1,2,0:T(8,128)(2,1)S(1)} %copy.27, s32[]{:T(128)S(6)} %select_n.34, bf16[64,128]{1,0:T(8,128)(2,1)S(1)} %get-tuple-element.21, bf16[64,128]{1,0:T(8,128)(2,1)S(1)} %get-tuple-element.20), kind=kOutput, calls=%fused_computation.9 | convolution fusion | flops 19202048 | bytes 917508 | tf_op jit(solution)/shard_map/cij,cz->ijz/dot_general | solution.py:553
  (8 shorter events, 0.0 us)
Async XLA Ops:
  0.6 75.8 %copy-start = (bf16[128,64]{0,1:T(8,128)(2,1)S(1)}, bf16[128,64]{0,1:T(8,128)(2,1)}, u32[]{:S(2)}) copy-start(bf16[128,64]{0,1:T(8,128)(2,1)} %param.23) | copy-start | bytes 49156
  1.3 0.9 %copy-start.10 = (bf16[128,256]{1,0:T(8,128)(2,1)S(1)}, bf16[128,256]{1,0:T(8,128)(2,1)}, u32[]{:S(2)}) copy-start(bf16[128,256]{1,0:T(8,128)(2,1)} %wo.1) | copy-start | bytes 196612
  1.5 0.7 copy-start.12
  1.5 0.7 copy-start.7
  1.5 0.9 %copy-start.8 = (bf16[4,128,64]{1,2,0:T(8,128)(2,1)S(1)}, bf16[4,128,64]{1,2,0:T(8,128)(2,1)}, u32[]{:S(2)}) copy-start(bf16[4,128,64]{1,2,0:T(8,128)(2,1)} %param.21) | copy-start | bytes 196612
  1.5 0.9 %copy-start.9 = (bf16[128,256]{1,0:T(8,128)(2,1)S(1)}, bf16[128,256]{1,0:T(8,128)(2,1)}, u32[]{:S(2)}) copy-start(bf16[128,256]{1,0:T(8,128)(2,1)} %row_o.1) | copy-start | bytes 196612
  2.2 0.7 copy-start.11
  2.9 1.0 %copy-start.1 = (bf16[3,384,128]{2,1,0:T(8,128)(2,1)S(1)}, bf16[3,384,128]{2,1,0:T(8,128)(2,1)}, u32[]{:S(2)}) copy-start(bf16[3,384,128]{2,1,0:T(8,128)(2,1)} %pair.1) | copy-start | bytes 884740
  3.9 1.0 %copy-start.3 = (bf16[2,384,256]{2,1,0:T(8,128)(2,1)S(1)}, bf16[2,384,256]{2,1,0:T(8,128)(2,1)}, u32[]{:S(2)}) copy-start(bf16[2,384,256]{2,1,0:T(8,128)(2,1)} %msa.1) | copy-start | bytes 1179652
  4.8 0.9 %copy-start.4 = (bf16[4,256,128]{2,1,0:T(8,128)(2,1)S(1)}, bf16[4,256,128]{2,1,0:T(8,128)(2,1)}, u32[]{:S(2)}) copy-start(bf16[4,256,128]{2,1,0:T(8,128)(2,1)} %param.16) | copy-start | bytes 786436
  5.8 0.9 %copy-start.5 = (bf16[4,256,128]{2,1,0:T(8,128)(2,1)S(1)}, bf16[4,256,128]{2,1,0:T(8,128)(2,1)}, u32[]{:S(2)}) copy-start(bf16[4,256,128]{2,1,0:T(8,128)(2,1)} %w.1) | copy-start | bytes 786436
  68.5 0.7 copy-start.13
  68.5 1.0 %copy-start.6 = (bf16[4,256,128]{2,1,0:T(8,128)(2,1)S(1)}, bf16[4,256,128]{2,1,0:T(8,128)(2,1)}, u32[]{:S(2)}) copy-start(bf16[4,256,128]{2,1,0:T(8,128)(2,1)} %w.1) | copy-start | bytes 786436
  77.0 1.0 %copy-start.2 = (bf16[3,384,128]{2,1,0:T(8,128)(2,1)S(1)}, bf16[3,384,128]{2,1,0:T(8,128)(2,1)}, u32[]{:S(2)}) copy-start(bf16[3,384,128]{2,1,0:T(8,128)(2,1)} %pair.1) | copy-start | bytes 884740

commit v7 on v6

--- a/solution.py
+++ b/solution.py
@@ -84,23 +84,30 @@
 
 
 def main_kernel(
-    pair,
+    pair_in,
+    side_in,
+    msa_in,
+    row_w_in,
+    row_o_in,
+    col_w_in,
+    col_o_in,
     pair_mask,
     offset_w,
-    side_w,
-    row_w,
-    col_w,
-    row_o,
-    col_o,
     final,
-    msa,
+    sigmoid_w,
     pick,
     hidden,
-    pair_ln,
+    pair_out,
     column,
-    product,
     col_wx,
     col_ox,
+    pair,
+    side_w,
+    msa,
+    row_w,
+    row_o,
+    pair_ln,
+    product,
     final_x,
     bias,
     sides,
@@ -129,10 +136,16 @@
     p_came,
     m_sent,
     m_came,
+    loaded,
     *,
     heads,
     block,
 ):
+    loads = []
+    moves = [(pair_in, pair), (side_in, side_w), (msa_in, msa), (row_w_in, row_w), (row_o_in, row_o)]
+    for n, (src, dst) in enumerate(moves):
+        loads.append(pltpu.make_async_copy(src, dst, loaded.at[n]))
+        loads[-1].start()
     z, x, y, c, r = place()
     deep, high = 4, 4
     plane = high * high
@@ -165,6 +178,8 @@
     greet((*here, c, 1 - r))
     greet((*here, 1 - c, 1 - r))
 
+    loads[0].wait()
+    loads[1].wait()
     for t in range(rows_each):
         part = slice(t * sites, (t + 1) * sites)
         normed = standardize_features(pair[t]).astype(jnp.bfloat16)
@@ -195,11 +210,11 @@
 
         else:
             send(bias, bias_all.at[r, xy, z], line_sent.at[0], line_came.at[0], (zt, x, y, r, c))
-    send(row_w.at[mine], row_wx.at[mine], line_sent.at[1], line_came.at[1], mirror)
-    send(col_w.at[mine], col_wx.at[mine], line_sent.at[2], line_came.at[2], mirror)
+    send(row_w_in.at[mine], row_wx.at[mine], line_sent.at[1], line_came.at[1], mirror)
+    send(col_w_in.at[mine], col_wx.at[mine], line_sent.at[2], line_came.at[2], mirror)
     o_half = pl.ds(pl.multiple_of(c * (row_o.shape[0] // 2), row_o.shape[0] // 2), row_o.shape[0] // 2)
-    send(row_o.at[o_half], row_ox.at[o_half], line_sent.at[3], line_came.at[3], mirror)
-    send(col_o.at[o_half], col_ox.at[o_half], line_sent.at[4], line_came.at[4], mirror)
+    send(row_o_in.at[o_half], row_ox.at[o_half], line_sent.at[3], line_came.at[3], mirror)
+    send(col_o_in.at[o_half], col_ox.at[o_half], line_sent.at[4], line_came.at[4], mirror)
     send(final, final_x, line_sent.at[5], line_came.at[5], mirror)
 
     def to_owner(i, carry):
@@ -308,6 +323,8 @@
     wait_bytes(bias_all.at[0], core_came.at[0])
     wait_bytes(row_wx.at[half_rows], core_came.at[1])
     wait_bytes(row_ox.at[o_half], core_came.at[3])
+    for load in loads[2:]:
+        load.wait()
     away = hidden[...]
 
     def place_bias(p, carry):
@@ -369,6 +386,30 @@
 
     send(seqs.at[chip], column.at[me], m_sent, m_came, (*here, r, 1 - r))
 
+    wait_bytes(product.at[pl.ds(0, 2 * chips - 1)], p_came)
+    wait_bytes(final_x, line_came.at[5])
+    ours, theirs = final[...].astype(jnp.float32), final_x[...].astype(jnp.float32)
+    first = jnp.where(r == 0, ours, theirs)
+    second = jnp.where(r == 0, theirs, ours)
+    finals = jnp.concatenate([first, second], 0).astype(jnp.bfloat16)
+    width = pair_out.shape[1]
+
+    def half_of(values):
+        return jnp.where(r == 0, values[:width], values[width:])
+
+    products = product[...].astype(jnp.float32)
+    for t in range(rows_each):
+        value = products[:, t, :]
+        mean = jnp.mean(value, axis=0, keepdims=True)
+        square = jnp.mean(value * value, axis=0, keepdims=True)
+        scaled = ((value - mean) * lax.rsqrt(square - mean * mean + EPS)).astype(jnp.bfloat16)
+        update = lax.dot_general(
+            finals, scaled, (((0,), (0,)), ((), ())), preferred_element_type=jnp.float32
+        )
+        gate = 1.0 / (1.0 + jnp.exp(-dot_last(sigmoid_w[...], pair_ln[t])))
+        keep = half_of(pair[t].astype(jnp.float32).T)
+        pair_out[t] = (keep + gate * half_of(update)).astype(jnp.bfloat16)
+
     for sem in (m_came, m_sent):
 
         @pl.when(c == r)
@@ -379,12 +420,10 @@
         def _():
             wait_bytes(column, sem)
 
-    for sem in (p_came, p_sent):
-        wait_bytes(product.at[pl.ds(0, 2 * chips - 1)], sem)
+    wait_bytes(product.at[pl.ds(0, 2 * chips - 1)], p_sent)
 
     half = pl.ds(0, plane * chunk)
     rest = pl.ds(0, (plane - 1) * chunk)
-    wait_bytes(final_x, line_came.at[5])
     for sems in (core_came, core_sent):
         wait_bytes(col_wx.at[half], sems.at[2])
         wait_bytes(col_ox.at[o_half], sems.at[4])
@@ -426,7 +465,7 @@
         half = wo.shape[0]
         delta = dot(mixed[:, :half], wo[:, at]) + dot(mixed[:, half:], wox[:, at])
         keep = column[:, pl.ds(pl.multiple_of(t * embed + r * width, width), width)]
-        out[:, t * width : (t + 1) * width] = (keep.astype(jnp.float32) + delta).astype(jnp.bfloat16)
+        out[t] = (keep.astype(jnp.float32) + delta).astype(jnp.bfloat16)
 
 
 def local_call(kernel, out, scratch, flops, *operands):
@@ -476,29 +515,37 @@
     hidden = (NEG * (res_float - 1.0))[None, :]
     operands = (
         pair,
+        side_w.swapaxes(1, 2),
+        msa,
+        row_w.reshape(flat_w),
+        row_out,
+        col_w.reshape(flat_w),
+        col_out,
         pair_mask,
         offset_w.T,
-        side_w.swapaxes(1, 2),
-        row_w.reshape(flat_w),
-        col_w.reshape(flat_w),
-        row_out,
-        col_out,
         final_w,
-        msa,
+        sigmoid_w.T,
         pick,
         hidden,
     )
     side_channels = side_w.shape[2]
+    half = channels // 2
     bf = jnp.bfloat16
     outs = [
-        pair.shape,
+        (rows_here, half, sites),
         (devices, seqs_here, rows_here * embed),
-        (devices, rows_here, sites),
         flat_w,
         col_out.shape,
-        final_w.shape,
     ]
     scratch = [
+        (pair.shape, bf),
+        ((side_w.shape[0], side_channels, channels), bf),
+        (msa.shape, bf),
+        (flat_w, bf),
+        (row_out.shape, bf),
+        (pair.shape, bf),
+        ((devices, rows_here, sites), bf),
+        (final_w.shape, bf),
         ((heads_here, flat), bf),
         ((side_channels, 2, flat), bf),
         ((2, 16, chips // 16, heads_here, flat), bf),
@@ -511,26 +558,24 @@
         ((seqs_here, queries, embed), jnp.float32),
         ((chips, seqs_here, rows_here * embed), bf),
     ]
-    semaphores = [0, 4, 6, 6, 0, 16, 0, 16, 0, 16, 6, 6, 0, 0, 0, 0]
-    pair_ln, column, product, col_wx, col_ox, final_x = pl.pallas_call(
+    semaphores = [0, 4, 6, 6, 0, 16, 0, 16, 0, 16, 6, 6, 0, 0, 0, 0, 5]
+    pair_output, column, col_wx, col_ox = pl.pallas_call(
         functools.partial(main_kernel, heads=heads, block=24),
         out_shape=[jax.ShapeDtypeStruct(shape, bf) for shape in outs],
-        in_specs=[VMEM] * len(operands),
+        in_specs=[pl.BlockSpec(memory_space=pl.ANY)] * 7 + [VMEM] * (len(operands) - 7),
         out_specs=[VMEM] * len(outs),
         scratch_shapes=[pltpu.VMEM(*one) for one in scratch]
         + [pltpu.SemaphoreType.DMA if n == 0 else pltpu.SemaphoreType.DMA((n,)) for n in semaphores],
         compiler_params=pltpu.CompilerParams(
-            collective_id=0, has_side_effects=True, vmem_limit_bytes=48 << 20
+            collective_id=0, has_side_effects=True, vmem_limit_bytes=60 << 20
         ),
     )(*operands)
-    pair_ln = pair_ln.reshape(flat, channels)
-
     column = column.reshape(devices * seqs_here, rows_here * embed)
     away = (NEG * (homolog_present.astype(jnp.float32) - 1.0))[None, :]
     width = embed // 2
     alignment_output = local_call(
         functools.partial(col_kernel, heads=heads, block=32),
-        (devices * seqs_here, rows_here * width),
+        (rows_here, devices * seqs_here, width),
         [((devices * seqs_here, embed), jnp.bfloat16)],
         3 << 30,
         column,
@@ -539,22 +584,9 @@
         col_wx.reshape(col_w.shape),
         col_out,
         col_ox,
-    ).reshape(devices * seqs_here, rows_here, width)
-
-    product = product.astype(jnp.float32)
-    mean = jnp.mean(product, axis=0)
-    square = jnp.mean(product * product, axis=0)
-    scaled = ((product - mean) * lax.rsqrt(square - mean * mean + EPS)).astype(jnp.bfloat16)
-    half = channels // 2
-    first = jnp.where(rep == 0, final_w, final_x)
-    second = jnp.where(rep == 0, final_x, final_w)
-    final_all = jnp.concatenate([first, second], 0)
-    final_half = lax.dynamic_slice_in_dim(final_all, rep * half, half, 1)
-    tri_update = jnp.einsum("cij,cz->ijz", scaled, final_half, preferred_element_type=jnp.float32)
-    pair_half = lax.dynamic_slice_in_dim(pair, rep * half, half, 2)
-    gate_out = jax.nn.sigmoid(dot(pair_ln, sigmoid_w)).reshape(rows_here, sites, half)
-    pair_output = (pair_half.astype(jnp.float32) + gate_out * tri_update).astype(jnp.bfloat16)
-    return (alignment_output, pair_output)
+    ).swapaxes(0, 1)
+
+    return (alignment_output, pair_output.swapaxes(1, 2))
 
 
 def solution(mesh):

time: 79.7 us -> 76 us (0.954)
  local copies, waits for them, and re-layouts: 8.01 us -> 3.91 us
  Pallas kernels: 67.7 us -> 69.2 us
  matrix products: 1.23 us -> 0 us
    unnamed x30 -> x15, local copies, waits for them, and re-layouts: 7.49 us -> 2.04 us
    dot_general x2 -> x0, matrix products: 1.23 us -> none  [the longest x1 0.98 us: per_device(): jnp.einsum('cij,cz->ijz', scaled, final_half, preferred_element_type=jnp....]
    reshape x1, local copies, waits for them, and re-layouts: 0.15 us -> 1.2 us  [per_device(): column = column.reshape(devices * seqs_here, rows_here * embed)]
    pallas_call x1, Pallas kernels: 61.7 us -> 62.6 us  [per_device(): pl.pallas_call(functools.partial(main_kernel, heads=heads, block=24), out...]
where the time goes in v7:
time: 76 us; the launch traced here: 75.5 us
  Pallas kernels  69.2 us (91%)
  local copies, waits for them, and re-layouts  3.91 us (5%)
  other arithmetic  1.58 us (2%)
    pallas_call x1, Pallas kernels, per_device(): pl.pallas_call(functools.partial(main_kernel, heads=heads, block=24), out...  62.6 us
    pallas_call x1, Pallas kernels, local_call(): pl.pallas_call(kernel, out_shape=jax.ShapeDtypeStruct(out, jnp.bfloat16),...  6.63 us
    unnamed x15, local copies, waits for them, and re-layouts  2.04 us

profile of v7, /device:TPU:1, one launch (start us, length us, event | category | flops | bytes accessed | tf_op | source)
XLA Modules:
  0.0 75.5 jit_solution(16050858902821258946)
XLA Ops:
  0.6 0.0 copy-start.5
  0.7 0.7 copy-done.5
  1.3 0.1 dynamic_slice.3
  1.4 0.7 broadcast_multiply_fusion.pair_mask
  2.1 0.9 %fusion.pick = bf16[192,384]{1,0:T(8,128)(2,1)} fusion(s32[192]{0:T(256)S(1)} %get-tuple-element.12, s32[192]{0:T(256)S(1)} %get-tuple-element.15, s32[]{:T(128)S(6)} %mul.55, s32[192]{0:T(256)S(1)} %get-tuple-element.13, s32[192]{0:T(256)S(1)} %get-tuple-element.14, pred[192]{0:T(512)(128)(4,1)S(1)} %get-tuple-element.10, pred[192]{0:T(512)(128)(4,1)S(1)} %get-tuple-element.11), kind=kLoop, calls=%fused_computation.1 | loop fusion | flops 516096 | bytes 150916 | tf_op jit(solution)/shard_map/convert_element_type | solution.py:514
  3.0 0.6 broadcast_in_dim.8.hidden
  3.6 62.6 %shard_map.131 = (bf16[3,64,384]{2,1,0:T(8,128)(2,1)}, bf16[128,2,768]{2,1,0:T(2,128)(2,1)}, bf16[1024,128]{1,0:T(8,128)(2,1)}, bf16[128,256]{1,0:T(8,128)(2,1)}) custom-call(bf16[3,384,128]{2,1,0:T(8,128)(2,1)} %pair_in.1, bf16[4,64,128]{2,1,0:T(8,128)(2,1)} %bitcast.14, bf16[2,384,256]{2,1,0:T(8,128)(2,1)} %msa_in.1, bf16[1024,128]{1,0:T(8,128)(2,1)} %bitcast.12, ...), custom_call_target="tpu_custom_call" | custom-call | tf_op jit(solution)/shard_map/pallas_call | solution.py:562
  66.2 0.0 copy-start
  66.2 0.0 copy-start.1
  66.2 0.0 copy-start.2
  66.2 0.0 copy-start.3
  66.2 1.2 %reshape.20.column = bf16[256,768]{1,0:T(8,128)(2,1)S(1)} reshape(bf16[128,2,768]{2,1,0:T(2,128)(2,1)} %get-tuple-element.6) | data formatting | bytes 786432 | tf_op jit(solution)/shard_map/reshape | solution.py:573
  67.4 0.0 copy-start.6
  67.5 0.7 copy-done.6
  68.1 0.0 copy-done
  68.1 0.0 copy-done.1
  68.1 0.0 copy-done.2
  68.1 0.0 copy-done.3
  68.2 0.0 copy-start.4
  68.2 6.6 %shard_map.132 = bf16[3,256,128]{2,1,0:T(8,128)(2,1)} custom-call(bf16[256,768]{1,0:T(8,128)(2,1)S(1)} %reshape.20.column, f32[1,256]{1,0:T(1,128)S(1)} %bitcast.10, bf16[4,256,128]{2,1,0:T(8,128)(2,1)S(1)} %copy-done, bf16[4,256,128]{2,1,0:T(8,128)(2,1)S(1)} %bitcast.11, bf16[128,256]{1,0:T(8,128)(2,1)S(1)} %copy-done.1, bf16[128,256]{1,0:T(8,128)(2,1)S(1)} %copy-done.3), custom_call_target="tpu_custom_call" | custom-call | flops 3221225472 | bytes 4194304 | tf_op jit(solution)/shard_map/pallas_call | solution.py:472
  74.8 0.0 copy-done.4
  74.8 0.7 copy.15
  (6 shorter events, 0.0 us)
Async XLA Ops:
  0.6 0.7 copy-start.5
  66.2 1.9 %copy-start = (bf16[4,256,128]{2,1,0:T(8,128)(2,1)S(1)}, bf16[4,256,128]{2,1,0:T(8,128)(2,1)}, u32[]{:S(2)}) copy-start(bf16[4,256,128]{2,1,0:T(8,128)(2,1)} %w.1) | copy-start | bytes 786436
  66.2 1.9 %copy-start.1 = (bf16[128,256]{1,0:T(8,128)(2,1)S(1)}, bf16[128,256]{1,0:T(8,128)(2,1)}, u32[]{:S(2)}) copy-start(bf16[128,256]{1,0:T(8,128)(2,1)} %wo.1) | copy-start | bytes 196612
  66.2 1.9 %copy-start.2 = (bf16[1024,128]{1,0:T(8,128)(2,1)S(1)}, bf16[1024,128]{1,0:T(8,128)(2,1)}, u32[]{:S(2)}) copy-start(bf16[1024,128]{1,0:T(8,128)(2,1)} %get-tuple-element.7) | copy-start | bytes 786436
  66.2 1.9 %copy-start.3 = (bf16[128,256]{1,0:T(8,128)(2,1)S(1)}, bf16[128,256]{1,0:T(8,128)(2,1)}, u32[]{:S(2)}) copy-start(bf16[128,256]{1,0:T(8,128)(2,1)} %get-tuple-element.8.wox) | copy-start | bytes 196612
  67.4 0.7 copy-start.6
  68.2 6.6 %copy-start.4 = (bf16[3,64,384]{2,1,0:T(8,128)(2,1)S(1)}, bf16[3,64,384]{2,1,0:T(8,128)(2,1)}, u32[]{:S(2)}) copy-start(bf16[3,64,384]{2,1,0:T(8,128)(2,1)} %get-tuple-element.9) | copy-start | bytes 442372

commit v8 on v7

--- a/solution.py
+++ b/solution.py
@@ -83,6 +83,15 @@
         mixed[part, :] = (out * gate).astype(jnp.bfloat16)
 
 
+def over_chips(step, chips):
+    def three(j, carry):
+        for n in range(3):
+            step(3 * j + n + 1, 0)
+        return carry
+
+    lax.fori_loop(0, (chips - 1) // 3, three, 0)
+
+
 def main_kernel(
     pair_in,
     side_in,
@@ -91,12 +100,10 @@
     row_o_in,
     col_w_in,
     col_o_in,
-    pair_mask,
+    amino,
     offset_w,
     final,
     sigmoid_w,
-    pick,
-    hidden,
     pair_out,
     column,
     col_wx,
@@ -137,6 +144,7 @@
     m_sent,
     m_came,
     loaded,
+    pick,
     *,
     heads,
     block,
@@ -173,10 +181,18 @@
                 greet((*there, ct, rt))
         return carry
 
-    lax.fori_loop(1, chips, greet_chip, 0)
+    over_chips(greet_chip, chips)
     greet((*here, 1 - c, r))
     greet((*here, c, 1 - r))
     greet((*here, 1 - c, 1 - r))
+
+    present = amino[...].astype(jnp.float32).reshape(1, sites)
+    at_site = lax.broadcasted_iota(jnp.int32, (1, sites), 1)
+    query = lax.broadcasted_iota(jnp.int32, pick.shape, 0)
+    picked = 2 * rows_each * (query & (chips - 1)) + rows_each * r + query // chips
+    pick[...] = jnp.where(
+        lax.broadcasted_iota(jnp.int32, pick.shape, 1) == picked, 1.0, 0.0
+    ).astype(jnp.bfloat16)
 
     loads[0].wait()
     loads[1].wait()
@@ -185,11 +201,13 @@
         normed = standardize_features(pair[t]).astype(jnp.bfloat16)
         pair_ln[t] = normed
         bias[:, part] = dot_last(offset_w[...], normed).astype(jnp.bfloat16)
+        here_too = jnp.where(at_site == me * rows_each + t, present, 0.0)
+        mask = present * jnp.sum(here_too, axis=1, keepdims=True)
         both = []
         for n in range(2):
             gate = dot_last(side_w[2 * n], normed)
             value = dot_last(side_w[2 * n + 1], normed)
-            side = value / (1.0 + jnp.exp(-gate)) * pair_mask[t : t + 1, :]
+            side = value / (1.0 + jnp.exp(-gate)) * mask
             both.append(side[:, None, :])
         sides[:, :, part] = jnp.concatenate(both, 1).astype(jnp.bfloat16)
     sides_all[c, chip] = sides[chip]
@@ -292,40 +310,13 @@
         wait_bytes(sides_all.at[0, pl.ds(0, plane)], s_came.at[level])
         pass_sides(level)
 
-    wait_bytes(sides_all.at[0], core_came.at[5])
-    site = lax.broadcasted_iota(jnp.int32, (sites, chips), 0)
-    owner = lax.broadcasted_iota(jnp.int32, (sites, chips), 1)
-
-    def side_of(core, t, n):
-        part = sides_all[core, :, :, t * sites : (t + 1) * sites].astype(jnp.float32)
-        return part[:, n, :].astype(jnp.bfloat16)
-
-    rights = jnp.zeros((sites, sites), jnp.float32)
-    for core in range(2):
-        for t in range(rows_each):
-            put = site == owner * (2 * rows_each) + (core * rows_each + t)
-            rights += dot(put.astype(jnp.float32).astype(jnp.bfloat16), side_of(core, t, 1))
-    rights = rights.astype(jnp.bfloat16)
-    parts = [dot_last(side_of(c, t, 0), rights)[:, None, :] for t in range(rows_each)]
-    rows[...] = jnp.concatenate(parts, 1).astype(jnp.bfloat16)
-    product[channel] = rows[chip]
-
-    def to_rows(i, carry):
-        to = lax.rem(chip + i, chips)
-        send(rows.at[to], product.at[channel], p_sent, p_came, (*chip_at(to), c, 1 - r))
-        send(rows.at[to], product.at[channel], p_sent, p_came, (*chip_at(to), c, r))
-        return carry
-
-    lax.fori_loop(1, chips, to_rows, 0)
-    send(rows.at[chip], product.at[channel], p_sent, p_came, (*here, c, 1 - r))
-
     half_rows = pl.ds(0, plane * chunk)
     wait_bytes(bias_all.at[0], core_came.at[0])
     wait_bytes(row_wx.at[half_rows], core_came.at[1])
     wait_bytes(row_ox.at[o_half], core_came.at[3])
     for load in loads[2:]:
         load.wait()
-    away = hidden[...]
+    away = NEG * (present - 1.0)
 
     def place_bias(p, carry):
         at, level = lax.rem(p, plane), p // plane
@@ -342,6 +333,33 @@
 
     lax.fori_loop(0, chips, place_bias, 0)
 
+    wait_bytes(sides_all.at[0], core_came.at[5])
+    site = lax.broadcasted_iota(jnp.int32, (sites, chips), 0)
+    owner = lax.broadcasted_iota(jnp.int32, (sites, chips), 1)
+
+    def side_of(core, t, n):
+        part = sides_all[core, :, :, t * sites : (t + 1) * sites].astype(jnp.float32)
+        return part[:, n, :].astype(jnp.bfloat16)
+
+    rights = jnp.zeros((sites, sites), jnp.float32)
+    for core in range(2):
+        for t in range(rows_each):
+            put = site == owner * (2 * rows_each) + (core * rows_each + t)
+            rights += dot(put.astype(jnp.float32).astype(jnp.bfloat16), side_of(core, t, 1))
+    rights = rights.astype(jnp.bfloat16)
+    parts = [dot_last(side_of(c, t, 0), rights)[:, None, :] for t in range(rows_each)]
+    rows[...] = jnp.concatenate(parts, 1).astype(jnp.bfloat16)
+    product[channel] = rows[chip]
+
+    def to_rows(i, carry):
+        to = lax.rem(chip + i, chips)
+        send(rows.at[to], product.at[channel], p_sent, p_came, (*chip_at(to), c, 1 - r))
+        send(rows.at[to], product.at[channel], p_sent, p_came, (*chip_at(to), c, r))
+        return carry
+
+    over_chips(to_rows, chips)
+    send(rows.at[chip], product.at[channel], p_sent, p_came, (*here, c, 1 - r))
+
     def part_of(n):
         return slice(n * embed, (n + 1) * embed)
 
@@ -378,7 +396,7 @@
         send(seqs.at[to], column.at[me], m_sent, m_came, (*chip_at(to), r, r))
         return carry
 
-    lax.fori_loop(1, chips, to_owner, 0)
+    over_chips(to_owner, chips)
 
     @pl.when(c != r)
     def _():
@@ -457,7 +475,7 @@
     embed = w.shape[1]
     width = embed // 2
     at = pl.ds(pl.multiple_of(r * width, width), width)
-    away = hidden[...]
+    away = NEG * (hidden[...].astype(jnp.float32).reshape(1, column.shape[0]) - 1.0)
     for t in range(column.shape[1] // embed):
         x = standardize_features(column[:, t * embed : (t + 1) * embed]).astype(jnp.bfloat16)
         q, k, v, g = [project(x, w[n], wx[n]) for n in range(4)]
@@ -494,25 +512,15 @@
     final_w,
     sigmoid_w,
 ):
-    rep = lax.axis_index("rep")
     rows_here, sites, channels = pair.shape
     seqs_here, embed = msa.shape[0], msa.shape[2]
     chips = lax.axis_size(CHIPS)
     devices = lax.axis_size(DAP)
     heads_here = offset_w.shape[1]
     heads = 2 * heads_here
-    row_start = lax.axis_index(DAP) * rows_here
-    res_float = amino_present.astype(jnp.float32)
-    mask_rows = lax.dynamic_slice_in_dim(res_float, row_start, rows_here, 0)
     flat = rows_here * sites
-    pair_mask = mask_rows[:, None] * res_float[None, :]
     flat_w = (row_w.shape[0] * row_w.shape[1], row_w.shape[2])
     queries = chips * rows_here
-    query = lax.broadcasted_iota(jnp.int32, (queries, sites), 0)
-    site = lax.broadcasted_iota(jnp.int32, (queries, sites), 1)
-    picked = 2 * rows_here * (query % chips) + rows_here * rep + query // chips
-    pick = (site == picked).astype(jnp.bfloat16)
-    hidden = (NEG * (res_float - 1.0))[None, :]
     operands = (
         pair,
         side_w.swapaxes(1, 2),
@@ -521,12 +529,10 @@
         row_out,
         col_w.reshape(flat_w),
         col_out,
-        pair_mask,
+        amino_present,
         offset_w.T,
         final_w,
         sigmoid_w.T,
-        pick,
-        hidden,
     )
     side_channels = side_w.shape[2]
     half = channels // 2
@@ -565,13 +571,13 @@
         in_specs=[pl.BlockSpec(memory_space=pl.ANY)] * 7 + [VMEM] * (len(operands) - 7),
         out_specs=[VMEM] * len(outs),
         scratch_shapes=[pltpu.VMEM(*one) for one in scratch]
-        + [pltpu.SemaphoreType.DMA if n == 0 else pltpu.SemaphoreType.DMA((n,)) for n in semaphores],
+        + [pltpu.SemaphoreType.DMA if n == 0 else pltpu.SemaphoreType.DMA((n,)) for n in semaphores]
+        + [pltpu.VMEM((queries, sites), bf)],
         compiler_params=pltpu.CompilerParams(
             collective_id=0, has_side_effects=True, vmem_limit_bytes=60 << 20
         ),
     )(*operands)
     column = column.reshape(devices * seqs_here, rows_here * embed)
-    away = (NEG * (homolog_present.astype(jnp.float32) - 1.0))[None, :]
     width = embed // 2
     alignment_output = local_call(
         functools.partial(col_kernel, heads=heads, block=32),
@@ -579,7 +585,7 @@
         [((devices * seqs_here, embed), jnp.bfloat16)],
         3 << 30,
         column,
-        away,
+        homolog_present,
         col_w,
         col_wx.reshape(col_w.shape),
         col_out,

time: 76 us -> 72.4 us (0.953)
  other arithmetic: 1.58 us -> 0 us
  local copies, waits for them, and re-layouts: 3.91 us -> 2.52 us
    convert_element_type x2 -> x0, other arithmetic: 0.89 us -> none  [the longest x1 0.89 us: per_device(): pick = (site == picked).astype(jnp.bfloat16)]
    unnamed x15 -> x13, local copies, waits for them, and re-layouts: 2.04 us -> 1.32 us
where the time goes in v8:
time: 72.4 us; the launch traced here: 72.2 us
  Pallas kernels  69 us (95%)
  local copies, waits for them, and re-layouts  2.52 us (3%)
    pallas_call x1, Pallas kernels, per_device(): pl.pallas_call(functools.partial(main_kernel, heads=heads, block=24), out...  62.3 us
    pallas_call x1, Pallas kernels, local_call(): pl.pallas_call(kernel, out_shape=jax.ShapeDtypeStruct(out, jnp.bfloat16),...  6.62 us

profile of v8, /device:TPU:1, one launch (start us, length us, event | category | flops | bytes accessed | tf_op | source)
XLA Modules:
  0.0 72.2 jit_solution(4062542355926375760)
XLA Ops:
  0.6 62.3 %shard_map.131 = (bf16[3,64,384]{2,1,0:T(8,128)(2,1)}, bf16[128,2,768]{2,1,0:T(2,128)(2,1)}, bf16[1024,128]{1,0:T(8,128)(2,1)}, bf16[128,256]{1,0:T(8,128)(2,1)}) custom-call(bf16[3,384,128]{2,1,0:T(8,128)(2,1)} %pair_in.1, bf16[4,64,128]{2,1,0:T(8,128)(2,1)} %bitcast.12, bf16[2,384,256]{2,1,0:T(8,128)(2,1)} %msa_in.1, bf16[1024,128]{1,0:T(8,128)(2,1)} %bitcast.10, ...), custom_call_target="tpu_custom_call" | custom-call | tf_op jit(solution)/shard_map/pallas_call | solution.py:568
  63.0 0.0 copy-start
  63.0 0.0 copy-start.1
  63.0 0.0 copy-start.2
  63.0 0.0 copy-start.3
  63.0 1.2 %reshape.18.column = bf16[256,768]{1,0:T(8,128)(2,1)S(1)} reshape(bf16[128,2,768]{2,1,0:T(2,128)(2,1)} %get-tuple-element.6) | data formatting | bytes 786432 | tf_op jit(solution)/shard_map/reshape | solution.py:580
  64.2 0.0 copy-start.4
  64.2 0.0 copy-done
  64.2 0.0 copy-done.1
  64.3 0.0 copy-done.2
  64.3 0.0 copy-done.3
  64.3 0.6 copy-done.4
  64.9 0.0 copy-start.5
  64.9 6.6 %shard_map.132 = bf16[3,256,128]{2,1,0:T(8,128)(2,1)} custom-call(bf16[256,768]{1,0:T(8,128)(2,1)S(1)} %reshape.18.column, s32[256]{0:T(256)S(1)} %copy-done.4, bf16[4,256,128]{2,1,0:T(8,128)(2,1)S(1)} %copy-done, bf16[4,256,128]{2,1,0:T(8,128)(2,1)S(1)} %bitcast.9, bf16[128,256]{1,0:T(8,128)(2,1)S(1)} %copy-done.1, bf16[128,256]{1,0:T(8,128)(2,1)S(1)} %copy-done.3), custom_call_target="tpu_custom_call" | custom-call | flops 3221225472 | bytes 4194304 | tf_op jit(solution)/shard_map/pallas_call | solution.py:490
  71.5 0.0 copy-done.5
  71.5 0.7 copy.15
Async XLA Ops:
  63.0 1.3 %copy-start = (bf16[4,256,128]{2,1,0:T(8,128)(2,1)S(1)}, bf16[4,256,128]{2,1,0:T(8,128)(2,1)}, u32[]{:S(2)}) copy-start(bf16[4,256,128]{2,1,0:T(8,128)(2,1)} %w.1) | copy-start | bytes 786436
  63.0 1.3 %copy-start.1 = (bf16[128,256]{1,0:T(8,128)(2,1)S(1)}, bf16[128,256]{1,0:T(8,128)(2,1)}, u32[]{:S(2)}) copy-start(bf16[128,256]{1,0:T(8,128)(2,1)} %wo.1) | copy-start | bytes 196612
  63.0 1.3 %copy-start.2 = (bf16[1024,128]{1,0:T(8,128)(2,1)S(1)}, bf16[1024,128]{1,0:T(8,128)(2,1)}, u32[]{:S(2)}) copy-start(bf16[1024,128]{1,0:T(8,128)(2,1)} %get-tuple-element.7) | copy-start | bytes 786436
  63.0 1.3 %copy-start.3 = (bf16[128,256]{1,0:T(8,128)(2,1)S(1)}, bf16[128,256]{1,0:T(8,128)(2,1)}, u32[]{:S(2)}) copy-start(bf16[128,256]{1,0:T(8,128)(2,1)} %get-tuple-element.8.wox) | copy-start | bytes 196612
  64.2 0.7 copy-start.4
  64.9 6.6 %copy-start.5 = (bf16[3,64,384]{2,1,0:T(8,128)(2,1)S(1)}, bf16[3,64,384]{2,1,0:T(8,128)(2,1)}, u32[]{:S(2)}) copy-start(bf16[3,64,384]{2,1,0:T(8,128)(2,1)} %get-tuple-element.9) | copy-start | bytes 442372

commit v9 on v8

--- a/solution.py
+++ b/solution.py
@@ -475,15 +475,16 @@
     embed = w.shape[1]
     width = embed // 2
     at = pl.ds(pl.multiple_of(r * width, width), width)
-    away = NEG * (hidden[...].astype(jnp.float32).reshape(1, column.shape[0]) - 1.0)
-    for t in range(column.shape[1] // embed):
-        x = standardize_features(column[:, t * embed : (t + 1) * embed]).astype(jnp.bfloat16)
+    away = NEG * (hidden[...].astype(jnp.float32).reshape(1, mixed.shape[0]) - 1.0)
+    for t in range(out.shape[0]):
+        here = column[:, :, t * embed : (t + 1) * embed].astype(jnp.float32).reshape(mixed.shape)
+        x = standardize_features(here).astype(jnp.bfloat16)
         q, k, v, g = [project(x, w[n], wx[n]) for n in range(4)]
         attend_rows(q, k, v, g, lambda n: away, mixed, block, heads)
         half = wo.shape[0]
         delta = dot(mixed[:, :half], wo[:, at]) + dot(mixed[:, half:], wox[:, at])
-        keep = column[:, pl.ds(pl.multiple_of(t * embed + r * width, width), width)]
-        out[t] = (keep.astype(jnp.float32) + delta).astype(jnp.bfloat16)
+        keep = jnp.where(r == 0, here[:, :width], here[:, width:])
+        out[t] = (keep + delta).astype(jnp.bfloat16)
 
 
 def local_call(kernel, out, scratch, flops, *operands):
@@ -577,7 +578,6 @@
             collective_id=0, has_side_effects=True, vmem_limit_bytes=60 << 20
         ),
     )(*operands)
-    column = column.reshape(devices * seqs_here, rows_here * embed)
     width = embed // 2
     alignment_output = local_call(
         functools.partial(col_kernel, heads=heads, block=32),

time: 72.4 us -> 74.2 us (1.025)
  local copies, waits for them, and re-layouts: 2.52 us -> 4.11 us
    unnamed x13 -> x15, local copies, waits for them, and re-layouts: 1.32 us -> 4.11 us
    reshape x1 -> x0, local copies, waits for them, and re-layouts: 1.2 us -> none  [per_device(): column = column.reshape(devices * seqs_here, rows_here * embed)]
where the time goes in v9:
time: 74.2 us; the launch traced here: 73.9 us
  Pallas kernels  69.1 us (93%)
  local copies, waits for them, and re-layouts  4.11 us (6%)
    pallas_call x1, Pallas kernels, per_device(): pl.pallas_call(functools.partial(main_kernel, heads=heads, block=24), out...  62.3 us
    pallas_call x1, Pallas kernels, local_call(): pl.pallas_call(kernel, out_shape=jax.ShapeDtypeStruct(out, jnp.bfloat16),...  6.82 us
    unnamed x15, local copies, waits for them, and re-layouts  4.11 us

profile of v9, /device:TPU:1, one launch (start us, length us, event | category | flops | bytes accessed | tf_op | source)
XLA Modules:
  0.0 73.9 jit_solution(5865618506141429309)
XLA Ops:
  0.6 0.0 copy-start
  0.6 0.0 copy-start.1
  0.7 62.3 %shard_map.131 = (bf16[3,64,384]{2,1,0:T(8,128)(2,1)}, bf16[128,2,768]{2,1,0:T(2,128)(2,1)}, bf16[1024,128]{1,0:T(8,128)(2,1)}, bf16[128,256]{1,0:T(8,128)(2,1)}) custom-call(bf16[3,384,128]{2,1,0:T(8,128)(2,1)} %pair_in.1, bf16[4,64,128]{2,1,0:T(8,128)(2,1)} %bitcast.12, bf16[2,384,256]{2,1,0:T(8,128)(2,1)} %msa_in.1, bf16[1024,128]{1,0:T(8,128)(2,1)} %bitcast.10, ...), custom_call_target="tpu_custom_call" | custom-call | tf_op jit(solution)/shard_map/pallas_call | solution.py:569
  63.0 0.0 copy-start.5
  63.0 0.0 copy-done
  63.0 0.0 copy-done.1
  63.0 0.7 copy-done.5
  63.7 0.0 copy-start.2
  63.7 1.0 %copy-done.2 = bf16[128,2,768]{2,1,0:T(2,128)(2,1)S(1)} copy-done((bf16[128,2,768]{2,1,0:T(2,128)(2,1)S(1)}, bf16[128,2,768]{2,1,0:T(2,128)(2,1)}, u32[]{:S(2)}) %copy-start.2) | copy-done | bytes 393240
  64.7 0.0 copy-start.3
  64.7 0.9 %copy-done.3 = bf16[1024,128]{1,0:T(8,128)(2,1)S(1)} copy-done((bf16[1024,128]{1,0:T(8,128)(2,1)S(1)}, bf16[1024,128]{1,0:T(8,128)(2,1)}, u32[]{:S(2)}) %copy-start.3) | copy-done | bytes 262168
  65.6 0.0 copy-start.4
  65.6 0.8 %copy-done.4 = bf16[128,256]{1,0:T(8,128)(2,1)S(1)} copy-done((bf16[128,256]{1,0:T(8,128)(2,1)S(1)}, bf16[128,256]{1,0:T(8,128)(2,1)}, u32[]{:S(2)}) %copy-start.4) | copy-done | bytes 65560
  66.5 0.0 copy-start.6
  66.5 6.8 %shard_map.132 = bf16[3,256,128]{2,1,0:T(8,128)(2,1)} custom-call(bf16[128,2,768]{2,1,0:T(2,128)(2,1)S(1)} %copy-done.2, s32[256]{0:T(256)S(1)} %copy-done.5, bf16[4,256,128]{2,1,0:T(8,128)(2,1)S(1)} %copy-done, bf16[4,256,128]{2,1,0:T(8,128)(2,1)S(1)} %bitcast.9, bf16[128,256]{1,0:T(8,128)(2,1)S(1)} %copy-done.1, bf16[128,256]{1,0:T(8,128)(2,1)S(1)} %copy-done.4), custom_call_target="tpu_custom_call" | custom-call | flops 3221225472 | bytes 4194304 | tf_op jit(solution)/shard_map/pallas_call | solution.py:491
  73.3 0.0 copy-done.6
  73.3 0.7 copy.15
Async XLA Ops:
  0.6 62.4 %copy-start = (bf16[4,256,128]{2,1,0:T(8,128)(2,1)S(1)}, bf16[4,256,128]{2,1,0:T(8,128)(2,1)}, u32[]{:S(2)}) copy-start(bf16[4,256,128]{2,1,0:T(8,128)(2,1)} %w.1) | copy-start | bytes 786436
  0.6 62.4 %copy-start.1 = (bf16[128,256]{1,0:T(8,128)(2,1)S(1)}, bf16[128,256]{1,0:T(8,128)(2,1)}, u32[]{:S(2)}) copy-start(bf16[128,256]{1,0:T(8,128)(2,1)} %wo.1) | copy-start | bytes 196612
  63.0 0.7 copy-start.5
  63.7 1.0 %copy-start.2 = (bf16[128,2,768]{2,1,0:T(2,128)(2,1)S(1)}, bf16[128,2,768]{2,1,0:T(2,128)(2,1)}, u32[]{:S(2)}) copy-start(bf16[128,2,768]{2,1,0:T(2,128)(2,1)} %get-tuple-element.6.column) | copy-start | bytes 1179652
  64.7 0.9 %copy-start.3 = (bf16[1024,128]{1,0:T(8,128)(2,1)S(1)}, bf16[1024,128]{1,0:T(8,128)(2,1)}, u32[]{:S(2)}) copy-start(bf16[1024,128]{1,0:T(8,128)(2,1)} %get-tuple-element.7) | copy-start | bytes 786436
  65.6 0.8 %copy-start.4 = (bf16[128,256]{1,0:T(8,128)(2,1)S(1)}, bf16[128,256]{1,0:T(8,128)(2,1)}, u32[]{:S(2)}) copy-start(bf16[128,256]{1,0:T(8,128)(2,1)} %get-tuple-element.8.wox) | copy-start | bytes 196612
  66.5 6.8 %copy-start.6 = (bf16[3,64,384]{2,1,0:T(8,128)(2,1)S(1)}, bf16[3,64,384]{2,1,0:T(8,128)(2,1)}, u32[]{:S(2)}) copy-start(bf16[3,64,384]{2,1,0:T(8,128)(2,1)} %get-tuple-element.9) | copy-start | bytes 442372
